TPU v7x, 512 devices: a whole 4x8x8 slice. The times are simulated.
512 devices in a mesh: tm: 32 (over y, z_lo), space: 16 (over x, z_hi, core).
Axes of the slice: x: 4, y: 8, z: 8 (z_hi: 2, z_lo: 4; z = z_hi * 4 + z_lo), core: 2. Of those that a mesh axis runs over, the one named last changes fastest.
Arguments:
- c_points: float32 [32, 256, 32, 128], P('tm', 'space'), may hold values from -15 to 15
- corrections: float32 [32, 256, 32, 128], P('tm', 'space'), may hold values from -3 to 3
- conductivity: float32 [256, 32, 128], P('space'), may hold values from 0.2 to 5
- forcing: float32 [256, 32, 128], P('space'), may hold values from -6 to 6
Outputs:
- f_states: float32 [32, 2, 256, 32, 128], P('tm', None, 'space')
All inputs are finite; a program needn't handle non-finite values.
Results may differ from a plain program's by a relative error of at most 0.0002.
Values sent between devices are 32-bit elements; how exact they have to be, the bound alone decides.
No kernel may reach another device: no remote copies, remote signals or barrier semaphores. Data moves between devices by JAX's collectives and lax.ppermute only.
A program may use at most 64 MiB of HBM per device.

v0:
```python
import jax
import jax.numpy as jnp
import numpy as np
from jax import lax
from jax.experimental import pallas as pl
from jax.experimental.pallas import tpu as pltpu
from jax.sharding import PartitionSpec as P


ITERS = 6
STEPS = 2
STEP_RATE = 4.0
SOURCE_WEIGHT = 0.25


LOW, HIGH = 1.0, 141.0
MID = 0.5 * (LOW + HIGH)
HALF = 0.5 * (HIGH - LOW)
SIGMA = 2.0 / HALF
KAPPA = SIGMA * (1.0 - MID)
FACE = 0.5 * STEP_RATE * SIGMA

RIM = STEPS * ITERS
KEEP = ITERS - 1
SUB = 8
LANES = 128
TOTALS = 2 * RIM + 1 + ITERS
GROUPS_OF_8 = (TOTALS + 7) // 8
NOISE = 1e-8
ALLOWED = 5e-5


def two_sum(a, b):
    s = a + b
    t = s - a
    return s, (a - (s - t)) + (b - t)


def quick_two_sum(a, b):
    s = a + b
    return s, b - (s - a)


def add2(a, b):
    s, e = two_sum(a[0], b[0])
    return quick_two_sum(s, e + (a[1] + b[1]))


def neg2(a):
    return -a[0], -a[1]


def split(a):
    t = 4097.0 * a
    hi = t - (t - a)
    return hi, a - hi


def two_prod(a, b):
    p = a * b
    ah, al = split(a)
    bh, bl = split(b)
    return p, ((ah * bh - p) + ah * bl + al * bh) + al * bl


def mul2(a, b):
    p, e = two_prod(a[0], b[0])
    return quick_two_sum(p, e + (a[0] * b[1] + a[1] * b[0]))


def const2(c):
    hi = float(np.float32(c))
    return hi, float(np.float32(c - hi))


def recip2(a):
    q = 1.0 / a[0]
    p, e = two_prod(q, a[0])
    r = (1.0 - p) - (e + q * a[1])
    return quick_two_sum(q, q * r)


def roll(v, shift, axis):
    return pltpu.roll(v, shift % v.shape[axis], axis)


def load_rows(ref, z, k):
    return ref[z, pl.ds(k, SUB, stride=4), :]


def times2(a, c):
    hi, lo = const2(c)
    return mul2(a, (jnp.full_like(a[0], hi), jnp.full_like(a[0], lo)))


def double2(a):
    return 2.0 * a[0], 2.0 * a[1]


def half2(a):
    return 0.5 * a[0], 0.5 * a[1]


def pack(totals, out):
    for shift in (4, 2, 1):
        totals = [add2(t, (roll(t[0], shift, 0), roll(t[1], shift, 0))) for t in totals]
    row = lax.broadcasted_iota(jnp.int32, (SUB, LANES), 0)
    lane = lax.broadcasted_iota(jnp.int32, (SUB, LANES), 1)
    result = jnp.zeros((SUB, LANES), jnp.float32)
    for g in range(GROUPS_OF_8):
        part = totals[8 * g : 8 * g + 8]
        hi = lo = jnp.zeros((SUB, LANES), jnp.float32)
        for i, t in enumerate(part):
            hi = jnp.where(row == i, t[0], hi)
            lo = jnp.where(row == i, t[1], lo)
        both = (hi, lo)
        for shift in (64, 32, 16, 8, 4, 2, 1):
            both = add2(both, (roll(both[0], shift, 1), roll(both[1], shift, 1)))
        result = jnp.where(lane == g, both[0], result)
        result = jnp.where(lane == GROUPS_OF_8 + g, both[1], result)
    for p in range(out.shape[0]):
        out[p] = result


def unpack(gathered):
    hi = gathered[0]
    lo = jnp.zeros_like(hi)
    for p in range(1, gathered.shape[0]):
        hi, e = two_sum(hi, gathered[p])
        lo = lo + e
    lo = lo + roll(hi, -GROUPS_OF_8, 1)
    hi, lo = quick_two_sum(hi, lo)
    whole = (SUB, LANES)
    spot = lambda v, i: jnp.broadcast_to(v[i % 8 : i % 8 + 1, i // 8 : i // 8 + 1], whole)
    return [(spot(hi, i), spot(lo, i)) for i in range(TOTALS)]


def galerkin(nu):
    image = []
    for k in range(2 * ITERS - 1):
        image.append(add2(times2(nu[k], MID), times2(add2(nu[k + 1], nu[abs(k - 1)]), 0.5 * HALF)))
    m = {(i, j): half2(add2(image[i + j], image[i - j])) for i in range(ITERS) for j in range(i + 1)}
    y = [nu[i] for i in range(ITERS)]
    inverse, unit = [], {}
    for j in range(ITERS):
        inverse.append(recip2(m[j, j]))
        for i in range(j + 1, ITERS):
            unit[i, j] = mul2(m[i, j], inverse[j])
        for i in range(j + 1, ITERS):
            minus = neg2(unit[i, j])
            for k in range(j + 1, i + 1):
                m[i, k] = add2(m[i, k], mul2(minus, m[k, j]))
            y[i] = add2(y[i], mul2(minus, y[j]))
    c = [mul2(y[j], inverse[j])[0] for j in range(ITERS)]
    for j in reversed(range(ITERS)):
        for i in range(j + 1, ITERS):
            c[j] = c[j] - unit[i, j][0] * c[i]
    return c


def next_moments(nu, c):
    zero = jnp.zeros_like(c[0])
    shifted = [(zero, zero)] * (ITERS + 2)

    def put(k, v):
        shifted[k] = add2(shifted[k], v)

    for k, v in enumerate(c):
        put(k + 1, (v if k == 0 else 0.5 * v, zero))
        if k > 0:
            put(k - 1, (0.5 * v, zero))
    q = []
    for k in range(ITERS + 1):
        u = times2(shifted[k], -HALF)
        if k < ITERS:
            u = add2(u, times2((c[k], zero), 1.0 - MID))
        q.append(add2((jnp.ones_like(zero), zero), u) if k == 0 else u)
    square = [(zero, zero)] * (2 * ITERS + 1)

    def gather(k, v):
        square[k] = v if square[k][0] is zero else add2(square[k], v)

    for i in range(ITERS + 1):
        for j in range(i + 1):
            v = mul2(q[i], q[j])
            if i == j:
                v = half2(v)
            gather(i + j, v)
            gather(i - j, v)
    result = []
    for k in range(2 * ITERS):
        total = None
        for i in range(2 * ITERS + 1):
            v = mul2(square[i], half2(add2(nu[i + k], nu[abs(i - k)])))
            total = v if total is None else add2(total, v)
        result.append(total)
    return [v[0] for v in q], result


def solve(totals):
    row = lax.broadcasted_iota(jnp.int32, (SUB, LANES), 0)
    shaken = []
    for i in range(2 * RIM):
        sign = jnp.where((row * (2 * i + 3) * 5 + i * 3 + row * row * (i + 1)) % 7 < 3, NOISE, -NOISE)
        sign = jnp.where(row == 0, 0.0, sign)
        scale = totals[i - i % 2][0]
        shaken.append(quick_two_sum(totals[i][0], totals[i][1] + sign * scale))
    nu = []
    for i in range(2 * RIM):
        nu.append(shaken[i] if i < 2 else add2(double2(shaken[i]), neg2(nu[i % 2])))
    c1 = galerkin(nu)
    q, nu2 = next_moments(nu, c1)
    c2 = galerkin(nu2)

    def proper(v):
        return jnp.broadcast_to(v[0:1], v.shape)

    def energy(d, m):
        total = None
        for i in range(ITERS):
            for j in range(i + 1):
                v = d[i] * d[j] * (m[i + j][0] + m[i - j][0])
                v = 0.5 * v if i == j else v
                total = v if total is None else total + v
        return total

    best1, best2 = [proper(v) for v in c1], [proper(v) for v in c2]
    moved = energy([a - b for a, b in zip(c1, best1)], nu) + energy([a - b for a, b in zip(c2, best2)], nu2)
    size = totals[2 * RIM][0] + energy(best1, nu)
    for i in range(ITERS):
        size = size + 2.0 * best1[i] * totals[2 * RIM + 1 + i][0]
    good = jnp.where(moved <= ALLOWED**2 * size, 1.0, 0.0)
    for shift in (4, 2, 1):
        good = jnp.minimum(good, roll(good, shift, 0))
    return best1, [proper(v) for v in q], best2, good


def fill_weights(conduct, fields, first, last):
    wz, wy, wx, wl, bd = fields
    row = lax.broadcasted_iota(jnp.int32, (SUB, LANES), 0)
    lane = lax.broadcasted_iota(jnp.int32, (SUB, LANES), 1)
    not_last_lane = jnp.where(lane < LANES - 1, FACE, 0.0)
    not_first_lane = jnp.where(lane > 0, FACE, 0.0)
    not_last_row = jnp.where(row < SUB - 1, FACE, 0.0)
    side = jnp.where((lane == 0) | (lane == LANES - 1), FACE, 0.0)
    edge = [side + jnp.where(row == 0, FACE, 0.0), side, side, side + jnp.where(row == SUB - 1, FACE, 0.0)]
    here = conduct(first)
    for e in range(first, last + 1):
        z = e - first
        nxt = [here[1], here[2], here[3], roll(here[0], -1, 0)]
        if e < last:
            above = conduct(e + 1)
        for q in range(4):
            if e < last:
                wz[z, q] = FACE * (here[q] + above[q])
            wx[z, q] = not_last_lane * (here[q] + roll(here[q], -1, 1))
            wl[z, q] = not_first_lane * (here[q] + roll(here[q], 1, 1))
            wy[z, q] = (FACE if q < 3 else not_last_row) * (here[q] + nxt[q])
            bd[z, q] = edge[q] * here[q]
        here = above


def flat_part(e, here, fields):
    _, wy, wx, wl, _ = fields
    right = [roll(v, -1, 1) for v in here]
    left = [roll(v, 1, 1) for v in here]
    nxt = [here[1], here[2], here[3], roll(here[0], -1, 0)]
    fy = [wy[e, k] * (nxt[k] - here[k]) for k in range(4)]
    prv = [roll(fy[3], 1, 0), fy[0], fy[1], fy[2]]
    return [
        (fy[k] - prv[k]) + (wx[e, k] * (right[k] - here[k]) - wl[e, k] * (here[k] - left[k])) for k in range(4)
    ]


def divergence(load, fields, first, last, emit, closed=False):
    wz = fields[0]
    here = load(first)
    if not closed:
        below = load(first - 1)
        flux_below = [wz[first - 1, k] * (here[k] - below[k]) for k in range(4)]
    for e in range(first, last + 1):
        div = flat_part(e, here, fields)
        if not (closed and e == last):
            above = load(e + 1)
            flux_above = [wz[e, k] * (above[k] - here[k]) for k in range(4)]
            div = [d + f for d, f in zip(div, flux_above)]
        if not (closed and e == first):
            div = [d - f for d, f in zip(div, flux_below)]
        emit(e, here, div)
        if not (closed and e == last):
            here, flux_below = above, flux_above


def planes(ref, *lead, shift=0):
    return lambda e: [ref[(*lead, e - shift, k)] for k in range(4)]


def conductivities(a, lo, hi):
    depth = a.shape[0]

    def conduct(e):
        ref, z = (lo, e) if e < RIM else (a, e - RIM) if e < RIM + depth else (hi, e - RIM - depth)
        return [ref[z, q] for q in range(4)]

    return conduct


def inside(lo, hi, low, high):
    one = jnp.ones((SUB, LANES), jnp.float32)
    return {
        low: jnp.where(lo[RIM - 1, 0] > 0, one, 0.0),
        high: jnp.where(hi[0, 0] > 0, one, 0.0),
    }


def stage_kernel(c, f, a, cs, fs, cond, tail, head):
    depth = c.shape[0]
    for z in range(depth):
        for q in range(4):
            cs[z, q] = load_rows(c, z, q)
            fs[z, q] = load_rows(f, z, q)
            v = load_rows(a, z, q)
            cond[z, q] = v
            if z < RIM:
                head[z, q] = v
            if z >= depth - RIM:
                tail[z - depth + RIM, q] = v


def open_kernel(c, fix, f, a, x, res, tail, head, *fields):
    depth = c.shape[0]
    fill_weights(planes(a), fields, 0, depth - 1)
    for z in range(depth):
        for q in range(4):
            v = c[z, q] + load_rows(fix, z, q)
            x[z, q] = v
            if z == 0:
                head[RIM, q] = v
            if z == depth - 1:
                tail[RIM, q] = v
    bd = fields[-1]

    def emit(z, v, div):
        for q in range(4):
            r = SOURCE_WEIGHT * f[z, q] - (1.0 / SIGMA) * (bd[z, q] * v[q] - div[q])
            res[z, q] = r
            if z < RIM:
                head[z, q] = r
            if z >= depth - RIM:
                tail[z - depth + RIM, q] = r

    divergence(planes(x), fields, 0, depth - 1, emit, closed=True)


def basis_kernel(x, res, lo, hi, a, alo, ahi, basis, sums, kept, ring, done, *fields):
    depth = x.shape[0]
    span = depth + 2 * RIM
    low, high = RIM - 1, RIM + depth
    mask = inside(alo, ahi, low, high)
    fill_weights(conductivities(a, alo, ahi), fields, 0, span - 1)
    wz, bd = fields[0], fields[-1]
    first, count = RIM - KEEP, depth + 2 * KEEP
    totals = {}

    def take(key, terms):
        s = (terms[0] + terms[1]) + (terms[2] + terms[3])
        if key in totals:
            hi_, e = two_sum(totals[key][0], s)
            totals[key] = (hi_, totals[key][1] + e)
        else:
            totals[key] = (s, jnp.zeros_like(s))

    def place(k):
        return (kept, k) if k <= ITERS else (ring, k % 3)

    def store(k, e, new, old):
        if e in mask:
            new = [n * mask[e] for n in new]
        if k < RIM:
            ref, slot = place(k)
            for q in range(4):
                ref[slot, e, q] = new[q]
        if RIM <= e < RIM + depth:
            if k < RIM:
                take(2 * k, [n * n for n in new])
            if k > 0:
                take(2 * k - 1, [n * o for n, o in zip(new, old)])
            if k < ITERS:
                v = [x[e - RIM, q] for q in range(4)]
                if k == 0:
                    take(2 * RIM, [u * u for u in v])
                take(2 * RIM + 1 + k, [n * u for n, u in zip(new, v)])

    def copy(k):
        return pltpu.make_async_copy(kept.at[k, pl.ds(first, count)], basis.at[k], done.at[k])

    for e in range(span):
        if e < RIM:
            new = [lo[e, q] for q in range(4)]
        elif e < RIM + depth:
            new = [res[e - RIM, q] for q in range(4)]
        else:
            new = [hi[e - RIM - depth, q] for q in range(4)]
        for face, inner, outer in ((low, 0, lo), (high - 1, depth - 1, hi)):
            if e in (face, face + 1):
                own = (e == face) == (face != low)
                for q in range(4):
                    flux = (1.0 / SIGMA) * wz[face, q] * (x[inner, q] - outer[RIM, q])
                    new[q] = new[q] - flux if own else new[q] + flux
        store(0, e, new, None)
    copy(0).start()
    for k in range(1, RIM + 1):

        def emit(e, v, div, k=k):
            image = [(KAPPA + bd[e, q]) * v[q] - div[q] for q in range(4)]
            if k == 1:
                new = [0.5 * i for i in image]
            else:
                ref, slot = place(k - 2)
                new = [i - ref[slot, e, q] for q, i in enumerate(image)]
            store(k, e, new, v)

        divergence(planes(*place(k - 1)), fields, k, span - 1 - k, emit)
        if k <= ITERS:
            copy(k).start()
    pack([totals[i] for i in range(TOTALS)], sums)
    for k in range(ITERS + 1):
        copy(k).wait()


def states_kernel(gathered, basis, x, a, alo, ahi, out, flag, kept, ring, final, done, *fields):
    depth = x.shape[0]
    first, count = RIM - KEEP, depth + 2 * KEEP
    copies = [pltpu.make_async_copy(basis.at[k], kept.at[k], done.at[k]) for k in range(ITERS + 1)]
    for copy in copies:
        copy.start()
    mask = inside(alo, ahi, KEEP - 1, KEEP + depth)
    conduct = conductivities(a, alo, ahi)
    fill_weights(lambda e: conduct(e + first), fields, 0, count - 1)
    bd = fields[-1]
    c1, q1, c2, good = solve(unpack(gathered))
    flag[...] = good
    for copy in copies:
        copy.wait()

    def store(k, e, new):
        if e in mask:
            new = [n * mask[e] for n in new]
        z = e - KEEP
        for q in range(4):
            if k < ITERS - 1:
                ring[k % 3, e, q] = new[q]
            if 0 <= z < depth:
                s = final[z, q] + c2[k] * new[q]
                if k < ITERS - 1:
                    final[z, q] = s
                else:
                    out[0, 1, z, pl.ds(q, SUB, stride=4), :] = s

    for e in range(count):
        z = e - KEEP
        new = []
        for q in range(4):
            parts = [kept[k, e, q] for k in range(ITERS + 1)]
            if 0 <= z < depth:
                s = x[z, q]
                for k in range(ITERS):
                    s = s + c1[k] * parts[k]
                final[z, q] = s
                out[0, 0, z, pl.ds(q, SUB, stride=4), :] = s
            r = q1[0] * parts[0]
            for k in range(1, ITERS + 1):
                r = r + q1[k] * parts[k]
            new.append(r)
        store(0, e, new)
    for k in range(1, ITERS):

        def emit(e, v, div, k=k):
            image = [(KAPPA + bd[e, q]) * v[q] - div[q] for q in range(4)]
            if k == 1:
                new = [0.5 * i for i in image]
            else:
                new = [i - ring[(k - 2) % 3, e, q] for q, i in enumerate(image)]
            store(k, e, new)

        divergence(planes(ring, (k - 1) % 3), fields, k, count - 1 - k, emit)


def call(kernel, outs, scratch, sent=None, read=None, inputs=0, copies=0, weights=True):
    vmem = pl.BlockSpec(memory_space=pltpu.VMEM)
    hbm = pl.BlockSpec(memory_space=pltpu.HBM)
    own = [pltpu.VMEM(s, jnp.float32) for s in scratch]
    if copies:
        own.append(pltpu.SemaphoreType.DMA((copies,)))
    return lambda fields: pl.pallas_call(
        kernel,
        out_shape=[(pltpu.HBM if i == sent else jax.ShapeDtypeStruct)(s, jnp.float32) for i, s in enumerate(outs)],
        in_specs=[hbm if i == read else vmem for i in range(inputs)],
        out_specs=[hbm if i == sent else vmem for i in range(len(outs))],
        scratch_shapes=own + [pltpu.VMEM(fields, jnp.float32)] * (5 if weights else 0),
        compiler_params=pltpu.CompilerParams(vmem_limit_bytes=20 * 2**20),
    )


def fast(c_points, corrections, conductivity, forcing):
    times, slabs = lax.axis_size("tm"), lax.axis_size("space")
    depth = forcing.shape[0]
    span, count = depth + 2 * RIM, depth + 2 * KEEP
    tile = (4, SUB, LANES)
    up = [(i, i + 1) for i in range(slabs - 1)]
    down = [(i + 1, i) for i in range(slabs - 1)]
    later = [(i, i + 1) for i in range(times - 1)]

    def short(moves):
        pairs = []
        for t in range(times):
            for s, d in moves:
                u = t if (s // 2) % 2 == (d // 2) % 2 else t // 4 * 4 + 3 - t % 4
                pairs.append((t * slabs + s, u * slabs + d))
        return pairs

    own, sent, rim = (depth, *tile), (RIM + 1, *tile), (RIM, *tile)
    fix = lax.ppermute(corrections[0], "tm", later)
    point, source, cond, tail, head = call(
        stage_kernel, [own, own, own, rim, rim], [], inputs=3, weights=False
    )(own)(c_points[0], forcing, conductivity)
    alo = lax.ppermute(tail, ("tm", "space"), short(up))
    ahi = lax.ppermute(head, ("tm", "space"), short(down))
    x, res, tail, head = call(open_kernel, [own, own, sent, sent], [], inputs=4)(own)(point, fix, source, cond)
    lo = lax.ppermute(tail, "space", up)
    hi = lax.ppermute(head, "space", down)
    field, part = (span, *tile), (count, *tile)
    basis, sums = call(
        basis_kernel,
        [(ITERS + 1, *part), (slabs, SUB, LANES)],
        [(ITERS + 1, *field), (3, *field)],
        sent=0,
        inputs=7,
        copies=ITERS + 1,
    )(field)(x, res, lo, hi, cond, alo, ahi)
    basis = pltpu.with_memory_space_constraint(basis, pltpu.HBM)
    sums = lax.all_to_all(sums, "space", 0, 0, tiled=True)
    return call(
        states_kernel,
        [(1, STEPS, depth, 4 * SUB, LANES), (SUB, LANES)],
        [(ITERS + 1, *part), (3, *part), own],
        read=1,
        inputs=6,
        copies=ITERS + 1,
    )(part)(sums, basis, x, cond, alo, ahi)


def copy_for_each(array, axis):
    devices = lax.axis_size(axis)
    return lax.all_to_all(
        jnp.broadcast_to(array[None], (devices, *array.shape)), axis, 0, 0, tiled=True
    )


def over_copies(array, axis):
    return copy_for_each(array, axis).sum(axis=0)


def packed_total(arrays, axis):
    ends = [0]
    for a in arrays:
        ends.append(ends[-1] + a.size)
    subtotal = over_copies(jnp.concatenate([a.ravel() for a in arrays]), axis)
    return tuple((subtotal[b:e].reshape(a.shape) for a, b, e in zip(arrays, ends, ends[1:])))


def extended(cells, sides, width):
    for axis, dim in sides:
        count = lax.axis_size(axis)
        ends = count - 1
        head = lax.slice_in_dim(cells, 0, width, axis=dim)
        tail = lax.slice_in_dim(cells, cells.shape[dim] - width, cells.shape[dim], axis=dim)
        cells = jnp.concatenate(
            [
                lax.ppermute(tail, axis, [(i, (i + 1) % count) for i in range(ends)]),
                cells,
                lax.ppermute(head, axis, [((i + 1) % count, i) for i in range(ends)]),
            ],
            axis=dim,
        )
    return cells


def from_behind(array, axis, by):
    devices = lax.axis_size(axis)
    pairs = [(i, i + by) for i in range(devices) if 0 <= i + by < devices]
    return lax.ppermute(array, axis, pairs)


def neighbours(padded):
    return (
        padded[2:, 1:-1, 1:-1],
        padded[:-2, 1:-1, 1:-1],
        padded[1:-1, 2:, 1:-1],
        padded[1:-1, :-2, 1:-1],
        padded[1:-1, 1:-1, 2:],
        padded[1:-1, 1:-1, :-2],
    )


def faces_of(padded_conductivity):
    centre = padded_conductivity[1:-1, 1:-1, 1:-1]
    return tuple((0.5 * (centre + beside) for beside in neighbours(padded_conductivity)))


def apply_operator(grid_field, padded, face_weights):
    flux_sum = jnp.zeros_like(grid_field)
    for face_weight, beside in zip(face_weights, neighbours(padded)):
        flux_sum = flux_sum + face_weight * (grid_field - beside)
    return grid_field + STEP_RATE * flux_sum


def pair_sums(residual, applied):
    return packed_total((jnp.sum(residual * residual), jnp.sum(residual * applied)), "space")


def plain(c_points, corrections, conductivity, forcing):
    rim_conductivity = extended(conductivity, (("space", 0),), 1)
    face_weights = faces_of(jnp.pad(rim_conductivity, ((0, 0), (1, 1), (1, 1))))

    def operate(grid_field):
        with_planes = extended(grid_field, (("space", 0),), 1)
        padded = jnp.pad(with_planes, ((0, 0), (1, 1), (1, 1)))
        return apply_operator(grid_field, padded, face_weights)

    own_point = c_points[0]
    own_fix = corrections[0]
    prior_fix = from_behind(own_fix, "tm", 1)
    current = own_point + prior_fix
    current_image = operate(current)
    sections = []
    for section in range(STEPS):
        right_side = current + SOURCE_WEIGHT * forcing
        if section > 0:
            current_image = operate(current)
        residual = right_side - current_image
        solution = current
        applied = operate(residual)
        norm_now, product = pair_sums(residual, applied)
        step_length = norm_now / product
        direction = residual
        along_dir = applied
        for sweep in range(ITERS):
            solution = solution + step_length * direction
            if sweep + 1 < ITERS:
                residual = residual - step_length * along_dir
                applied = operate(residual)
                norm_next, product = pair_sums(residual, applied)
                beta_ratio = norm_next / norm_now
                step_length = norm_next / (product - beta_ratio * norm_next / step_length)
                direction = residual + beta_ratio * direction
                along_dir = applied + beta_ratio * along_dir
                norm_now = norm_next
        sections.append(solution)
        current = solution
    return jnp.stack(sections)[None]


def body(c_points, corrections, conductivity, forcing):
    args = (c_points, corrections, conductivity, forcing)
    out, good = fast(*args)
    return lax.cond(good[0, 0] > 0, lambda: out, lambda: plain(*args))


def solution(mesh):
    in_specs = (
        P("tm", "space", None, None),
        P("tm", "space", None, None),
        P("space", None, None),
        P("space", None, None),
    )
    out_specs = P("tm", None, "space", None, None)
    return jax.shard_map(body, mesh=mesh, in_specs=in_specs, out_specs=out_specs, check_vma=False)
```

profile of v0, /device:TPU:1, one launch (start us, length us, event | category | flops | bytes accessed | tf_op | source)
XLA Modules:
  0.0 563.0 jit_solution(8909527365719197066)
XLA Ops:
  0.0 4.8 collective-permute-start.31
  8.9 13.0 %collective-permute-start.32 = (f32[13,4,8,128]{3,2,1,0:T(8,128)S(1)}, f32[13,4,8,128]{3,2,1,0:T(8,128)S(1)}, u32[]{:S(2)}, u32[]{:S(2)}) collective-permute-start(f32[13,4,8,128]{3,2,1,0:T(8,128)S(1)} %get-tuple-element.39), channel_id=1, source_target_pairs={{0,1},{1,2},{2,3},{3,4},{4,5},{5,6},{6,7},{7,8},{8,9},{9,10},{10,1... | collective-permute-start | bytes 638984 | tf_op jit(solution)/shard_map/ppermute | solution.py:530
  23.8 8.5 %collective-permute-start.34 = (f32[12,4,8,128]{3,2,1,0:T(8,128)S(1)}, f32[12,4,8,128]{3,2,1,0:T(8,128)S(1)}, u32[]{:S(2)}, u32[]{:S(2)}) collective-permute-start(f32[12,4,8,128]{3,2,1,0:T(8,128)S(1)} %get-tuple-element.41), channel_id=1, source_target_pairs={{0,1},{1,50},{2,3},{3,52},{4,5},{5,54},{6,7},{7,56},{8,9},{9,58},{... | collective-permute-start | bytes 589832 | tf_op jit(solution)/shard_map/ppermute | solution.py:527
  34.2 2.8 collective-permute-done.34.alo
  36.9 5.6 collective-permute-done.35.ahi
  42.6 6.1 %shard_map.50 = (f32[7,26,4,8,128]{4,3,2,1,0:T(8,128)}, f32[16,8,128]{2,1,0:T(8,128)}) custom-call(f32[16,4,8,128]{3,2,1,0:T(8,128)S(1)} %get-tuple-element.37.x, f32[16,4,8,128]{3,2,1,0:T(8,128)S(1)} %get-tuple-element.38.res, f32[13,4,8,128]{3,2,1,0:T(8,128)S(1)} %collective-permute-done.32.lo, f32[13,4,8,128]{3,2,1,0:T(8,128)S(1)} %collective-permute-done.33.hi, ...), custom_call_target="tpu_custom_call" | custom-call | tf_op jit(solution)/shard_map/pallas_call | solution.py:533
  48.7 7.9 %all-to-all-start.12 = ((f32[16,8,128]{2,1,0:T(8,128)}), f32[16,8,128]{2,1,0:T(8,128)S(1)}, u32[]{:S(2)}, u32[]{:S(2)}) async-start(f32[16,8,128]{2,1,0:T(8,128)} %get-tuple-element.43), calls=%async_computation.12 | async-start | bytes 131072 | tf_op jit(solution)/shard_map/all_to_all | solution.py:542
  56.6 9.7 %all-to-all-done.12.gathered = f32[16,8,128]{2,1,0:T(8,128)S(1)} async-done(((f32[16,8,128]{2,1,0:T(8,128)}), f32[16,8,128]{2,1,0:T(8,128)S(1)}, u32[]{:S(2)}, u32[]{:S(2)}) %all-to-all-start.12) | async-done | bytes 65568 | tf_op jit(solution)/shard_map/all_to_all | solution.py:542
  66.3 6.4 %shard_map.51 = (f32[1,2,16,32,128]{4,3,2,1,0:T(8,128)}, f32[8,128]{1,0:T(8,128)S(1)}) custom-call(f32[16,8,128]{2,1,0:T(8,128)S(1)} %all-to-all-done.12.gathered, f32[7,26,4,8,128]{4,3,2,1,0:T(8,128)} %get-tuple-element.44.basis, f32[16,4,8,128]{3,2,1,0:T(8,128)S(1)} %get-tuple-element.37.x, f32[16,4,8,128]{3,2,1,0:T(8,128)S(1)} %get-tuple-element.36.a, ...), custom_call_target="tpu_custom_call" | custom-call | tf_op jit(solution)/shard_map/pallas_call | solution.py:543
  74.0 489.0 %conditional.1 = (f32[1,2,16,32,128]{4,3,2,1,0:T(8,128)}) conditional(s32[]{:T(128)} %bitcast.55, (f32[1,16,32,128]{3,2,1,0:T(8,128)S(1)}, f32[1,16,32,128]{3,2,1,0:T(8,128)S(1)}, f32[16,32,128]{2,1,0:T(8,128)S(1)}, f32[16,32,128]{2,1,0:T(8,128)S(1)}) %tuple.75, f32[1,2,16,32,128]{4,3,2,1,0:T(8,128)} %get-tuple-element.46), branch_computations={%region_0.37_spmd, %region_37.38_spmd} | conditional | flops 52701000 | bytes 76249768 | solution.py:667
  80.9 6.6 %collective-permute-start.4 = (f32[1,32,128]{2,1,0:T(8,128)S(1)}, f32[1,32,128]{2,1,0:T(8,128)S(1)}, u32[]{:S(2)}, u32[]{:S(2)}) collective-permute-start(f32[1,32,128]{2,1,0:T(8,128)S(1)} %get-tuple-element.119), channel_id=1, source_target_pairs={{0,1},{1,2},{2,3},{3,4},{4,5},{5,6},{6,7},{7,8},{8,9},{9,10},{10,1... | collective-permute-start | bytes 49160 | tf_op jit(solution)/shard_map/cond/branch_0_fun/ppermute | solution.py:580
  90.0 6.6 %collective-permute-done.2 = f32[1,32,128]{2,1,0:T(8,128)S(1)} collective-permute-done((f32[1,32,128]{2,1,0:T(8,128)S(1)}, f32[1,32,128]{2,1,0:T(8,128)S(1)}, u32[]{:S(2)}, u32[]{:S(2)}) %collective-permute-start.2) | collective-permute-done | bytes 16416 | tf_op jit(solution)/shard_map/cond/branch_0_fun/ppermute | solution.py:582
  101.7 8.0 %collective-permute-done.5 = f32[1,32,128]{2,1,0:T(8,128)S(1)} collective-permute-done((f32[1,32,128]{2,1,0:T(8,128)S(1)}, f32[1,32,128]{2,1,0:T(8,128)S(1)}, u32[]{:S(2)}, u32[]{:S(2)}) %collective-permute-start.5) | collective-permute-done | bytes 16416 | tf_op jit(solution)/shard_map/cond/branch_0_fun/ppermute | solution.py:582
  112.4 18.6 %all_to_all.65 = f32[16,1,2]{2,1,0:T(1,128)S(1)} all-to-all(f32[16,1,2]{2,1,0:T(1,128)S(1)} %broadcast_in_dim.0), channel_id=1, replica_groups=mesh['tm'=32,'space'=16] {'space'}, dimensions={0} | all-to-all | bytes 256 | tf_op jit(solution)/shard_map/cond/branch_0_fun/all_to_all | solution.py:555
  132.9 2.8 collective-permute-start.8
  137.6 7.0 %collective-permute-done.7 = f32[1,32,128]{2,1,0:T(8,128)S(1)} collective-permute-done((f32[1,32,128]{2,1,0:T(8,128)S(1)}, f32[1,32,128]{2,1,0:T(8,128)S(1)}, u32[]{:S(2)}, u32[]{:S(2)}) %collective-permute-start.7) | collective-permute-done | bytes 16416 | tf_op jit(solution)/shard_map/cond/branch_0_fun/ppermute | solution.py:582
  147.1 18.4 %all_to_all.66 = f32[16,1,2]{2,1,0:T(1,128)S(1)} all-to-all(f32[16,1,2]{2,1,0:T(1,128)S(1)} %broadcast_in_dim.1), channel_id=1, replica_groups=mesh['tm'=32,'space'=16] {'space'}, dimensions={0} | all-to-all | bytes 256 | tf_op jit(solution)/shard_map/cond/branch_0_fun/all_to_all | solution.py:555
  170.8 2.8 collective-permute-start.10
  175.5 7.0 %collective-permute-done.9 = f32[1,32,128]{2,1,0:T(8,128)S(1)} collective-permute-done((f32[1,32,128]{2,1,0:T(8,128)S(1)}, f32[1,32,128]{2,1,0:T(8,128)S(1)}, u32[]{:S(2)}, u32[]{:S(2)}) %collective-permute-start.9) | collective-permute-done | bytes 16416 | tf_op jit(solution)/shard_map/cond/branch_0_fun/ppermute | solution.py:582
  185.8 18.4 %all_to_all.67 = f32[16,1,2]{2,1,0:T(1,128)S(1)} all-to-all(f32[16,1,2]{2,1,0:T(1,128)S(1)} %broadcast_in_dim.2), channel_id=1, replica_groups=mesh['tm'=32,'space'=16] {'space'}, dimensions={0} | all-to-all | bytes 256 | tf_op jit(solution)/shard_map/cond/branch_0_fun/all_to_all | solution.py:555
  209.8 2.8 collective-permute-start.12
  214.5 7.0 %collective-permute-done.11 = f32[1,32,128]{2,1,0:T(8,128)S(1)} collective-permute-done((f32[1,32,128]{2,1,0:T(8,128)S(1)}, f32[1,32,128]{2,1,0:T(8,128)S(1)}, u32[]{:S(2)}, u32[]{:S(2)}) %collective-permute-start.11) | collective-permute-done | bytes 16416 | tf_op jit(solution)/shard_map/cond/branch_0_fun/ppermute | solution.py:582
  224.2 18.4 %all_to_all.68 = f32[16,1,2]{2,1,0:T(1,128)S(1)} all-to-all(f32[16,1,2]{2,1,0:T(1,128)S(1)} %broadcast_in_dim.3), channel_id=1, replica_groups=mesh['tm'=32,'space'=16] {'space'}, dimensions={0} | all-to-all | bytes 256 | tf_op jit(solution)/shard_map/cond/branch_0_fun/all_to_all | solution.py:555
  247.2 2.8 collective-permute-start.14
  251.9 7.0 %collective-permute-done.13 = f32[1,32,128]{2,1,0:T(8,128)S(1)} collective-permute-done((f32[1,32,128]{2,1,0:T(8,128)S(1)}, f32[1,32,128]{2,1,0:T(8,128)S(1)}, u32[]{:S(2)}, u32[]{:S(2)}) %collective-permute-start.13) | collective-permute-done | bytes 16416 | tf_op jit(solution)/shard_map/cond/branch_0_fun/ppermute | solution.py:582
  262.2 18.4 %all_to_all.69 = f32[16,1,2]{2,1,0:T(1,128)S(1)} all-to-all(f32[16,1,2]{2,1,0:T(1,128)S(1)} %broadcast_in_dim.4), channel_id=1, replica_groups=mesh['tm'=32,'space'=16] {'space'}, dimensions={0} | all-to-all | bytes 256 | tf_op jit(solution)/shard_map/cond/branch_0_fun/all_to_all | solution.py:555
  286.0 2.8 collective-permute-start.16
  290.7 7.0 %collective-permute-done.15 = f32[1,32,128]{2,1,0:T(8,128)S(1)} collective-permute-done((f32[1,32,128]{2,1,0:T(8,128)S(1)}, f32[1,32,128]{2,1,0:T(8,128)S(1)}, u32[]{:S(2)}, u32[]{:S(2)}) %collective-permute-start.15) | collective-permute-done | bytes 16416 | tf_op jit(solution)/shard_map/cond/branch_0_fun/ppermute | solution.py:582
  300.4 18.4 %all_to_all.70 = f32[16,1,2]{2,1,0:T(1,128)S(1)} all-to-all(f32[16,1,2]{2,1,0:T(1,128)S(1)} %broadcast_in_dim.5), channel_id=1, replica_groups=mesh['tm'=32,'space'=16] {'space'}, dimensions={0} | all-to-all | bytes 256 | tf_op jit(solution)/shard_map/cond/branch_0_fun/all_to_all | solution.py:555
  323.4 2.8 collective-permute-start.18
  328.1 7.0 %collective-permute-done.17 = f32[1,32,128]{2,1,0:T(8,128)S(1)} collective-permute-done((f32[1,32,128]{2,1,0:T(8,128)S(1)}, f32[1,32,128]{2,1,0:T(8,128)S(1)}, u32[]{:S(2)}, u32[]{:S(2)}) %collective-permute-start.17) | collective-permute-done | bytes 16416 | tf_op jit(solution)/shard_map/cond/branch_0_fun/ppermute | solution.py:582
  341.1 7.3 %collective-permute-done.19 = f32[1,32,128]{2,1,0:T(8,128)S(1)} collective-permute-done((f32[1,32,128]{2,1,0:T(8,128)S(1)}, f32[1,32,128]{2,1,0:T(8,128)S(1)}, u32[]{:S(2)}, u32[]{:S(2)}) %collective-permute-start.19) | collective-permute-done | bytes 16416 | tf_op jit(solution)/shard_map/cond/branch_0_fun/ppermute | solution.py:582
  351.0 18.6 %all_to_all.71 = f32[16,1,2]{2,1,0:T(1,128)S(1)} all-to-all(f32[16,1,2]{2,1,0:T(1,128)S(1)} %broadcast_in_dim.6), channel_id=1, replica_groups=mesh['tm'=32,'space'=16] {'space'}, dimensions={0} | all-to-all | bytes 256 | tf_op jit(solution)/shard_map/cond/branch_0_fun/all_to_all | solution.py:555
  371.6 2.8 collective-permute-start.22
  376.3 7.0 %collective-permute-done.21 = f32[1,32,128]{2,1,0:T(8,128)S(1)} collective-permute-done((f32[1,32,128]{2,1,0:T(8,128)S(1)}, f32[1,32,128]{2,1,0:T(8,128)S(1)}, u32[]{:S(2)}, u32[]{:S(2)}) %collective-permute-start.21) | collective-permute-done | bytes 16416 | tf_op jit(solution)/shard_map/cond/branch_0_fun/ppermute | solution.py:582
  385.9 18.4 %all_to_all.72 = f32[16,1,2]{2,1,0:T(1,128)S(1)} all-to-all(f32[16,1,2]{2,1,0:T(1,128)S(1)} %broadcast_in_dim.7), channel_id=1, replica_groups=mesh['tm'=32,'space'=16] {'space'}, dimensions={0} | all-to-all | bytes 256 | tf_op jit(solution)/shard_map/cond/branch_0_fun/all_to_all | solution.py:555
  409.4 2.8 collective-permute-start.24
  414.1 7.0 %collective-permute-done.23 = f32[1,32,128]{2,1,0:T(8,128)S(1)} collective-permute-done((f32[1,32,128]{2,1,0:T(8,128)S(1)}, f32[1,32,128]{2,1,0:T(8,128)S(1)}, u32[]{:S(2)}, u32[]{:S(2)}) %collective-permute-start.23) | collective-permute-done | bytes 16416 | tf_op jit(solution)/shard_map/cond/branch_0_fun/ppermute | solution.py:582
  424.4 18.5 %all_to_all.73 = f32[16,1,2]{2,1,0:T(1,128)S(1)} all-to-all(f32[16,1,2]{2,1,0:T(1,128)S(1)} %broadcast_in_dim.8), channel_id=1, replica_groups=mesh['tm'=32,'space'=16] {'space'}, dimensions={0} | all-to-all | bytes 256 | tf_op jit(solution)/shard_map/cond/branch_0_fun/all_to_all | solution.py:555
  448.3 2.8 collective-permute-start.26
  453.1 7.0 %collective-permute-done.25 = f32[1,32,128]{2,1,0:T(8,128)S(1)} collective-permute-done((f32[1,32,128]{2,1,0:T(8,128)S(1)}, f32[1,32,128]{2,1,0:T(8,128)S(1)}, u32[]{:S(2)}, u32[]{:S(2)}) %collective-permute-start.25) | collective-permute-done | bytes 16416 | tf_op jit(solution)/shard_map/cond/branch_0_fun/ppermute | solution.py:582
  462.6 18.4 %all_to_all.74 = f32[16,1,2]{2,1,0:T(1,128)S(1)} all-to-all(f32[16,1,2]{2,1,0:T(1,128)S(1)} %broadcast_in_dim.9), channel_id=1, replica_groups=mesh['tm'=32,'space'=16] {'space'}, dimensions={0} | all-to-all | bytes 256 | tf_op jit(solution)/shard_map/cond/branch_0_fun/all_to_all | solution.py:555
  485.4 2.8 collective-permute-start.28
  490.1 7.0 %collective-permute-done.27 = f32[1,32,128]{2,1,0:T(8,128)S(1)} collective-permute-done((f32[1,32,128]{2,1,0:T(8,128)S(1)}, f32[1,32,128]{2,1,0:T(8,128)S(1)}, u32[]{:S(2)}, u32[]{:S(2)}) %collective-permute-start.27) | collective-permute-done | bytes 16416 | tf_op jit(solution)/shard_map/cond/branch_0_fun/ppermute | solution.py:582
  500.6 18.4 %all_to_all.75 = f32[16,1,2]{2,1,0:T(1,128)S(1)} all-to-all(f32[16,1,2]{2,1,0:T(1,128)S(1)} %broadcast_in_dim.10), channel_id=1, replica_groups=mesh['tm'=32,'space'=16] {'space'}, dimensions={0} | all-to-all | bytes 256 | tf_op jit(solution)/shard_map/cond/branch_0_fun/all_to_all | solution.py:555
  524.7 2.8 collective-permute-start.30
  529.4 7.0 %collective-permute-done.29 = f32[1,32,128]{2,1,0:T(8,128)S(1)} collective-permute-done((f32[1,32,128]{2,1,0:T(8,128)S(1)}, f32[1,32,128]{2,1,0:T(8,128)S(1)}, u32[]{:S(2)}, u32[]{:S(2)}) %collective-permute-start.29) | collective-permute-done | bytes 16416 | tf_op jit(solution)/shard_map/cond/branch_0_fun/ppermute | solution.py:582
  539.0 18.4 %all_to_all.76 = f32[16,1,2]{2,1,0:T(1,128)S(1)} all-to-all(f32[16,1,2]{2,1,0:T(1,128)S(1)} %broadcast_in_dim.11), channel_id=1, replica_groups=mesh['tm'=32,'space'=16] {'space'}, dimensions={0} | all-to-all | bytes 256 | tf_op jit(solution)/shard_map/cond/branch_0_fun/all_to_all | solution.py:555
  (164 shorter events, 97.8 us)
Async XLA Ops:
  0.0 8.4 %collective-permute-start.31 = (f32[16,32,128]{2,1,0:T(8,128)}, f32[16,32,128]{2,1,0:T(8,128)S(1)}, u32[]{:S(2)}, u32[]{:S(2)}) collective-permute-start(f32[16,32,128]{2,1,0:T(8,128)} %bitcast.61), channel_id=1, source_target_pairs={{0,16},{16,32},{32,48},{48,64},{64,80},{80,96},{96,112},{112,128},... | collective-permute-start | bytes 786440 | tf_op jit(solution)/shard_map/ppermute | solution.py:523
  8.8 65.2 %copy-start = (f32[16,32,128]{2,1,0:T(8,128)S(1)}, f32[16,32,128]{2,1,0:T(8,128)}, u32[]{:S(2)}) copy-start(f32[16,32,128]{2,1,0:T(8,128)} %a.1) | copy-start | bytes 786436
  8.8 65.2 %copy-start.1 = (f32[16,32,128]{2,1,0:T(8,128)S(1)}, f32[16,32,128]{2,1,0:T(8,128)}, u32[]{:S(2)}) copy-start(f32[16,32,128]{2,1,0:T(8,128)} %f.1) | copy-start | bytes 786436
  8.8 65.2 %copy-start.5 = (f32[1,16,32,128]{3,2,1,0:T(8,128)S(1)}, f32[1,16,32,128]{3,2,1,0:T(8,128)}, u32[]{:S(2)}) copy-start(f32[1,16,32,128]{3,2,1,0:T(8,128)} %param.6) | copy-start | bytes 786436
  8.8 65.2 %copy-start.6 = (f32[1,16,32,128]{3,2,1,0:T(8,128)S(1)}, f32[1,16,32,128]{3,2,1,0:T(8,128)}, u32[]{:S(2)}) copy-start(f32[1,16,32,128]{3,2,1,0:T(8,128)} %param.7) | copy-start | bytes 786436
  8.9 33.7 %collective-permute-start.32 = (f32[13,4,8,128]{3,2,1,0:T(8,128)S(1)}, f32[13,4,8,128]{3,2,1,0:T(8,128)S(1)}, u32[]{:S(2)}, u32[]{:S(2)}) collective-permute-start(f32[13,4,8,128]{3,2,1,0:T(8,128)S(1)} %get-tuple-element.39), channel_id=1, source_target_pairs={{0,1},{1,2},{2,3},{3,4},{4,5},{5,6},{6,7},{7,8},{8,9},{9,10},{10,1... | collective-permute-start | bytes 638984 | tf_op jit(solution)/shard_map/ppermute | solution.py:530
  21.8 20.7 %collective-permute-start.33 = (f32[13,4,8,128]{3,2,1,0:T(8,128)S(1)}, f32[13,4,8,128]{3,2,1,0:T(8,128)S(1)}, u32[]{:S(2)}, u32[]{:S(2)}) collective-permute-start(f32[13,4,8,128]{3,2,1,0:T(8,128)S(1)} %get-tuple-element.40), channel_id=1, source_target_pairs={{1,0},{2,1},{3,2},{4,3},{5,4},{6,5},{7,6},{8,7},{9,8},{10,9},{11,1... | collective-permute-start | bytes 638984 | tf_op jit(solution)/shard_map/ppermute | solution.py:531
  23.8 13.2 %collective-permute-start.34 = (f32[12,4,8,128]{3,2,1,0:T(8,128)S(1)}, f32[12,4,8,128]{3,2,1,0:T(8,128)S(1)}, u32[]{:S(2)}, u32[]{:S(2)}) collective-permute-start(f32[12,4,8,128]{3,2,1,0:T(8,128)S(1)} %get-tuple-element.41), channel_id=1, source_target_pairs={{0,1},{1,50},{2,3},{3,52},{4,5},{5,54},{6,7},{7,56},{8,9},{9,58},{... | collective-permute-start | bytes 589832 | tf_op jit(solution)/shard_map/ppermute | solution.py:527
  32.2 10.3 %collective-permute-start.35 = (f32[12,4,8,128]{3,2,1,0:T(8,128)S(1)}, f32[12,4,8,128]{3,2,1,0:T(8,128)S(1)}, u32[]{:S(2)}, u32[]{:S(2)}) collective-permute-start(f32[12,4,8,128]{3,2,1,0:T(8,128)S(1)} %get-tuple-element.42), channel_id=1, source_target_pairs={{1,0},{2,49},{3,2},{4,51},{5,4},{6,53},{7,6},{8,55},{9,8},{10,57},... | collective-permute-start | bytes 589832 | tf_op jit(solution)/shard_map/ppermute | solution.py:528
  48.7 17.6 %all-to-all-start.12 = ((f32[16,8,128]{2,1,0:T(8,128)}), f32[16,8,128]{2,1,0:T(8,128)S(1)}, u32[]{:S(2)}, u32[]{:S(2)}) async-start(f32[16,8,128]{2,1,0:T(8,128)} %get-tuple-element.43), calls=%async_computation.12 | async-start | bytes 131072 | tf_op jit(solution)/shard_map/all_to_all | solution.py:542
  74.0 23.3 %copy-start.2 = (f32[16,32,128]{2,1,0:T(8,128)}, f32[16,32,128]{2,1,0:T(8,128)S(1)}, u32[]{:S(2)}) copy-start(f32[16,32,128]{2,1,0:T(8,128)S(1)} %get-tuple-element.19) | copy-start | bytes 786436 | tf_op jit(solution)/shard_map/cond
  74.1 6.8 %collective-permute-start = (f32[16,32,128]{2,1,0:T(8,128)S(1)}, f32[16,32,128]{2,1,0:T(8,128)S(1)}, u32[]{:S(2)}, u32[]{:S(2)}) collective-permute-start(f32[16,32,128]{2,1,0:T(8,128)S(1)} %bitcast.62), channel_id=1, source_target_pairs={{0,16},{16,32},{32,48},{48,64},{64,80},{80,96},{96,112},{112,128},... | collective-permute-start | bytes 786440 | tf_op jit(solution)/shard_map/cond/branch_0_fun/ppermute | solution.py:592
  75.4 14.3 %collective-permute-start.3 = (f32[1,32,128]{2,1,0:T(8,128)S(1)}, f32[1,32,128]{2,1,0:T(8,128)S(1)}, u32[]{:S(2)}, u32[]{:S(2)}) collective-permute-start(f32[1,32,128]{2,1,0:T(8,128)S(1)} %get-tuple-element.117), channel_id=1, source_target_pairs={{0,1},{1,2},{2,3},{3,4},{4,5},{5,6},{6,7},{7,8},{8,9},{9,10},{10,1... | collective-permute-start | bytes 49160 | tf_op jit(solution)/shard_map/cond/branch_0_fun/ppermute | solution.py:580
  78.0 11.7 %collective-permute-start.1 = (f32[1,32,128]{2,1,0:T(8,128)S(1)}, f32[1,32,128]{2,1,0:T(8,128)S(1)}, u32[]{:S(2)}, u32[]{:S(2)}) collective-permute-start(f32[1,32,128]{2,1,0:T(8,128)S(1)} %get-tuple-element.118), channel_id=1, source_target_pairs={{1,0},{2,1},{3,2},{4,3},{5,4},{6,5},{7,6},{8,7},{9,8},{10,9},{11,1... | collective-permute-start | bytes 49160 | tf_op jit(solution)/shard_map/cond/branch_0_fun/ppermute | solution.py:582
  80.9 9.0 %collective-permute-start.4 = (f32[1,32,128]{2,1,0:T(8,128)S(1)}, f32[1,32,128]{2,1,0:T(8,128)S(1)}, u32[]{:S(2)}, u32[]{:S(2)}) collective-permute-start(f32[1,32,128]{2,1,0:T(8,128)S(1)} %get-tuple-element.119), channel_id=1, source_target_pairs={{0,1},{1,2},{2,3},{3,4},{4,5},{5,6},{6,7},{7,8},{8,9},{9,10},{10,1... | collective-permute-start | bytes 49160 | tf_op jit(solution)/shard_map/cond/branch_0_fun/ppermute | solution.py:580
  87.5 9.0 %collective-permute-start.2 = (f32[1,32,128]{2,1,0:T(8,128)S(1)}, f32[1,32,128]{2,1,0:T(8,128)S(1)}, u32[]{:S(2)}, u32[]{:S(2)}) collective-permute-start(f32[1,32,128]{2,1,0:T(8,128)S(1)} %get-tuple-element.120), channel_id=1, source_target_pairs={{1,0},{2,1},{3,2},{4,3},{5,4},{6,5},{7,6},{8,7},{9,8},{10,9},{11,1... | collective-permute-start | bytes 49160 | tf_op jit(solution)/shard_map/cond/branch_0_fun/ppermute | solution.py:582
  97.4 4.3 collective-permute-start.6
  99.3 10.5 %collective-permute-start.5 = (f32[1,32,128]{2,1,0:T(8,128)S(1)}, f32[1,32,128]{2,1,0:T(8,128)S(1)}, u32[]{:S(2)}, u32[]{:S(2)}) collective-permute-start(f32[1,32,128]{2,1,0:T(8,128)S(1)} %get-tuple-element.116), channel_id=1, source_target_pairs={{1,0},{2,1},{3,2},{4,3},{5,4},{6,5},{7,6},{8,7},{9,8},{10,9},{11,1... | collective-permute-start | bytes 49160 | tf_op jit(solution)/shard_map/cond/branch_0_fun/ppermute | solution.py:582
  132.9 4.7 collective-permute-start.8
  135.6 9.0 %collective-permute-start.7 = (f32[1,32,128]{2,1,0:T(8,128)S(1)}, f32[1,32,128]{2,1,0:T(8,128)S(1)}, u32[]{:S(2)}, u32[]{:S(2)}) collective-permute-start(f32[1,32,128]{2,1,0:T(8,128)S(1)} %get-tuple-element.114), channel_id=1, source_target_pairs={{1,0},{2,1},{3,2},{4,3},{5,4},{6,5},{7,6},{8,7},{9,8},{10,9},{11,1... | collective-permute-start | bytes 49160 | tf_op jit(solution)/shard_map/cond/branch_0_fun/ppermute | solution.py:582
  170.8 4.7 collective-permute-start.10
  173.6 9.0 %collective-permute-start.9 = (f32[1,32,128]{2,1,0:T(8,128)S(1)}, f32[1,32,128]{2,1,0:T(8,128)S(1)}, u32[]{:S(2)}, u32[]{:S(2)}) collective-permute-start(f32[1,32,128]{2,1,0:T(8,128)S(1)} %get-tuple-element.112), channel_id=1, source_target_pairs={{1,0},{2,1},{3,2},{4,3},{5,4},{6,5},{7,6},{8,7},{9,8},{10,9},{11,1... | collective-permute-start | bytes 49160 | tf_op jit(solution)/shard_map/cond/branch_0_fun/ppermute | solution.py:582
  209.7 49.5 %copy-start.3 = (f32[16,32,128]{2,1,0:T(8,128)}, f32[16,32,128]{2,1,0:T(8,128)S(1)}, u32[]{:S(2)}) copy-start(f32[16,32,128]{2,1,0:T(8,128)S(1)} %get-tuple-element.82) | copy-start | bytes 786436 | tf_op jit(solution)/shard_map/cond
  209.8 4.7 collective-permute-start.12
  212.5 9.0 %collective-permute-start.11 = (f32[1,32,128]{2,1,0:T(8,128)S(1)}, f32[1,32,128]{2,1,0:T(8,128)S(1)}, u32[]{:S(2)}, u32[]{:S(2)}) collective-permute-start(f32[1,32,128]{2,1,0:T(8,128)S(1)} %get-tuple-element.110), channel_id=1, source_target_pairs={{1,0},{2,1},{3,2},{4,3},{5,4},{6,5},{7,6},{8,7},{9,8},{10,9},{11,1... | collective-permute-start | bytes 49160 | tf_op jit(solution)/shard_map/cond/branch_0_fun/ppermute | solution.py:582
  247.2 4.7 collective-permute-start.14
  250.0 9.0 %collective-permute-start.13 = (f32[1,32,128]{2,1,0:T(8,128)S(1)}, f32[1,32,128]{2,1,0:T(8,128)S(1)}, u32[]{:S(2)}, u32[]{:S(2)}) collective-permute-start(f32[1,32,128]{2,1,0:T(8,128)S(1)} %get-tuple-element.108), channel_id=1, source_target_pairs={{1,0},{2,1},{3,2},{4,3},{5,4},{6,5},{7,6},{8,7},{9,8},{10,9},{11,1... | collective-permute-start | bytes 49160 | tf_op jit(solution)/shard_map/cond/branch_0_fun/ppermute | solution.py:582
  286.0 4.7 collective-permute-start.16
  288.8 9.0 %collective-permute-start.15 = (f32[1,32,128]{2,1,0:T(8,128)S(1)}, f32[1,32,128]{2,1,0:T(8,128)S(1)}, u32[]{:S(2)}, u32[]{:S(2)}) collective-permute-start(f32[1,32,128]{2,1,0:T(8,128)S(1)} %get-tuple-element.106), channel_id=1, source_target_pairs={{1,0},{2,1},{3,2},{4,3},{5,4},{6,5},{7,6},{8,7},{9,8},{10,9},{11,1... | collective-permute-start | bytes 49160 | tf_op jit(solution)/shard_map/cond/branch_0_fun/ppermute | solution.py:582
  323.4 4.7 collective-permute-start.18
  326.2 9.0 %collective-permute-start.17 = (f32[1,32,128]{2,1,0:T(8,128)S(1)}, f32[1,32,128]{2,1,0:T(8,128)S(1)}, u32[]{:S(2)}, u32[]{:S(2)}) collective-permute-start(f32[1,32,128]{2,1,0:T(8,128)S(1)} %get-tuple-element.104), channel_id=1, source_target_pairs={{1,0},{2,1},{3,2},{4,3},{5,4},{6,5},{7,6},{8,7},{9,8},{10,9},{11,1... | collective-permute-start | bytes 49160 | tf_op jit(solution)/shard_map/cond/branch_0_fun/ppermute | solution.py:582
  336.7 4.3 collective-permute-start.20
  338.7 9.7 %collective-permute-start.19 = (f32[1,32,128]{2,1,0:T(8,128)S(1)}, f32[1,32,128]{2,1,0:T(8,128)S(1)}, u32[]{:S(2)}, u32[]{:S(2)}) collective-permute-start(f32[1,32,128]{2,1,0:T(8,128)S(1)} %get-tuple-element.102), channel_id=1, source_target_pairs={{1,0},{2,1},{3,2},{4,3},{5,4},{6,5},{7,6},{8,7},{9,8},{10,9},{11,1... | collective-permute-start | bytes 49160 | tf_op jit(solution)/shard_map/cond/branch_0_fun/ppermute | solution.py:582
  371.6 4.7 collective-permute-start.22
  374.3 9.0 %collective-permute-start.21 = (f32[1,32,128]{2,1,0:T(8,128)S(1)}, f32[1,32,128]{2,1,0:T(8,128)S(1)}, u32[]{:S(2)}, u32[]{:S(2)}) collective-permute-start(f32[1,32,128]{2,1,0:T(8,128)S(1)} %get-tuple-element.100), channel_id=1, source_target_pairs={{1,0},{2,1},{3,2},{4,3},{5,4},{6,5},{7,6},{8,7},{9,8},{10,9},{11,1... | collective-permute-start | bytes 49160 | tf_op jit(solution)/shard_map/cond/branch_0_fun/ppermute | solution.py:582
  409.4 4.7 collective-permute-start.24
  412.2 9.0 %collective-permute-start.23 = (f32[1,32,128]{2,1,0:T(8,128)S(1)}, f32[1,32,128]{2,1,0:T(8,128)S(1)}, u32[]{:S(2)}, u32[]{:S(2)}) collective-permute-start(f32[1,32,128]{2,1,0:T(8,128)S(1)} %get-tuple-element.98), channel_id=1, source_target_pairs={{1,0},{2,1},{3,2},{4,3},{5,4},{6,5},{7,6},{8,7},{9,8},{10,9},{11,1... | collective-permute-start | bytes 49160 | tf_op jit(solution)/shard_map/cond/branch_0_fun/ppermute | solution.py:582
  448.3 4.7 collective-permute-start.26
  451.1 9.0 %collective-permute-start.25 = (f32[1,32,128]{2,1,0:T(8,128)S(1)}, f32[1,32,128]{2,1,0:T(8,128)S(1)}, u32[]{:S(2)}, u32[]{:S(2)}) collective-permute-start(f32[1,32,128]{2,1,0:T(8,128)S(1)} %get-tuple-element.96), channel_id=1, source_target_pairs={{1,0},{2,1},{3,2},{4,3},{5,4},{6,5},{7,6},{8,7},{9,8},{10,9},{11,1... | collective-permute-start | bytes 49160 | tf_op jit(solution)/shard_map/cond/branch_0_fun/ppermute | solution.py:582
  461.4 62.2 %copy-start.4 = (f32[16,32,128]{2,1,0:T(8,128)}, f32[16,32,128]{2,1,0:T(8,128)S(1)}, u32[]{:S(2)}) copy-start(f32[16,32,128]{2,1,0:T(8,128)S(1)} %get-tuple-element.73) | copy-start | bytes 786436 | tf_op jit(solution)/shard_map/cond
  485.4 4.7 collective-permute-start.28
  488.2 9.0 %collective-permute-start.27 = (f32[1,32,128]{2,1,0:T(8,128)S(1)}, f32[1,32,128]{2,1,0:T(8,128)S(1)}, u32[]{:S(2)}, u32[]{:S(2)}) collective-permute-start(f32[1,32,128]{2,1,0:T(8,128)S(1)} %get-tuple-element.94), channel_id=1, source_target_pairs={{1,0},{2,1},{3,2},{4,3},{5,4},{6,5},{7,6},{8,7},{9,8},{10,9},{11,1... | collective-permute-start | bytes 49160 | tf_op jit(solution)/shard_map/cond/branch_0_fun/ppermute | solution.py:582
  524.7 4.7 collective-permute-start.30
  527.5 9.0 %collective-permute-start.29 = (f32[1,32,128]{2,1,0:T(8,128)S(1)}, f32[1,32,128]{2,1,0:T(8,128)S(1)}, u32[]{:S(2)}, u32[]{:S(2)}) collective-permute-start(f32[1,32,128]{2,1,0:T(8,128)S(1)} %get-tuple-element.92), channel_id=1, source_target_pairs={{1,0},{2,1},{3,2},{4,3},{5,4},{6,5},{7,6},{8,7},{9,8},{10,9},{11,1... | collective-permute-start | bytes 49160 | tf_op jit(solution)/shard_map/cond/branch_0_fun/ppermute | solution.py:582
where the time goes:
time: 569 us; the launch traced here: 563 us
  blocking collectives  221 us (39%)
  waiting for transfers between devices  121 us (21%)
  starting transfers between devices  113 us (20%)
  other arithmetic  42.9 us (8%)
  loops' own time  42.6 us (7%)
  Pallas kernels  14.1 us (2%)
  local copies, waits for them, and re-layouts  8.35 us (1%)
    all_to_all x12, blocking collectives, copy_for_each(): lax.all_to_all(jnp.broadcast_to(array[None], (devices, *array.shape)), ax...  221 us
    ppermute x15, waiting for transfers between devices, extended(): lax.ppermute(head, axis, [((i + 1) % count, i) for i in range(ends)])  99.2 us
    ppermute x15, starting transfers between devices, extended(): lax.ppermute(tail, axis, [(i, (i + 1) % count) for i in range(ends)])  43.5 us
    another operation x1, loops' own time, body(): return lax.cond(good[0, 0] > 0, lambda: out, lambda: plain(*args))  42.6 us
    ppermute x15, starting transfers between devices, extended(): lax.ppermute(head, axis, [((i + 1) % count, i) for i in range(ends)])  29.9 us
    concatenate x12, other arithmetic, packed_total(): subtotal = over_copies(jnp.concatenate([a.ravel() for a in arrays]), axis)  15.6 us
    reduce_sum x12, other arithmetic, pair_sums(): jnp.sum(residual * residual)  15.1 us
    ppermute x1, starting transfers between devices, fast(): lo = lax.ppermute(tail, 'space', up)  13 us
  transfers between devices with their start and end apart: 37, of which 19 were waited for; matrix products, arithmetic and copies ran while one was open for 0% of the time, Pallas kernels for 0%

commit v1 on v0

--- a/solution.py
+++ b/solution.py
@@ -116,22 +116,25 @@
         both = (hi, lo)
         for shift in (64, 32, 16, 8, 4, 2, 1):
             both = add2(both, (roll(both[0], shift, 1), roll(both[1], shift, 1)))
-        result = jnp.where(lane == g, both[0], result)
-        result = jnp.where(lane == GROUPS_OF_8 + g, both[1], result)
+        result = jnp.where(lane == 8 * g + row, both[0], result)
+        result = jnp.where(lane == 64 + 8 * g + row, both[1], result)
+    for shift in (4, 2, 1):
+        result = result + roll(result, shift, 0)
     for p in range(out.shape[0]):
-        out[p] = result
+        out[p] = result[0:1]
 
 
 def unpack(gathered):
-    hi = gathered[0]
+    whole = (SUB, LANES)
+    row = lambda p: jnp.broadcast_to(gathered[p], whole)
+    hi = row(0)
     lo = jnp.zeros_like(hi)
     for p in range(1, gathered.shape[0]):
-        hi, e = two_sum(hi, gathered[p])
+        hi, e = two_sum(hi, row(p))
         lo = lo + e
-    lo = lo + roll(hi, -GROUPS_OF_8, 1)
+    lo = lo + roll(hi, 64, 1)
     hi, lo = quick_two_sum(hi, lo)
-    whole = (SUB, LANES)
-    spot = lambda v, i: jnp.broadcast_to(v[i % 8 : i % 8 + 1, i // 8 : i // 8 + 1], whole)
+    spot = lambda v, i: jnp.broadcast_to(v[:, i : i + 1], whole)
     return [(spot(hi, i), spot(lo, i)) for i in range(TOTALS)]
 
 
@@ -236,7 +239,7 @@
 
 
 def fill_weights(conduct, fields, first, last):
-    wz, wy, wx, wl, bd = fields
+    wz, wy, wx, wl, bd, dg = fields
     row = lax.broadcasted_iota(jnp.int32, (SUB, LANES), 0)
     lane = lax.broadcasted_iota(jnp.int32, (SUB, LANES), 1)
     not_last_lane = jnp.where(lane < LANES - 1, FACE, 0.0)
@@ -253,41 +256,44 @@
         for q in range(4):
             if e < last:
                 wz[z, q] = FACE * (here[q] + above[q])
-            wx[z, q] = not_last_lane * (here[q] + roll(here[q], -1, 1))
-            wl[z, q] = not_first_lane * (here[q] + roll(here[q], 1, 1))
+            right = not_last_lane * (here[q] + roll(here[q], -1, 1))
+            left = not_first_lane * (here[q] + roll(here[q], 1, 1))
+            bound = edge[q] * here[q]
+            wx[z, q] = right
+            wl[z, q] = left
             wy[z, q] = (FACE if q < 3 else not_last_row) * (here[q] + nxt[q])
-            bd[z, q] = edge[q] * here[q]
+            bd[z, q] = bound
+            dg[z, q] = KAPPA + (bound + (right + left))
         here = above
 
 
-def flat_part(e, here, fields):
-    _, wy, wx, wl, _ = fields
-    right = [roll(v, -1, 1) for v in here]
-    left = [roll(v, 1, 1) for v in here]
-    nxt = [here[1], here[2], here[3], roll(here[0], -1, 0)]
-    fy = [wy[e, k] * (nxt[k] - here[k]) for k in range(4)]
-    prv = [roll(fy[3], 1, 0), fy[0], fy[1], fy[2]]
-    return [
-        (fy[k] - prv[k]) + (wx[e, k] * (right[k] - here[k]) - wl[e, k] * (here[k] - left[k])) for k in range(4)
-    ]
-
-
-def divergence(load, fields, first, last, emit, closed=False):
-    wz = fields[0]
+def across(load, fields, first, last, emit, residual=False):
+    wz, wy, wx, wl, bd, dg = fields
     here = load(first)
-    if not closed:
+    if not residual:
         below = load(first - 1)
         flux_below = [wz[first - 1, k] * (here[k] - below[k]) for k in range(4)]
     for e in range(first, last + 1):
-        div = flat_part(e, here, fields)
-        if not (closed and e == last):
+        right = [roll(v, -1, 1) for v in here]
+        left = [roll(v, 1, 1) for v in here]
+        nxt = [here[1], here[2], here[3], roll(here[0], -1, 0)]
+        fy = [wy[e, k] * (nxt[k] - here[k]) for k in range(4)]
+        prv = [roll(fy[3], 1, 0), fy[0], fy[1], fy[2]]
+        if residual:
+            w = [
+                bd[e, k] * here[k] - (wx[e, k] * (right[k] - here[k]) - wl[e, k] * (here[k] - left[k])) for k in range(4)
+            ]
+        else:
+            w = [dg[e, k] * here[k] - wx[e, k] * right[k] - wl[e, k] * left[k] for k in range(4)]
+        w = [w[k] - fy[k] + prv[k] for k in range(4)]
+        if not (residual and e == last):
             above = load(e + 1)
             flux_above = [wz[e, k] * (above[k] - here[k]) for k in range(4)]
-            div = [d + f for d, f in zip(div, flux_above)]
-        if not (closed and e == first):
-            div = [d - f for d, f in zip(div, flux_below)]
-        emit(e, here, div)
-        if not (closed and e == last):
+            w = [d - f for d, f in zip(w, flux_above)]
+        if not (residual and e == first):
+            w = [d + f for d, f in zip(w, flux_below)]
+        emit(e, here, w)
+        if not (residual and e == last):
             here, flux_below = above, flux_above
 
 
@@ -338,18 +344,17 @@
                 head[RIM, q] = v
             if z == depth - 1:
                 tail[RIM, q] = v
-    bd = fields[-1]
-
-    def emit(z, v, div):
+
+    def emit(z, v, image):
         for q in range(4):
-            r = SOURCE_WEIGHT * f[z, q] - (1.0 / SIGMA) * (bd[z, q] * v[q] - div[q])
+            r = SOURCE_WEIGHT * f[z, q] - (1.0 / SIGMA) * image[q]
             res[z, q] = r
             if z < RIM:
                 head[z, q] = r
             if z >= depth - RIM:
                 tail[z - depth + RIM, q] = r
 
-    divergence(planes(x), fields, 0, depth - 1, emit, closed=True)
+    across(planes(x), fields, 0, depth - 1, emit, residual=True)
 
 
 def basis_kernel(x, res, lo, hi, a, alo, ahi, basis, sums, kept, ring, done, *fields):
@@ -358,7 +363,7 @@
     low, high = RIM - 1, RIM + depth
     mask = inside(alo, ahi, low, high)
     fill_weights(conductivities(a, alo, ahi), fields, 0, span - 1)
-    wz, bd = fields[0], fields[-1]
+    wz = fields[0]
     first, count = RIM - KEEP, depth + 2 * KEEP
     totals = {}
 
@@ -411,8 +416,7 @@
     copy(0).start()
     for k in range(1, RIM + 1):
 
-        def emit(e, v, div, k=k):
-            image = [(KAPPA + bd[e, q]) * v[q] - div[q] for q in range(4)]
+        def emit(e, v, image, k=k):
             if k == 1:
                 new = [0.5 * i for i in image]
             else:
@@ -420,7 +424,7 @@
                 new = [i - ref[slot, e, q] for q, i in enumerate(image)]
             store(k, e, new, v)
 
-        divergence(planes(*place(k - 1)), fields, k, span - 1 - k, emit)
+        across(planes(*place(k - 1)), fields, k, span - 1 - k, emit)
         if k <= ITERS:
             copy(k).start()
     pack([totals[i] for i in range(TOTALS)], sums)
@@ -437,9 +441,8 @@
     mask = inside(alo, ahi, KEEP - 1, KEEP + depth)
     conduct = conductivities(a, alo, ahi)
     fill_weights(lambda e: conduct(e + first), fields, 0, count - 1)
-    bd = fields[-1]
     c1, q1, c2, good = solve(unpack(gathered))
-    flag[...] = good
+    flag[0] = good[0, 0].astype(jnp.int32)
     for copy in copies:
         copy.wait()
 
@@ -475,29 +478,34 @@
         store(0, e, new)
     for k in range(1, ITERS):
 
-        def emit(e, v, div, k=k):
-            image = [(KAPPA + bd[e, q]) * v[q] - div[q] for q in range(4)]
+        def emit(e, v, image, k=k):
             if k == 1:
                 new = [0.5 * i for i in image]
             else:
                 new = [i - ring[(k - 2) % 3, e, q] for q, i in enumerate(image)]
             store(k, e, new)
 
-        divergence(planes(ring, (k - 1) % 3), fields, k, count - 1 - k, emit)
+        across(planes(ring, (k - 1) % 3), fields, k, count - 1 - k, emit)
 
 
 def call(kernel, outs, scratch, sent=None, read=None, inputs=0, copies=0, weights=True):
     vmem = pl.BlockSpec(memory_space=pltpu.VMEM)
     hbm = pl.BlockSpec(memory_space=pltpu.HBM)
+    smem = pl.BlockSpec(memory_space=pltpu.SMEM)
     own = [pltpu.VMEM(s, jnp.float32) for s in scratch]
     if copies:
         own.append(pltpu.SemaphoreType.DMA((copies,)))
     return lambda fields: pl.pallas_call(
         kernel,
-        out_shape=[(pltpu.HBM if i == sent else jax.ShapeDtypeStruct)(s, jnp.float32) for i, s in enumerate(outs)],
+        out_shape=[
+            jax.ShapeDtypeStruct((1,), jnp.int32)
+            if s is None
+            else (pltpu.HBM if i == sent else jax.ShapeDtypeStruct)(s, jnp.float32)
+            for i, s in enumerate(outs)
+        ],
         in_specs=[hbm if i == read else vmem for i in range(inputs)],
-        out_specs=[hbm if i == sent else vmem for i in range(len(outs))],
-        scratch_shapes=own + [pltpu.VMEM(fields, jnp.float32)] * (5 if weights else 0),
+        out_specs=[smem if s is None else hbm if i == sent else vmem for i, s in enumerate(outs)],
+        scratch_shapes=own + [pltpu.VMEM(fields, jnp.float32)] * (6 if weights else 0),
         compiler_params=pltpu.CompilerParams(vmem_limit_bytes=20 * 2**20),
     )
 
@@ -511,28 +519,20 @@
     down = [(i + 1, i) for i in range(slabs - 1)]
     later = [(i, i + 1) for i in range(times - 1)]
 
-    def short(moves):
-        pairs = []
-        for t in range(times):
-            for s, d in moves:
-                u = t if (s // 2) % 2 == (d // 2) % 2 else t // 4 * 4 + 3 - t % 4
-                pairs.append((t * slabs + s, u * slabs + d))
-        return pairs
-
     own, sent, rim = (depth, *tile), (RIM + 1, *tile), (RIM, *tile)
     fix = lax.ppermute(corrections[0], "tm", later)
     point, source, cond, tail, head = call(
         stage_kernel, [own, own, own, rim, rim], [], inputs=3, weights=False
     )(own)(c_points[0], forcing, conductivity)
-    alo = lax.ppermute(tail, ("tm", "space"), short(up))
-    ahi = lax.ppermute(head, ("tm", "space"), short(down))
+    alo = lax.ppermute(tail, "space", up)
+    ahi = lax.ppermute(head, "space", down)
     x, res, tail, head = call(open_kernel, [own, own, sent, sent], [], inputs=4)(own)(point, fix, source, cond)
     lo = lax.ppermute(tail, "space", up)
     hi = lax.ppermute(head, "space", down)
     field, part = (span, *tile), (count, *tile)
     basis, sums = call(
         basis_kernel,
-        [(ITERS + 1, *part), (slabs, SUB, LANES)],
+        [(ITERS + 1, *part), (slabs, 1, LANES)],
         [(ITERS + 1, *field), (3, *field)],
         sent=0,
         inputs=7,
@@ -542,7 +542,7 @@
     sums = lax.all_to_all(sums, "space", 0, 0, tiled=True)
     return call(
         states_kernel,
-        [(1, STEPS, depth, 4 * SUB, LANES), (SUB, LANES)],
+        [(1, STEPS, depth, 4 * SUB, LANES), None],
         [(ITERS + 1, *part), (3, *part), own],
         read=1,
         inputs=6,
@@ -664,7 +664,7 @@
 def body(c_points, corrections, conductivity, forcing):
     args = (c_points, corrections, conductivity, forcing)
     out, good = fast(*args)
-    return lax.cond(good[0, 0] > 0, lambda: out, lambda: plain(*args))
+    return lax.cond(good[0] > 0, lambda: out, lambda: plain(*args))
 
 
 def solution(mesh):

time: 569 us -> 569 us (level)
  transfers between devices with their start and end apart: 37 -> 37, of which waited for: 19 -> 18; matrix products, arithmetic and copies ran while one was open for 0% -> 0% of each run, Pallas kernels for 0% -> 0%
where the time goes in v1:
time: 569 us; the launch traced here: 565 us
  blocking collectives  221 us (39%)
  waiting for transfers between devices  122 us (21%)
  starting transfers between devices  115 us (20%)
  other arithmetic  42.9 us (8%)
  loops' own time  42.6 us (7%)
  Pallas kernels  13.3 us (2%)
  local copies, waits for them, and re-layouts  7.75 us (1%)
    all_to_all x12, blocking collectives, copy_for_each(): lax.all_to_all(jnp.broadcast_to(array[None], (devices, *array.shape)), ax...  221 us
    ppermute x15, waiting for transfers between devices, extended(): lax.ppermute(head, axis, [((i + 1) % count, i) for i in range(ends)])  99.3 us
    ppermute x15, starting transfers between devices, extended(): lax.ppermute(tail, axis, [(i, (i + 1) % count) for i in range(ends)])  44.8 us
    another operation x1, loops' own time, body(): return lax.cond(good[0] > 0, lambda: out, lambda: plain(*args))  42.6 us
    ppermute x15, starting transfers between devices, extended(): lax.ppermute(head, axis, [((i + 1) % count, i) for i in range(ends)])  29.9 us
    concatenate x12, other arithmetic, packed_total(): subtotal = over_copies(jnp.concatenate([a.ravel() for a in arrays]), axis)  15.6 us
    reduce_sum x12, other arithmetic, pair_sums(): jnp.sum(residual * residual)  15.1 us
    ppermute x1, starting transfers between devices, fast(): lo = lax.ppermute(tail, 'space', up)  13 us
  transfers between devices with their start and end apart: 37, of which 18 were waited for; matrix products, arithmetic and copies ran while one was open for 0% of the time, Pallas kernels for 0%

profile of v1, /device:TPU:1, one launch (start us, length us, event | category | flops | bytes accessed | tf_op | source)
XLA Modules:
  0.0 564.8 jit_solution(4676926898200620296)
XLA Ops:
  0.0 4.8 collective-permute-start.31
  8.9 13.0 %collective-permute-start.32 = (f32[13,4,8,128]{3,2,1,0:T(8,128)S(1)}, f32[13,4,8,128]{3,2,1,0:T(8,128)S(1)}, u32[]{:S(2)}, u32[]{:S(2)}) collective-permute-start(f32[13,4,8,128]{3,2,1,0:T(8,128)S(1)} %get-tuple-element.39), channel_id=1, source_target_pairs={{0,1},{1,2},{2,3},{3,4},{4,5},{5,6},{6,7},{7,8},{8,9},{9,10},{10,1... | collective-permute-start | bytes 638984 | tf_op jit(solution)/shard_map/ppermute | solution.py:530
  23.7 7.5 %collective-permute-start.34 = (f32[12,4,8,128]{3,2,1,0:T(8,128)S(1)}, f32[12,4,8,128]{3,2,1,0:T(8,128)S(1)}, u32[]{:S(2)}, u32[]{:S(2)}) collective-permute-start(f32[12,4,8,128]{3,2,1,0:T(8,128)S(1)} %get-tuple-element.41), channel_id=1, source_target_pairs={{0,1},{1,2},{2,3},{3,4},{4,5},{5,6},{6,7},{7,8},{8,9},{9,10},{10,1... | collective-permute-start | bytes 589832 | tf_op jit(solution)/shard_map/ppermute | solution.py:527
  33.9 9.8 %collective-permute-done.35.ahi = f32[12,4,8,128]{3,2,1,0:T(8,128)S(1)} collective-permute-done((f32[12,4,8,128]{3,2,1,0:T(8,128)S(1)}, f32[12,4,8,128]{3,2,1,0:T(8,128)S(1)}, u32[]{:S(2)}, u32[]{:S(2)}) %collective-permute-start.35) | collective-permute-done | bytes 196640 | tf_op jit(solution)/shard_map/ppermute | solution.py:528
  43.8 5.8 %shard_map.50 = (f32[7,26,4,8,128]{4,3,2,1,0:T(8,128)}, f32[16,1,128]{2,1,0:T(1,128)}) custom-call(f32[16,4,8,128]{3,2,1,0:T(8,128)S(1)} %get-tuple-element.37.x, f32[16,4,8,128]{3,2,1,0:T(8,128)S(1)} %get-tuple-element.38.res, f32[13,4,8,128]{3,2,1,0:T(8,128)S(1)} %collective-permute-done.32.lo, f32[13,4,8,128]{3,2,1,0:T(8,128)S(1)} %collective-permute-done.33.hi, ...), custom_call_target="tpu_custom_call" | custom-call | tf_op jit(solution)/shard_map/pallas_call | solution.py:533
  49.6 6.8 %all-to-all-start.12 = ((f32[16,1,128]{2,1,0:T(1,128)}), f32[16,1,128]{2,1,0:T(1,128)S(1)}, u32[]{:S(2)}, u32[]{:S(2)}) async-start(f32[16,1,128]{2,1,0:T(1,128)} %get-tuple-element.43), calls=%async_computation.12 | async-start | bytes 16384 | tf_op jit(solution)/shard_map/all_to_all | solution.py:542
  56.4 9.3 %all-to-all-done.12.gathered = f32[16,1,128]{2,1,0:T(1,128)S(1)} async-done(((f32[16,1,128]{2,1,0:T(1,128)}), f32[16,1,128]{2,1,0:T(1,128)S(1)}, u32[]{:S(2)}, u32[]{:S(2)}) %all-to-all-start.12) | async-done | bytes 8224 | tf_op jit(solution)/shard_map/all_to_all | solution.py:542
  65.8 5.9 %shard_map.51 = (f32[1,2,16,32,128]{4,3,2,1,0:T(8,128)}, s32[1]{0:T(128)}) custom-call(f32[16,1,128]{2,1,0:T(1,128)S(1)} %all-to-all-done.12.gathered, f32[7,26,4,8,128]{4,3,2,1,0:T(8,128)} %get-tuple-element.44.basis, f32[16,4,8,128]{3,2,1,0:T(8,128)S(1)} %get-tuple-element.37.x, f32[16,4,8,128]{3,2,1,0:T(8,128)S(1)} %get-tuple-element.36.a, ...), custom_call_target="tpu_custom_call" | custom-call | tf_op jit(solution)/shard_map/pallas_call | solution.py:543
  72.3 492.5 %conditional.1 = (f32[1,2,16,32,128]{4,3,2,1,0:T(8,128)}) conditional(s32[]{:T(128)} %bitcast.55, (f32[1,16,32,128]{3,2,1,0:T(8,128)S(1)}, f32[1,16,32,128]{3,2,1,0:T(8,128)S(1)}, f32[16,32,128]{2,1,0:T(8,128)S(1)}, f32[16,32,128]{2,1,0:T(8,128)S(1)}) %tuple.75, f32[1,2,16,32,128]{4,3,2,1,0:T(8,128)} %get-tuple-element.46), branch_computations={%region_0.37_spmd, %region_37.38_spmd} | conditional | flops 52701000 | bytes 76249768 | solution.py:667
  72.3 4.2 collective-permute-start
  76.5 3.0 collective-permute-start.3
  81.6 7.5 %collective-permute-start.4 = (f32[1,32,128]{2,1,0:T(8,128)S(1)}, f32[1,32,128]{2,1,0:T(8,128)S(1)}, u32[]{:S(2)}, u32[]{:S(2)}) collective-permute-start(f32[1,32,128]{2,1,0:T(8,128)S(1)} %get-tuple-element.119), channel_id=1, source_target_pairs={{0,1},{1,2},{2,3},{3,4},{4,5},{5,6},{6,7},{7,8},{8,9},{9,10},{10,1... | collective-permute-start | bytes 49160 | tf_op jit(solution)/shard_map/cond/branch_0_fun/ppermute | solution.py:580
  91.4 6.7 %collective-permute-done.2 = f32[1,32,128]{2,1,0:T(8,128)S(1)} collective-permute-done((f32[1,32,128]{2,1,0:T(8,128)S(1)}, f32[1,32,128]{2,1,0:T(8,128)S(1)}, u32[]{:S(2)}, u32[]{:S(2)}) %collective-permute-start.2) | collective-permute-done | bytes 16416 | tf_op jit(solution)/shard_map/cond/branch_0_fun/ppermute | solution.py:582
  103.5 8.0 %collective-permute-done.5 = f32[1,32,128]{2,1,0:T(8,128)S(1)} collective-permute-done((f32[1,32,128]{2,1,0:T(8,128)S(1)}, f32[1,32,128]{2,1,0:T(8,128)S(1)}, u32[]{:S(2)}, u32[]{:S(2)}) %collective-permute-start.5) | collective-permute-done | bytes 16416 | tf_op jit(solution)/shard_map/cond/branch_0_fun/ppermute | solution.py:582
  114.1 18.6 %all_to_all.65 = f32[16,1,2]{2,1,0:T(1,128)S(1)} all-to-all(f32[16,1,2]{2,1,0:T(1,128)S(1)} %broadcast_in_dim.0), channel_id=1, replica_groups=mesh['tm'=32,'space'=16] {'space'}, dimensions={0} | all-to-all | bytes 256 | tf_op jit(solution)/shard_map/cond/branch_0_fun/all_to_all | solution.py:555
  134.6 2.8 collective-permute-start.8
  139.3 7.0 %collective-permute-done.7 = f32[1,32,128]{2,1,0:T(8,128)S(1)} collective-permute-done((f32[1,32,128]{2,1,0:T(8,128)S(1)}, f32[1,32,128]{2,1,0:T(8,128)S(1)}, u32[]{:S(2)}, u32[]{:S(2)}) %collective-permute-start.7) | collective-permute-done | bytes 16416 | tf_op jit(solution)/shard_map/cond/branch_0_fun/ppermute | solution.py:582
  148.8 18.4 %all_to_all.66 = f32[16,1,2]{2,1,0:T(1,128)S(1)} all-to-all(f32[16,1,2]{2,1,0:T(1,128)S(1)} %broadcast_in_dim.1), channel_id=1, replica_groups=mesh['tm'=32,'space'=16] {'space'}, dimensions={0} | all-to-all | bytes 256 | tf_op jit(solution)/shard_map/cond/branch_0_fun/all_to_all | solution.py:555
  172.5 2.8 collective-permute-start.10
  177.2 7.0 %collective-permute-done.9 = f32[1,32,128]{2,1,0:T(8,128)S(1)} collective-permute-done((f32[1,32,128]{2,1,0:T(8,128)S(1)}, f32[1,32,128]{2,1,0:T(8,128)S(1)}, u32[]{:S(2)}, u32[]{:S(2)}) %collective-permute-start.9) | collective-permute-done | bytes 16416 | tf_op jit(solution)/shard_map/cond/branch_0_fun/ppermute | solution.py:582
  187.5 18.4 %all_to_all.67 = f32[16,1,2]{2,1,0:T(1,128)S(1)} all-to-all(f32[16,1,2]{2,1,0:T(1,128)S(1)} %broadcast_in_dim.2), channel_id=1, replica_groups=mesh['tm'=32,'space'=16] {'space'}, dimensions={0} | all-to-all | bytes 256 | tf_op jit(solution)/shard_map/cond/branch_0_fun/all_to_all | solution.py:555
  211.5 2.8 collective-permute-start.12
  216.2 7.0 %collective-permute-done.11 = f32[1,32,128]{2,1,0:T(8,128)S(1)} collective-permute-done((f32[1,32,128]{2,1,0:T(8,128)S(1)}, f32[1,32,128]{2,1,0:T(8,128)S(1)}, u32[]{:S(2)}, u32[]{:S(2)}) %collective-permute-start.11) | collective-permute-done | bytes 16416 | tf_op jit(solution)/shard_map/cond/branch_0_fun/ppermute | solution.py:582
  225.9 18.4 %all_to_all.68 = f32[16,1,2]{2,1,0:T(1,128)S(1)} all-to-all(f32[16,1,2]{2,1,0:T(1,128)S(1)} %broadcast_in_dim.3), channel_id=1, replica_groups=mesh['tm'=32,'space'=16] {'space'}, dimensions={0} | all-to-all | bytes 256 | tf_op jit(solution)/shard_map/cond/branch_0_fun/all_to_all | solution.py:555
  248.9 2.8 collective-permute-start.14
  253.6 7.0 %collective-permute-done.13 = f32[1,32,128]{2,1,0:T(8,128)S(1)} collective-permute-done((f32[1,32,128]{2,1,0:T(8,128)S(1)}, f32[1,32,128]{2,1,0:T(8,128)S(1)}, u32[]{:S(2)}, u32[]{:S(2)}) %collective-permute-start.13) | collective-permute-done | bytes 16416 | tf_op jit(solution)/shard_map/cond/branch_0_fun/ppermute | solution.py:582
  263.9 18.4 %all_to_all.69 = f32[16,1,2]{2,1,0:T(1,128)S(1)} all-to-all(f32[16,1,2]{2,1,0:T(1,128)S(1)} %broadcast_in_dim.4), channel_id=1, replica_groups=mesh['tm'=32,'space'=16] {'space'}, dimensions={0} | all-to-all | bytes 256 | tf_op jit(solution)/shard_map/cond/branch_0_fun/all_to_all | solution.py:555
  287.7 2.8 collective-permute-start.16
  292.4 7.0 %collective-permute-done.15 = f32[1,32,128]{2,1,0:T(8,128)S(1)} collective-permute-done((f32[1,32,128]{2,1,0:T(8,128)S(1)}, f32[1,32,128]{2,1,0:T(8,128)S(1)}, u32[]{:S(2)}, u32[]{:S(2)}) %collective-permute-start.15) | collective-permute-done | bytes 16416 | tf_op jit(solution)/shard_map/cond/branch_0_fun/ppermute | solution.py:582
  302.1 18.4 %all_to_all.70 = f32[16,1,2]{2,1,0:T(1,128)S(1)} all-to-all(f32[16,1,2]{2,1,0:T(1,128)S(1)} %broadcast_in_dim.5), channel_id=1, replica_groups=mesh['tm'=32,'space'=16] {'space'}, dimensions={0} | all-to-all | bytes 256 | tf_op jit(solution)/shard_map/cond/branch_0_fun/all_to_all | solution.py:555
  325.1 2.8 collective-permute-start.18
  329.8 7.0 %collective-permute-done.17 = f32[1,32,128]{2,1,0:T(8,128)S(1)} collective-permute-done((f32[1,32,128]{2,1,0:T(8,128)S(1)}, f32[1,32,128]{2,1,0:T(8,128)S(1)}, u32[]{:S(2)}, u32[]{:S(2)}) %collective-permute-start.17) | collective-permute-done | bytes 16416 | tf_op jit(solution)/shard_map/cond/branch_0_fun/ppermute | solution.py:582
  342.8 7.3 %collective-permute-done.19 = f32[1,32,128]{2,1,0:T(8,128)S(1)} collective-permute-done((f32[1,32,128]{2,1,0:T(8,128)S(1)}, f32[1,32,128]{2,1,0:T(8,128)S(1)}, u32[]{:S(2)}, u32[]{:S(2)}) %collective-permute-start.19) | collective-permute-done | bytes 16416 | tf_op jit(solution)/shard_map/cond/branch_0_fun/ppermute | solution.py:582
  352.7 18.6 %all_to_all.71 = f32[16,1,2]{2,1,0:T(1,128)S(1)} all-to-all(f32[16,1,2]{2,1,0:T(1,128)S(1)} %broadcast_in_dim.6), channel_id=1, replica_groups=mesh['tm'=32,'space'=16] {'space'}, dimensions={0} | all-to-all | bytes 256 | tf_op jit(solution)/shard_map/cond/branch_0_fun/all_to_all | solution.py:555
  373.3 2.8 collective-permute-start.22
  378.0 7.0 %collective-permute-done.21 = f32[1,32,128]{2,1,0:T(8,128)S(1)} collective-permute-done((f32[1,32,128]{2,1,0:T(8,128)S(1)}, f32[1,32,128]{2,1,0:T(8,128)S(1)}, u32[]{:S(2)}, u32[]{:S(2)}) %collective-permute-start.21) | collective-permute-done | bytes 16416 | tf_op jit(solution)/shard_map/cond/branch_0_fun/ppermute | solution.py:582
  387.7 18.4 %all_to_all.72 = f32[16,1,2]{2,1,0:T(1,128)S(1)} all-to-all(f32[16,1,2]{2,1,0:T(1,128)S(1)} %broadcast_in_dim.7), channel_id=1, replica_groups=mesh['tm'=32,'space'=16] {'space'}, dimensions={0} | all-to-all | bytes 256 | tf_op jit(solution)/shard_map/cond/branch_0_fun/all_to_all | solution.py:555
  411.1 2.8 collective-permute-start.24
  415.8 7.0 %collective-permute-done.23 = f32[1,32,128]{2,1,0:T(8,128)S(1)} collective-permute-done((f32[1,32,128]{2,1,0:T(8,128)S(1)}, f32[1,32,128]{2,1,0:T(8,128)S(1)}, u32[]{:S(2)}, u32[]{:S(2)}) %collective-permute-start.23) | collective-permute-done | bytes 16416 | tf_op jit(solution)/shard_map/cond/branch_0_fun/ppermute | solution.py:582
  426.1 18.4 %all_to_all.73 = f32[16,1,2]{2,1,0:T(1,128)S(1)} all-to-all(f32[16,1,2]{2,1,0:T(1,128)S(1)} %broadcast_in_dim.8), channel_id=1, replica_groups=mesh['tm'=32,'space'=16] {'space'}, dimensions={0} | all-to-all | bytes 256 | tf_op jit(solution)/shard_map/cond/branch_0_fun/all_to_all | solution.py:555
  449.9 2.8 collective-permute-start.26
  454.6 7.0 %collective-permute-done.25 = f32[1,32,128]{2,1,0:T(8,128)S(1)} collective-permute-done((f32[1,32,128]{2,1,0:T(8,128)S(1)}, f32[1,32,128]{2,1,0:T(8,128)S(1)}, u32[]{:S(2)}, u32[]{:S(2)}) %collective-permute-start.25) | collective-permute-done | bytes 16416 | tf_op jit(solution)/shard_map/cond/branch_0_fun/ppermute | solution.py:582
  464.2 18.5 %all_to_all.74 = f32[16,1,2]{2,1,0:T(1,128)S(1)} all-to-all(f32[16,1,2]{2,1,0:T(1,128)S(1)} %broadcast_in_dim.9), channel_id=1, replica_groups=mesh['tm'=32,'space'=16] {'space'}, dimensions={0} | all-to-all | bytes 256 | tf_op jit(solution)/shard_map/cond/branch_0_fun/all_to_all | solution.py:555
  487.1 2.8 collective-permute-start.28
  491.8 7.0 %collective-permute-done.27 = f32[1,32,128]{2,1,0:T(8,128)S(1)} collective-permute-done((f32[1,32,128]{2,1,0:T(8,128)S(1)}, f32[1,32,128]{2,1,0:T(8,128)S(1)}, u32[]{:S(2)}, u32[]{:S(2)}) %collective-permute-start.27) | collective-permute-done | bytes 16416 | tf_op jit(solution)/shard_map/cond/branch_0_fun/ppermute | solution.py:582
  502.3 18.4 %all_to_all.75 = f32[16,1,2]{2,1,0:T(1,128)S(1)} all-to-all(f32[16,1,2]{2,1,0:T(1,128)S(1)} %broadcast_in_dim.10), channel_id=1, replica_groups=mesh['tm'=32,'space'=16] {'space'}, dimensions={0} | all-to-all | bytes 256 | tf_op jit(solution)/shard_map/cond/branch_0_fun/all_to_all | solution.py:555
  531.1 7.0 %collective-permute-done.29 = f32[1,32,128]{2,1,0:T(8,128)S(1)} collective-permute-done((f32[1,32,128]{2,1,0:T(8,128)S(1)}, f32[1,32,128]{2,1,0:T(8,128)S(1)}, u32[]{:S(2)}, u32[]{:S(2)}) %collective-permute-start.29) | collective-permute-done | bytes 16416 | tf_op jit(solution)/shard_map/cond/branch_0_fun/ppermute | solution.py:582
  540.8 18.4 %all_to_all.76 = f32[16,1,2]{2,1,0:T(1,128)S(1)} all-to-all(f32[16,1,2]{2,1,0:T(1,128)S(1)} %broadcast_in_dim.11), channel_id=1, replica_groups=mesh['tm'=32,'space'=16] {'space'}, dimensions={0} | all-to-all | bytes 256 | tf_op jit(solution)/shard_map/cond/branch_0_fun/all_to_all | solution.py:555
  (163 shorter events, 95.8 us)
Async XLA Ops:
  0.0 8.4 %collective-permute-start.31 = (f32[16,32,128]{2,1,0:T(8,128)}, f32[16,32,128]{2,1,0:T(8,128)S(1)}, u32[]{:S(2)}, u32[]{:S(2)}) collective-permute-start(f32[16,32,128]{2,1,0:T(8,128)} %bitcast.61), channel_id=1, source_target_pairs={{0,16},{16,32},{32,48},{48,64},{64,80},{80,96},{96,112},{112,128},... | collective-permute-start | bytes 786440 | tf_op jit(solution)/shard_map/ppermute | solution.py:523
  8.8 63.4 %copy-start = (f32[16,32,128]{2,1,0:T(8,128)S(1)}, f32[16,32,128]{2,1,0:T(8,128)}, u32[]{:S(2)}) copy-start(f32[16,32,128]{2,1,0:T(8,128)} %a.1) | copy-start | bytes 786436
  8.8 63.4 %copy-start.1 = (f32[16,32,128]{2,1,0:T(8,128)S(1)}, f32[16,32,128]{2,1,0:T(8,128)}, u32[]{:S(2)}) copy-start(f32[16,32,128]{2,1,0:T(8,128)} %f.1) | copy-start | bytes 786436
  8.8 63.4 %copy-start.5 = (f32[1,16,32,128]{3,2,1,0:T(8,128)S(1)}, f32[1,16,32,128]{3,2,1,0:T(8,128)}, u32[]{:S(2)}) copy-start(f32[1,16,32,128]{3,2,1,0:T(8,128)} %param.6) | copy-start | bytes 786436
  8.8 63.4 %copy-start.6 = (f32[1,16,32,128]{3,2,1,0:T(8,128)S(1)}, f32[1,16,32,128]{3,2,1,0:T(8,128)}, u32[]{:S(2)}) copy-start(f32[1,16,32,128]{3,2,1,0:T(8,128)} %param.7) | copy-start | bytes 786436
  8.9 34.9 %collective-permute-start.32 = (f32[13,4,8,128]{3,2,1,0:T(8,128)S(1)}, f32[13,4,8,128]{3,2,1,0:T(8,128)S(1)}, u32[]{:S(2)}, u32[]{:S(2)}) collective-permute-start(f32[13,4,8,128]{3,2,1,0:T(8,128)S(1)} %get-tuple-element.39), channel_id=1, source_target_pairs={{0,1},{1,2},{2,3},{3,4},{4,5},{5,6},{6,7},{7,8},{8,9},{9,10},{10,1... | collective-permute-start | bytes 638984 | tf_op jit(solution)/shard_map/ppermute | solution.py:530
  21.8 22.0 %collective-permute-start.33 = (f32[13,4,8,128]{3,2,1,0:T(8,128)S(1)}, f32[13,4,8,128]{3,2,1,0:T(8,128)S(1)}, u32[]{:S(2)}, u32[]{:S(2)}) collective-permute-start(f32[13,4,8,128]{3,2,1,0:T(8,128)S(1)} %get-tuple-element.40), channel_id=1, source_target_pairs={{1,0},{2,1},{3,2},{4,3},{5,4},{6,5},{7,6},{8,7},{9,8},{10,9},{11,1... | collective-permute-start | bytes 638984 | tf_op jit(solution)/shard_map/ppermute | solution.py:531
  23.7 10.2 %collective-permute-start.34 = (f32[12,4,8,128]{3,2,1,0:T(8,128)S(1)}, f32[12,4,8,128]{3,2,1,0:T(8,128)S(1)}, u32[]{:S(2)}, u32[]{:S(2)}) collective-permute-start(f32[12,4,8,128]{3,2,1,0:T(8,128)S(1)} %get-tuple-element.41), channel_id=1, source_target_pairs={{0,1},{1,2},{2,3},{3,4},{4,5},{5,6},{6,7},{7,8},{8,9},{9,10},{10,1... | collective-permute-start | bytes 589832 | tf_op jit(solution)/shard_map/ppermute | solution.py:527
  31.3 12.5 %collective-permute-start.35 = (f32[12,4,8,128]{3,2,1,0:T(8,128)S(1)}, f32[12,4,8,128]{3,2,1,0:T(8,128)S(1)}, u32[]{:S(2)}, u32[]{:S(2)}) collective-permute-start(f32[12,4,8,128]{3,2,1,0:T(8,128)S(1)} %get-tuple-element.42), channel_id=1, source_target_pairs={{1,0},{2,1},{3,2},{4,3},{5,4},{6,5},{7,6},{8,7},{9,8},{10,9},{11,1... | collective-permute-start | bytes 589832 | tf_op jit(solution)/shard_map/ppermute | solution.py:528
  49.6 16.2 %all-to-all-start.12 = ((f32[16,1,128]{2,1,0:T(1,128)}), f32[16,1,128]{2,1,0:T(1,128)S(1)}, u32[]{:S(2)}, u32[]{:S(2)}) async-start(f32[16,1,128]{2,1,0:T(1,128)} %get-tuple-element.43), calls=%async_computation.12 | async-start | bytes 16384 | tf_op jit(solution)/shard_map/all_to_all | solution.py:542
  72.3 26.6 %copy-start.2 = (f32[16,32,128]{2,1,0:T(8,128)}, f32[16,32,128]{2,1,0:T(8,128)S(1)}, u32[]{:S(2)}) copy-start(f32[16,32,128]{2,1,0:T(8,128)S(1)} %get-tuple-element.19) | copy-start | bytes 786436 | tf_op jit(solution)/shard_map/cond
  72.3 9.2 %collective-permute-start = (f32[16,32,128]{2,1,0:T(8,128)S(1)}, f32[16,32,128]{2,1,0:T(8,128)S(1)}, u32[]{:S(2)}, u32[]{:S(2)}) collective-permute-start(f32[16,32,128]{2,1,0:T(8,128)S(1)} %bitcast.62), channel_id=1, source_target_pairs={{0,16},{16,32},{32,48},{48,64},{64,80},{80,96},{96,112},{112,128},... | collective-permute-start | bytes 786440 | tf_op jit(solution)/shard_map/cond/branch_0_fun/ppermute | solution.py:592
  76.5 14.5 %collective-permute-start.3 = (f32[1,32,128]{2,1,0:T(8,128)S(1)}, f32[1,32,128]{2,1,0:T(8,128)S(1)}, u32[]{:S(2)}, u32[]{:S(2)}) collective-permute-start(f32[1,32,128]{2,1,0:T(8,128)S(1)} %get-tuple-element.117), channel_id=1, source_target_pairs={{0,1},{1,2},{2,3},{3,4},{4,5},{5,6},{6,7},{7,8},{8,9},{9,10},{10,1... | collective-permute-start | bytes 49160 | tf_op jit(solution)/shard_map/cond/branch_0_fun/ppermute | solution.py:580
  79.6 11.5 %collective-permute-start.1 = (f32[1,32,128]{2,1,0:T(8,128)S(1)}, f32[1,32,128]{2,1,0:T(8,128)S(1)}, u32[]{:S(2)}, u32[]{:S(2)}) collective-permute-start(f32[1,32,128]{2,1,0:T(8,128)S(1)} %get-tuple-element.118), channel_id=1, source_target_pairs={{1,0},{2,1},{3,2},{4,3},{5,4},{6,5},{7,6},{8,7},{9,8},{10,9},{11,1... | collective-permute-start | bytes 49160 | tf_op jit(solution)/shard_map/cond/branch_0_fun/ppermute | solution.py:582
  81.6 9.8 %collective-permute-start.4 = (f32[1,32,128]{2,1,0:T(8,128)S(1)}, f32[1,32,128]{2,1,0:T(8,128)S(1)}, u32[]{:S(2)}, u32[]{:S(2)}) collective-permute-start(f32[1,32,128]{2,1,0:T(8,128)S(1)} %get-tuple-element.119), channel_id=1, source_target_pairs={{0,1},{1,2},{2,3},{3,4},{4,5},{5,6},{6,7},{7,8},{8,9},{9,10},{10,1... | collective-permute-start | bytes 49160 | tf_op jit(solution)/shard_map/cond/branch_0_fun/ppermute | solution.py:580
  89.1 9.0 %collective-permute-start.2 = (f32[1,32,128]{2,1,0:T(8,128)S(1)}, f32[1,32,128]{2,1,0:T(8,128)S(1)}, u32[]{:S(2)}, u32[]{:S(2)}) collective-permute-start(f32[1,32,128]{2,1,0:T(8,128)S(1)} %get-tuple-element.120), channel_id=1, source_target_pairs={{1,0},{2,1},{3,2},{4,3},{5,4},{6,5},{7,6},{8,7},{9,8},{10,9},{11,1... | collective-permute-start | bytes 49160 | tf_op jit(solution)/shard_map/cond/branch_0_fun/ppermute | solution.py:582
  99.0 4.5 collective-permute-start.6
  100.9 10.6 %collective-permute-start.5 = (f32[1,32,128]{2,1,0:T(8,128)S(1)}, f32[1,32,128]{2,1,0:T(8,128)S(1)}, u32[]{:S(2)}, u32[]{:S(2)}) collective-permute-start(f32[1,32,128]{2,1,0:T(8,128)S(1)} %get-tuple-element.116), channel_id=1, source_target_pairs={{1,0},{2,1},{3,2},{4,3},{5,4},{6,5},{7,6},{8,7},{9,8},{10,9},{11,1... | collective-permute-start | bytes 49160 | tf_op jit(solution)/shard_map/cond/branch_0_fun/ppermute | solution.py:582
  134.6 4.7 collective-permute-start.8
  137.3 9.0 %collective-permute-start.7 = (f32[1,32,128]{2,1,0:T(8,128)S(1)}, f32[1,32,128]{2,1,0:T(8,128)S(1)}, u32[]{:S(2)}, u32[]{:S(2)}) collective-permute-start(f32[1,32,128]{2,1,0:T(8,128)S(1)} %get-tuple-element.114), channel_id=1, source_target_pairs={{1,0},{2,1},{3,2},{4,3},{5,4},{6,5},{7,6},{8,7},{9,8},{10,9},{11,1... | collective-permute-start | bytes 49160 | tf_op jit(solution)/shard_map/cond/branch_0_fun/ppermute | solution.py:582
  172.5 4.7 collective-permute-start.10
  175.3 9.0 %collective-permute-start.9 = (f32[1,32,128]{2,1,0:T(8,128)S(1)}, f32[1,32,128]{2,1,0:T(8,128)S(1)}, u32[]{:S(2)}, u32[]{:S(2)}) collective-permute-start(f32[1,32,128]{2,1,0:T(8,128)S(1)} %get-tuple-element.112), channel_id=1, source_target_pairs={{1,0},{2,1},{3,2},{4,3},{5,4},{6,5},{7,6},{8,7},{9,8},{10,9},{11,1... | collective-permute-start | bytes 49160 | tf_op jit(solution)/shard_map/cond/branch_0_fun/ppermute | solution.py:582
  211.5 49.5 %copy-start.3 = (f32[16,32,128]{2,1,0:T(8,128)}, f32[16,32,128]{2,1,0:T(8,128)S(1)}, u32[]{:S(2)}) copy-start(f32[16,32,128]{2,1,0:T(8,128)S(1)} %get-tuple-element.82) | copy-start | bytes 786436 | tf_op jit(solution)/shard_map/cond
  211.5 4.7 collective-permute-start.12
  214.2 9.0 %collective-permute-start.11 = (f32[1,32,128]{2,1,0:T(8,128)S(1)}, f32[1,32,128]{2,1,0:T(8,128)S(1)}, u32[]{:S(2)}, u32[]{:S(2)}) collective-permute-start(f32[1,32,128]{2,1,0:T(8,128)S(1)} %get-tuple-element.110), channel_id=1, source_target_pairs={{1,0},{2,1},{3,2},{4,3},{5,4},{6,5},{7,6},{8,7},{9,8},{10,9},{11,1... | collective-permute-start | bytes 49160 | tf_op jit(solution)/shard_map/cond/branch_0_fun/ppermute | solution.py:582
  248.9 4.7 collective-permute-start.14
  251.7 9.0 %collective-permute-start.13 = (f32[1,32,128]{2,1,0:T(8,128)S(1)}, f32[1,32,128]{2,1,0:T(8,128)S(1)}, u32[]{:S(2)}, u32[]{:S(2)}) collective-permute-start(f32[1,32,128]{2,1,0:T(8,128)S(1)} %get-tuple-element.108), channel_id=1, source_target_pairs={{1,0},{2,1},{3,2},{4,3},{5,4},{6,5},{7,6},{8,7},{9,8},{10,9},{11,1... | collective-permute-start | bytes 49160 | tf_op jit(solution)/shard_map/cond/branch_0_fun/ppermute | solution.py:582
  287.7 4.7 collective-permute-start.16
  290.5 9.0 %collective-permute-start.15 = (f32[1,32,128]{2,1,0:T(8,128)S(1)}, f32[1,32,128]{2,1,0:T(8,128)S(1)}, u32[]{:S(2)}, u32[]{:S(2)}) collective-permute-start(f32[1,32,128]{2,1,0:T(8,128)S(1)} %get-tuple-element.106), channel_id=1, source_target_pairs={{1,0},{2,1},{3,2},{4,3},{5,4},{6,5},{7,6},{8,7},{9,8},{10,9},{11,1... | collective-permute-start | bytes 49160 | tf_op jit(solution)/shard_map/cond/branch_0_fun/ppermute | solution.py:582
  325.1 4.7 collective-permute-start.18
  327.9 9.0 %collective-permute-start.17 = (f32[1,32,128]{2,1,0:T(8,128)S(1)}, f32[1,32,128]{2,1,0:T(8,128)S(1)}, u32[]{:S(2)}, u32[]{:S(2)}) collective-permute-start(f32[1,32,128]{2,1,0:T(8,128)S(1)} %get-tuple-element.104), channel_id=1, source_target_pairs={{1,0},{2,1},{3,2},{4,3},{5,4},{6,5},{7,6},{8,7},{9,8},{10,9},{11,1... | collective-permute-start | bytes 49160 | tf_op jit(solution)/shard_map/cond/branch_0_fun/ppermute | solution.py:582
  338.4 4.3 collective-permute-start.20
  340.4 9.7 %collective-permute-start.19 = (f32[1,32,128]{2,1,0:T(8,128)S(1)}, f32[1,32,128]{2,1,0:T(8,128)S(1)}, u32[]{:S(2)}, u32[]{:S(2)}) collective-permute-start(f32[1,32,128]{2,1,0:T(8,128)S(1)} %get-tuple-element.102), channel_id=1, source_target_pairs={{1,0},{2,1},{3,2},{4,3},{5,4},{6,5},{7,6},{8,7},{9,8},{10,9},{11,1... | collective-permute-start | bytes 49160 | tf_op jit(solution)/shard_map/cond/branch_0_fun/ppermute | solution.py:582
  373.3 4.7 collective-permute-start.22
  376.0 9.0 %collective-permute-start.21 = (f32[1,32,128]{2,1,0:T(8,128)S(1)}, f32[1,32,128]{2,1,0:T(8,128)S(1)}, u32[]{:S(2)}, u32[]{:S(2)}) collective-permute-start(f32[1,32,128]{2,1,0:T(8,128)S(1)} %get-tuple-element.100), channel_id=1, source_target_pairs={{1,0},{2,1},{3,2},{4,3},{5,4},{6,5},{7,6},{8,7},{9,8},{10,9},{11,1... | collective-permute-start | bytes 49160 | tf_op jit(solution)/shard_map/cond/branch_0_fun/ppermute | solution.py:582
  411.1 4.7 collective-permute-start.24
  413.9 9.0 %collective-permute-start.23 = (f32[1,32,128]{2,1,0:T(8,128)S(1)}, f32[1,32,128]{2,1,0:T(8,128)S(1)}, u32[]{:S(2)}, u32[]{:S(2)}) collective-permute-start(f32[1,32,128]{2,1,0:T(8,128)S(1)} %get-tuple-element.98), channel_id=1, source_target_pairs={{1,0},{2,1},{3,2},{4,3},{5,4},{6,5},{7,6},{8,7},{9,8},{10,9},{11,1... | collective-permute-start | bytes 49160 | tf_op jit(solution)/shard_map/cond/branch_0_fun/ppermute | solution.py:582
  449.9 4.7 collective-permute-start.26
  452.6 9.0 %collective-permute-start.25 = (f32[1,32,128]{2,1,0:T(8,128)S(1)}, f32[1,32,128]{2,1,0:T(8,128)S(1)}, u32[]{:S(2)}, u32[]{:S(2)}) collective-permute-start(f32[1,32,128]{2,1,0:T(8,128)S(1)} %get-tuple-element.96), channel_id=1, source_target_pairs={{1,0},{2,1},{3,2},{4,3},{5,4},{6,5},{7,6},{8,7},{9,8},{10,9},{11,1... | collective-permute-start | bytes 49160 | tf_op jit(solution)/shard_map/cond/branch_0_fun/ppermute | solution.py:582
  462.9 62.4 %copy-start.4 = (f32[16,32,128]{2,1,0:T(8,128)}, f32[16,32,128]{2,1,0:T(8,128)S(1)}, u32[]{:S(2)}) copy-start(f32[16,32,128]{2,1,0:T(8,128)S(1)} %get-tuple-element.73) | copy-start | bytes 786436 | tf_op jit(solution)/shard_map/cond
  487.1 4.7 collective-permute-start.28
  489.9 9.0 %collective-permute-start.27 = (f32[1,32,128]{2,1,0:T(8,128)S(1)}, f32[1,32,128]{2,1,0:T(8,128)S(1)}, u32[]{:S(2)}, u32[]{:S(2)}) collective-permute-start(f32[1,32,128]{2,1,0:T(8,128)S(1)} %get-tuple-element.94), channel_id=1, source_target_pairs={{1,0},{2,1},{3,2},{4,3},{5,4},{6,5},{7,6},{8,7},{9,8},{10,9},{11,1... | collective-permute-start | bytes 49160 | tf_op jit(solution)/shard_map/cond/branch_0_fun/ppermute | solution.py:582
  526.4 4.7 collective-permute-start.30
  529.2 9.0 %collective-permute-start.29 = (f32[1,32,128]{2,1,0:T(8,128)S(1)}, f32[1,32,128]{2,1,0:T(8,128)S(1)}, u32[]{:S(2)}, u32[]{:S(2)}) collective-permute-start(f32[1,32,128]{2,1,0:T(8,128)S(1)} %get-tuple-element.92), channel_id=1, source_target_pairs={{1,0},{2,1},{3,2},{4,3},{5,4},{6,5},{7,6},{8,7},{9,8},{10,9},{11,1... | collective-permute-start | bytes 49160 | tf_op jit(solution)/shard_map/cond/branch_0_fun/ppermute | solution.py:582

commit v2 on v1

--- a/solution.py
+++ b/solution.py
@@ -301,66 +301,84 @@
     return lambda e: [ref[(*lead, e - shift, k)] for k in range(4)]
 
 
-def conductivities(a, lo, hi):
+def conductivities(a, low, high):
     depth = a.shape[0]
 
     def conduct(e):
-        ref, z = (lo, e) if e < RIM else (a, e - RIM) if e < RIM + depth else (hi, e - RIM - depth)
-        return [ref[z, q] for q in range(4)]
+        if e < RIM:
+            return [low(e, q) for q in range(4)]
+        if e < RIM + depth:
+            return [a[e - RIM, q] for q in range(4)]
+        return [high(e - RIM - depth, q) for q in range(4)]
 
     return conduct
 
 
-def inside(lo, hi, low, high):
+def inside(low, high, below, above):
     one = jnp.ones((SUB, LANES), jnp.float32)
     return {
-        low: jnp.where(lo[RIM - 1, 0] > 0, one, 0.0),
-        high: jnp.where(hi[0, 0] > 0, one, 0.0),
+        below: jnp.where(low(RIM - 1, 0) > 0, one, 0.0),
+        above: jnp.where(high(0, 0) > 0, one, 0.0),
     }
 
 
-def stage_kernel(c, f, a, cs, fs, cond, tail, head):
+def is_odd():
+    return lax.axis_index("space") % 2 == 1
+
+
+def swap(far, near, z, q, odd, tail, head):
+    far[z, q] = jnp.where(odd, tail, head)
+    near[z, q] = jnp.where(odd, head, tail)
+
+
+def sides(far, near, odd):
+    low = lambda z, q: jnp.where(odd, near[z, q], far[z, q])
+    high = lambda z, q: jnp.where(odd, far[z, q], near[z, q])
+    return low, high
+
+
+def stage_kernel(c, f, a, cs, fs, cond, far, near):
     depth = c.shape[0]
     for z in range(depth):
         for q in range(4):
             cs[z, q] = load_rows(c, z, q)
             fs[z, q] = load_rows(f, z, q)
-            v = load_rows(a, z, q)
-            cond[z, q] = v
-            if z < RIM:
-                head[z, q] = v
-            if z >= depth - RIM:
-                tail[z - depth + RIM, q] = v
-
-
-def open_kernel(c, fix, f, a, x, res, tail, head, *fields):
+            cond[z, q] = load_rows(a, z, q)
+    odd = is_odd()
+    for z in range(RIM):
+        for q in range(4):
+            swap(far, near, z, q, odd, cond[z + depth - RIM, q], cond[z, q])
+
+
+def open_kernel(c, fix, f, a, x, res, far, near, *fields):
     depth = c.shape[0]
     fill_weights(planes(a), fields, 0, depth - 1)
     for z in range(depth):
         for q in range(4):
             v = c[z, q] + load_rows(fix, z, q)
             x[z, q] = v
-            if z == 0:
-                head[RIM, q] = v
-            if z == depth - 1:
-                tail[RIM, q] = v
 
     def emit(z, v, image):
         for q in range(4):
             r = SOURCE_WEIGHT * f[z, q] - (1.0 / SIGMA) * image[q]
             res[z, q] = r
-            if z < RIM:
-                head[z, q] = r
-            if z >= depth - RIM:
-                tail[z - depth + RIM, q] = r
 
     across(planes(x), fields, 0, depth - 1, emit, residual=True)
-
-
-def basis_kernel(x, res, lo, hi, a, alo, ahi, basis, sums, kept, ring, done, *fields):
+    odd = is_odd()
+    for z in range(RIM):
+        for q in range(4):
+            swap(far, near, z, q, odd, res[z + depth - RIM, q], res[z, q])
+    for q in range(4):
+        swap(far, near, RIM, q, odd, x[depth - 1, q], x[0, q])
+
+
+def basis_kernel(x, res, far, near, a, afar, anear, basis, sums, kept, ring, done, *fields):
     depth = x.shape[0]
     span = depth + 2 * RIM
     low, high = RIM - 1, RIM + depth
+    odd = is_odd()
+    lo, hi = sides(far, near, odd)
+    alo, ahi = sides(afar, anear, odd)
     mask = inside(alo, ahi, low, high)
     fill_weights(conductivities(a, alo, ahi), fields, 0, span - 1)
     wz = fields[0]
@@ -401,16 +419,16 @@
 
     for e in range(span):
         if e < RIM:
-            new = [lo[e, q] for q in range(4)]
+            new = [lo(e, q) for q in range(4)]
         elif e < RIM + depth:
             new = [res[e - RIM, q] for q in range(4)]
         else:
-            new = [hi[e - RIM - depth, q] for q in range(4)]
+            new = [hi(e - RIM - depth, q) for q in range(4)]
         for face, inner, outer in ((low, 0, lo), (high - 1, depth - 1, hi)):
             if e in (face, face + 1):
                 own = (e == face) == (face != low)
                 for q in range(4):
-                    flux = (1.0 / SIGMA) * wz[face, q] * (x[inner, q] - outer[RIM, q])
+                    flux = (1.0 / SIGMA) * wz[face, q] * (x[inner, q] - outer(RIM, q))
                     new[q] = new[q] - flux if own else new[q] + flux
         store(0, e, new, None)
     copy(0).start()
@@ -432,12 +450,13 @@
         copy(k).wait()
 
 
-def states_kernel(gathered, basis, x, a, alo, ahi, out, flag, kept, ring, final, done, *fields):
+def states_kernel(gathered, basis, x, a, afar, anear, out, flag, kept, ring, final, done, *fields):
     depth = x.shape[0]
     first, count = RIM - KEEP, depth + 2 * KEEP
     copies = [pltpu.make_async_copy(basis.at[k], kept.at[k], done.at[k]) for k in range(ITERS + 1)]
     for copy in copies:
         copy.start()
+    alo, ahi = sides(afar, anear, is_odd())
     mask = inside(alo, ahi, KEEP - 1, KEEP + depth)
     conduct = conductivities(a, alo, ahi)
     fill_weights(lambda e: conduct(e + first), fields, 0, count - 1)
@@ -515,20 +534,20 @@
     depth = forcing.shape[0]
     span, count = depth + 2 * RIM, depth + 2 * KEEP
     tile = (4, SUB, LANES)
-    up = [(i, i + 1) for i in range(slabs - 1)]
-    down = [(i + 1, i) for i in range(slabs - 1)]
+    far_pairs = [p for i in range(1, slabs - 1, 2) for p in ((i, i + 1), (i + 1, i))]
+    near_pairs = [p for i in range(0, slabs - 1, 2) for p in ((i, i + 1), (i + 1, i))]
     later = [(i, i + 1) for i in range(times - 1)]
 
     own, sent, rim = (depth, *tile), (RIM + 1, *tile), (RIM, *tile)
     fix = lax.ppermute(corrections[0], "tm", later)
-    point, source, cond, tail, head = call(
+    point, source, cond, far, near = call(
         stage_kernel, [own, own, own, rim, rim], [], inputs=3, weights=False
     )(own)(c_points[0], forcing, conductivity)
-    alo = lax.ppermute(tail, "space", up)
-    ahi = lax.ppermute(head, "space", down)
-    x, res, tail, head = call(open_kernel, [own, own, sent, sent], [], inputs=4)(own)(point, fix, source, cond)
-    lo = lax.ppermute(tail, "space", up)
-    hi = lax.ppermute(head, "space", down)
+    afar = lax.ppermute(far, "space", far_pairs)
+    anear = lax.ppermute(near, "space", near_pairs)
+    x, res, far, near = call(open_kernel, [own, own, sent, sent], [], inputs=4)(own)(point, fix, source, cond)
+    far = lax.ppermute(far, "space", far_pairs)
+    near = lax.ppermute(near, "space", near_pairs)
     field, part = (span, *tile), (count, *tile)
     basis, sums = call(
         basis_kernel,
@@ -537,7 +556,7 @@
         sent=0,
         inputs=7,
         copies=ITERS + 1,
-    )(field)(x, res, lo, hi, cond, alo, ahi)
+    )(field)(x, res, far, near, cond, afar, anear)
     basis = pltpu.with_memory_space_constraint(basis, pltpu.HBM)
     sums = lax.all_to_all(sums, "space", 0, 0, tiled=True)
     return call(
@@ -547,7 +566,7 @@
         read=1,
         inputs=6,
         copies=ITERS + 1,
-    )(part)(sums, basis, x, cond, alo, ahi)
+    )(part)(sums, basis, x, cond, afar, anear)
 
 
 def copy_for_each(array, axis):
@@ -664,6 +683,7 @@
 def body(c_points, corrections, conductivity, forcing):
     args = (c_points, corrections, conductivity, forcing)
     out, good = fast(*args)
+    args, good = lax.optimization_barrier((args, good))
     return lax.cond(good[0] > 0, lambda: out, lambda: plain(*args))
 
 

time: 569 us -> 565 us (level)
  blocking collectives: 221 us -> 239 us
  starting transfers between devices: 115 us -> 104 us
  waiting for transfers between devices: 122 us -> 113 us
    all_to_all x0 -> x1, blocking collectives: none -> 18 us  [fast(): sums = lax.all_to_all(sums, 'space', 0, 0, tiled=True)]
    all_to_all x1 -> x0, waiting for transfers between devices: 9.34 us -> none  [fast(): sums = lax.all_to_all(sums, 'space', 0, 0, tiled=True)]
    all_to_all x1 -> x0, starting transfers between devices: 6.85 us -> none  [fast(): sums = lax.all_to_all(sums, 'space', 0, 0, tiled=True)]
  transfers between devices with their start and end apart: 37 -> 36, of which waited for: 18 -> 16; matrix products, arithmetic and copies ran while one was open for 0% -> 0% of each run, Pallas kernels for 0% -> 0%
where the time goes in v2:
time: 565 us; the launch traced here: 563 us
  blocking collectives  239 us (42%)
  waiting for transfers between devices  113 us (20%)
  starting transfers between devices  104 us (18%)
  other arithmetic  42.9 us (8%)
  loops' own time  42.6 us (8%)
  Pallas kernels  12.4 us (2%)
  local copies, waits for them, and re-layouts  7.75 us (1%)
    all_to_all x12, blocking collectives, copy_for_each(): lax.all_to_all(jnp.broadcast_to(array[None], (devices, *array.shape)), ax...  221 us
    ppermute x15, waiting for transfers between devices, extended(): lax.ppermute(head, axis, [((i + 1) % count, i) for i in range(ends)])  99.3 us
    ppermute x15, starting transfers between devices, extended(): lax.ppermute(tail, axis, [(i, (i + 1) % count) for i in range(ends)])  44.8 us
    another operation x1, loops' own time, body(): return lax.cond(good[0] > 0, lambda: out, lambda: plain(*args))  42.6 us
    ppermute x15, starting transfers between devices, extended(): lax.ppermute(head, axis, [((i + 1) % count, i) for i in range(ends)])  29.9 us
    all_to_all x1, blocking collectives, fast(): sums = lax.all_to_all(sums, 'space', 0, 0, tiled=True)  18 us
    concatenate x12, other arithmetic, packed_total(): subtotal = over_copies(jnp.concatenate([a.ravel() for a in arrays]), axis)  15.6 us
    reduce_sum x12, other arithmetic, pair_sums(): jnp.sum(residual * residual)  15.1 us
  transfers between devices with their start and end apart: 36, of which 16 were waited for; matrix products, arithmetic and copies ran while one was open for 0% of the time, Pallas kernels for 0%

profile of v2, /device:TPU:1, one launch (start us, length us, event | category | flops | bytes accessed | tf_op | source)
XLA Modules:
  0.0 562.5 jit_solution(12713600416054017042)
XLA Ops:
  0.0 4.8 collective-permute-start.31
  8.9 13.0 %collective-permute-start.32 = (f32[13,4,8,128]{3,2,1,0:T(8,128)S(1)}, f32[13,4,8,128]{3,2,1,0:T(8,128)S(1)}, u32[]{:S(2)}, u32[]{:S(2)}) collective-permute-start(f32[13,4,8,128]{3,2,1,0:T(8,128)S(1)} %get-tuple-element.44), channel_id=1, source_target_pairs={{1,2},{2,1},{3,4},{4,3},{5,6},{6,5},{7,8},{8,7},{9,10},{10,9},{11,... | collective-permute-start | bytes 638984 | tf_op jit(solution)/shard_map/ppermute | solution.py:549
  27.6 11.3 %collective-permute-done.34.afar = f32[12,4,8,128]{3,2,1,0:T(8,128)S(1)} collective-permute-done((f32[12,4,8,128]{3,2,1,0:T(8,128)S(1)}, f32[12,4,8,128]{3,2,1,0:T(8,128)S(1)}, u32[]{:S(2)}, u32[]{:S(2)}) %collective-permute-start.34) | collective-permute-done | bytes 196640 | tf_op jit(solution)/shard_map/ppermute | solution.py:546
  38.9 5.2 shard_map.50
  44.1 18.0 %all_to_all.77.gathered = f32[16,1,128]{2,1,0:T(1,128)S(1)} all-to-all(f32[16,1,128]{2,1,0:T(1,128)S(1)} %get-tuple-element.48), channel_id=1, replica_groups=mesh['tm'=32,'space'=16] {'space'}, dimensions={0} | all-to-all | bytes 16384 | tf_op jit(solution)/shard_map/all_to_all | solution.py:561
  62.2 5.7 %shard_map.51 = (f32[1,2,16,32,128]{4,3,2,1,0:T(8,128)}, s32[1]{0:T(128)}) custom-call(f32[16,1,128]{2,1,0:T(1,128)S(1)} %all_to_all.77.gathered, f32[7,26,4,8,128]{4,3,2,1,0:T(8,128)} %get-tuple-element.49.basis, f32[16,4,8,128]{3,2,1,0:T(8,128)S(1)} %get-tuple-element.42.x, f32[16,4,8,128]{3,2,1,0:T(8,128)S(1)} %get-tuple-element.41.a, ...), custom_call_target="tpu_custom_call" | custom-call | tf_op jit(solution)/shard_map/pallas_call | solution.py:562
  68.4 494.1 %conditional.1 = (f32[1,2,16,32,128]{4,3,2,1,0:T(8,128)}) conditional(s32[]{:T(128)} %bitcast.55, (f32[1,16,32,128]{3,2,1,0:T(8,128)S(1)}, f32[1,16,32,128]{3,2,1,0:T(8,128)S(1)}, f32[16,32,128]{2,1,0:T(8,128)S(1)}, f32[16,32,128]{2,1,0:T(8,128)S(1)}) %tuple.77, f32[1,2,16,32,128]{4,3,2,1,0:T(8,128)} %get-tuple-element.56), branch_computations={%region_0.37_spmd, %region_37.38_spmd} | conditional | flops 52701000 | bytes 76249768 | solution.py:687
  68.4 5.9 %collective-permute-start = (f32[16,32,128]{2,1,0:T(8,128)S(1)}, f32[16,32,128]{2,1,0:T(8,128)S(1)}, u32[]{:S(2)}, u32[]{:S(2)}) collective-permute-start(f32[16,32,128]{2,1,0:T(8,128)S(1)} %bitcast.62), channel_id=1, source_target_pairs={{0,16},{16,32},{32,48},{48,64},{64,80},{80,96},{96,112},{112,128},... | collective-permute-start | bytes 786440 | tf_op jit(solution)/shard_map/cond/branch_0_fun/ppermute | solution.py:611
  74.3 3.0 collective-permute-start.3
  79.4 7.5 %collective-permute-start.4 = (f32[1,32,128]{2,1,0:T(8,128)S(1)}, f32[1,32,128]{2,1,0:T(8,128)S(1)}, u32[]{:S(2)}, u32[]{:S(2)}) collective-permute-start(f32[1,32,128]{2,1,0:T(8,128)S(1)} %get-tuple-element.129), channel_id=1, source_target_pairs={{0,1},{1,2},{2,3},{3,4},{4,5},{5,6},{6,7},{7,8},{8,9},{9,10},{10,1... | collective-permute-start | bytes 49160 | tf_op jit(solution)/shard_map/cond/branch_0_fun/ppermute | solution.py:599
  89.1 6.7 %collective-permute-done.2 = f32[1,32,128]{2,1,0:T(8,128)S(1)} collective-permute-done((f32[1,32,128]{2,1,0:T(8,128)S(1)}, f32[1,32,128]{2,1,0:T(8,128)S(1)}, u32[]{:S(2)}, u32[]{:S(2)}) %collective-permute-start.2) | collective-permute-done | bytes 16416 | tf_op jit(solution)/shard_map/cond/branch_0_fun/ppermute | solution.py:601
  98.7 2.6 collective-permute-start.5
  101.3 8.0 %collective-permute-done.5 = f32[1,32,128]{2,1,0:T(8,128)S(1)} collective-permute-done((f32[1,32,128]{2,1,0:T(8,128)S(1)}, f32[1,32,128]{2,1,0:T(8,128)S(1)}, u32[]{:S(2)}, u32[]{:S(2)}) %collective-permute-start.5) | collective-permute-done | bytes 16416 | tf_op jit(solution)/shard_map/cond/branch_0_fun/ppermute | solution.py:601
  111.9 18.6 %all_to_all.65 = f32[16,1,2]{2,1,0:T(1,128)S(1)} all-to-all(f32[16,1,2]{2,1,0:T(1,128)S(1)} %broadcast_in_dim.0), channel_id=1, replica_groups=mesh['tm'=32,'space'=16] {'space'}, dimensions={0} | all-to-all | bytes 256 | tf_op jit(solution)/shard_map/cond/branch_0_fun/all_to_all | solution.py:574
  132.4 2.8 collective-permute-start.8
  137.1 7.0 %collective-permute-done.7 = f32[1,32,128]{2,1,0:T(8,128)S(1)} collective-permute-done((f32[1,32,128]{2,1,0:T(8,128)S(1)}, f32[1,32,128]{2,1,0:T(8,128)S(1)}, u32[]{:S(2)}, u32[]{:S(2)}) %collective-permute-start.7) | collective-permute-done | bytes 16416 | tf_op jit(solution)/shard_map/cond/branch_0_fun/ppermute | solution.py:601
  146.6 18.4 %all_to_all.66 = f32[16,1,2]{2,1,0:T(1,128)S(1)} all-to-all(f32[16,1,2]{2,1,0:T(1,128)S(1)} %broadcast_in_dim.1), channel_id=1, replica_groups=mesh['tm'=32,'space'=16] {'space'}, dimensions={0} | all-to-all | bytes 256 | tf_op jit(solution)/shard_map/cond/branch_0_fun/all_to_all | solution.py:574
  170.3 2.8 collective-permute-start.10
  175.0 7.0 %collective-permute-done.9 = f32[1,32,128]{2,1,0:T(8,128)S(1)} collective-permute-done((f32[1,32,128]{2,1,0:T(8,128)S(1)}, f32[1,32,128]{2,1,0:T(8,128)S(1)}, u32[]{:S(2)}, u32[]{:S(2)}) %collective-permute-start.9) | collective-permute-done | bytes 16416 | tf_op jit(solution)/shard_map/cond/branch_0_fun/ppermute | solution.py:601
  185.3 18.4 %all_to_all.67 = f32[16,1,2]{2,1,0:T(1,128)S(1)} all-to-all(f32[16,1,2]{2,1,0:T(1,128)S(1)} %broadcast_in_dim.2), channel_id=1, replica_groups=mesh['tm'=32,'space'=16] {'space'}, dimensions={0} | all-to-all | bytes 256 | tf_op jit(solution)/shard_map/cond/branch_0_fun/all_to_all | solution.py:574
  209.3 2.8 collective-permute-start.12
  214.0 7.0 %collective-permute-done.11 = f32[1,32,128]{2,1,0:T(8,128)S(1)} collective-permute-done((f32[1,32,128]{2,1,0:T(8,128)S(1)}, f32[1,32,128]{2,1,0:T(8,128)S(1)}, u32[]{:S(2)}, u32[]{:S(2)}) %collective-permute-start.11) | collective-permute-done | bytes 16416 | tf_op jit(solution)/shard_map/cond/branch_0_fun/ppermute | solution.py:601
  223.7 18.4 %all_to_all.68 = f32[16,1,2]{2,1,0:T(1,128)S(1)} all-to-all(f32[16,1,2]{2,1,0:T(1,128)S(1)} %broadcast_in_dim.3), channel_id=1, replica_groups=mesh['tm'=32,'space'=16] {'space'}, dimensions={0} | all-to-all | bytes 256 | tf_op jit(solution)/shard_map/cond/branch_0_fun/all_to_all | solution.py:574
  246.7 2.8 collective-permute-start.14
  251.4 7.0 %collective-permute-done.13 = f32[1,32,128]{2,1,0:T(8,128)S(1)} collective-permute-done((f32[1,32,128]{2,1,0:T(8,128)S(1)}, f32[1,32,128]{2,1,0:T(8,128)S(1)}, u32[]{:S(2)}, u32[]{:S(2)}) %collective-permute-start.13) | collective-permute-done | bytes 16416 | tf_op jit(solution)/shard_map/cond/branch_0_fun/ppermute | solution.py:601
  261.7 18.4 %all_to_all.69 = f32[16,1,2]{2,1,0:T(1,128)S(1)} all-to-all(f32[16,1,2]{2,1,0:T(1,128)S(1)} %broadcast_in_dim.4), channel_id=1, replica_groups=mesh['tm'=32,'space'=16] {'space'}, dimensions={0} | all-to-all | bytes 256 | tf_op jit(solution)/shard_map/cond/branch_0_fun/all_to_all | solution.py:574
  285.5 2.8 collective-permute-start.16
  290.2 7.0 %collective-permute-done.15 = f32[1,32,128]{2,1,0:T(8,128)S(1)} collective-permute-done((f32[1,32,128]{2,1,0:T(8,128)S(1)}, f32[1,32,128]{2,1,0:T(8,128)S(1)}, u32[]{:S(2)}, u32[]{:S(2)}) %collective-permute-start.15) | collective-permute-done | bytes 16416 | tf_op jit(solution)/shard_map/cond/branch_0_fun/ppermute | solution.py:601
  299.9 18.4 %all_to_all.70 = f32[16,1,2]{2,1,0:T(1,128)S(1)} all-to-all(f32[16,1,2]{2,1,0:T(1,128)S(1)} %broadcast_in_dim.5), channel_id=1, replica_groups=mesh['tm'=32,'space'=16] {'space'}, dimensions={0} | all-to-all | bytes 256 | tf_op jit(solution)/shard_map/cond/branch_0_fun/all_to_all | solution.py:574
  322.9 2.8 collective-permute-start.18
  327.6 7.0 %collective-permute-done.17 = f32[1,32,128]{2,1,0:T(8,128)S(1)} collective-permute-done((f32[1,32,128]{2,1,0:T(8,128)S(1)}, f32[1,32,128]{2,1,0:T(8,128)S(1)}, u32[]{:S(2)}, u32[]{:S(2)}) %collective-permute-start.17) | collective-permute-done | bytes 16416 | tf_op jit(solution)/shard_map/cond/branch_0_fun/ppermute | solution.py:601
  340.6 7.3 %collective-permute-done.19 = f32[1,32,128]{2,1,0:T(8,128)S(1)} collective-permute-done((f32[1,32,128]{2,1,0:T(8,128)S(1)}, f32[1,32,128]{2,1,0:T(8,128)S(1)}, u32[]{:S(2)}, u32[]{:S(2)}) %collective-permute-start.19) | collective-permute-done | bytes 16416 | tf_op jit(solution)/shard_map/cond/branch_0_fun/ppermute | solution.py:601
  350.4 18.6 %all_to_all.71 = f32[16,1,2]{2,1,0:T(1,128)S(1)} all-to-all(f32[16,1,2]{2,1,0:T(1,128)S(1)} %broadcast_in_dim.6), channel_id=1, replica_groups=mesh['tm'=32,'space'=16] {'space'}, dimensions={0} | all-to-all | bytes 256 | tf_op jit(solution)/shard_map/cond/branch_0_fun/all_to_all | solution.py:574
  371.1 2.8 collective-permute-start.22
  375.8 7.0 %collective-permute-done.21 = f32[1,32,128]{2,1,0:T(8,128)S(1)} collective-permute-done((f32[1,32,128]{2,1,0:T(8,128)S(1)}, f32[1,32,128]{2,1,0:T(8,128)S(1)}, u32[]{:S(2)}, u32[]{:S(2)}) %collective-permute-start.21) | collective-permute-done | bytes 16416 | tf_op jit(solution)/shard_map/cond/branch_0_fun/ppermute | solution.py:601
  385.4 18.4 %all_to_all.72 = f32[16,1,2]{2,1,0:T(1,128)S(1)} all-to-all(f32[16,1,2]{2,1,0:T(1,128)S(1)} %broadcast_in_dim.7), channel_id=1, replica_groups=mesh['tm'=32,'space'=16] {'space'}, dimensions={0} | all-to-all | bytes 256 | tf_op jit(solution)/shard_map/cond/branch_0_fun/all_to_all | solution.py:574
  408.9 2.8 collective-permute-start.24
  413.6 7.0 %collective-permute-done.23 = f32[1,32,128]{2,1,0:T(8,128)S(1)} collective-permute-done((f32[1,32,128]{2,1,0:T(8,128)S(1)}, f32[1,32,128]{2,1,0:T(8,128)S(1)}, u32[]{:S(2)}, u32[]{:S(2)}) %collective-permute-start.23) | collective-permute-done | bytes 16416 | tf_op jit(solution)/shard_map/cond/branch_0_fun/ppermute | solution.py:601
  423.9 18.4 %all_to_all.73 = f32[16,1,2]{2,1,0:T(1,128)S(1)} all-to-all(f32[16,1,2]{2,1,0:T(1,128)S(1)} %broadcast_in_dim.8), channel_id=1, replica_groups=mesh['tm'=32,'space'=16] {'space'}, dimensions={0} | all-to-all | bytes 256 | tf_op jit(solution)/shard_map/cond/branch_0_fun/all_to_all | solution.py:574
  447.7 2.8 collective-permute-start.26
  452.4 7.0 %collective-permute-done.25 = f32[1,32,128]{2,1,0:T(8,128)S(1)} collective-permute-done((f32[1,32,128]{2,1,0:T(8,128)S(1)}, f32[1,32,128]{2,1,0:T(8,128)S(1)}, u32[]{:S(2)}, u32[]{:S(2)}) %collective-permute-start.25) | collective-permute-done | bytes 16416 | tf_op jit(solution)/shard_map/cond/branch_0_fun/ppermute | solution.py:601
  461.9 18.5 %all_to_all.74 = f32[16,1,2]{2,1,0:T(1,128)S(1)} all-to-all(f32[16,1,2]{2,1,0:T(1,128)S(1)} %broadcast_in_dim.9), channel_id=1, replica_groups=mesh['tm'=32,'space'=16] {'space'}, dimensions={0} | all-to-all | bytes 256 | tf_op jit(solution)/shard_map/cond/branch_0_fun/all_to_all | solution.py:574
  484.9 2.8 collective-permute-start.28
  489.6 7.0 %collective-permute-done.27 = f32[1,32,128]{2,1,0:T(8,128)S(1)} collective-permute-done((f32[1,32,128]{2,1,0:T(8,128)S(1)}, f32[1,32,128]{2,1,0:T(8,128)S(1)}, u32[]{:S(2)}, u32[]{:S(2)}) %collective-permute-start.27) | collective-permute-done | bytes 16416 | tf_op jit(solution)/shard_map/cond/branch_0_fun/ppermute | solution.py:601
  500.1 18.4 %all_to_all.75 = f32[16,1,2]{2,1,0:T(1,128)S(1)} all-to-all(f32[16,1,2]{2,1,0:T(1,128)S(1)} %broadcast_in_dim.10), channel_id=1, replica_groups=mesh['tm'=32,'space'=16] {'space'}, dimensions={0} | all-to-all | bytes 256 | tf_op jit(solution)/shard_map/cond/branch_0_fun/all_to_all | solution.py:574
  524.2 2.8 collective-permute-start.30
  528.9 7.0 %collective-permute-done.29 = f32[1,32,128]{2,1,0:T(8,128)S(1)} collective-permute-done((f32[1,32,128]{2,1,0:T(8,128)S(1)}, f32[1,32,128]{2,1,0:T(8,128)S(1)}, u32[]{:S(2)}, u32[]{:S(2)}) %collective-permute-start.29) | collective-permute-done | bytes 16416 | tf_op jit(solution)/shard_map/cond/branch_0_fun/ppermute | solution.py:601
  538.5 18.4 %all_to_all.76 = f32[16,1,2]{2,1,0:T(1,128)S(1)} all-to-all(f32[16,1,2]{2,1,0:T(1,128)S(1)} %broadcast_in_dim.11), channel_id=1, replica_groups=mesh['tm'=32,'space'=16] {'space'}, dimensions={0} | all-to-all | bytes 256 | tf_op jit(solution)/shard_map/cond/branch_0_fun/all_to_all | solution.py:574
  (162 shorter events, 91.7 us)
Async XLA Ops:
  0.0 8.4 %collective-permute-start.31 = (f32[16,32,128]{2,1,0:T(8,128)}, f32[16,32,128]{2,1,0:T(8,128)S(1)}, u32[]{:S(2)}, u32[]{:S(2)}) collective-permute-start(f32[16,32,128]{2,1,0:T(8,128)} %bitcast.61), channel_id=1, source_target_pairs={{0,16},{16,32},{32,48},{48,64},{64,80},{80,96},{96,112},{112,128},... | collective-permute-start | bytes 786440 | tf_op jit(solution)/shard_map/ppermute | solution.py:542
  8.8 59.6 %copy-start = (f32[16,32,128]{2,1,0:T(8,128)S(1)}, f32[16,32,128]{2,1,0:T(8,128)}, u32[]{:S(2)}) copy-start(f32[16,32,128]{2,1,0:T(8,128)} %a.1) | copy-start | bytes 786436
  8.8 59.6 %copy-start.1 = (f32[16,32,128]{2,1,0:T(8,128)S(1)}, f32[16,32,128]{2,1,0:T(8,128)}, u32[]{:S(2)}) copy-start(f32[16,32,128]{2,1,0:T(8,128)} %f.1) | copy-start | bytes 786436
  8.8 59.6 %copy-start.5 = (f32[1,16,32,128]{3,2,1,0:T(8,128)S(1)}, f32[1,16,32,128]{3,2,1,0:T(8,128)}, u32[]{:S(2)}) copy-start(f32[1,16,32,128]{3,2,1,0:T(8,128)} %param.6) | copy-start | bytes 786436
  8.9 59.6 %copy-start.6 = (f32[1,16,32,128]{3,2,1,0:T(8,128)S(1)}, f32[1,16,32,128]{3,2,1,0:T(8,128)}, u32[]{:S(2)}) copy-start(f32[1,16,32,128]{3,2,1,0:T(8,128)} %param.7) | copy-start | bytes 786436
  8.9 30.0 %collective-permute-start.32 = (f32[13,4,8,128]{3,2,1,0:T(8,128)S(1)}, f32[13,4,8,128]{3,2,1,0:T(8,128)S(1)}, u32[]{:S(2)}, u32[]{:S(2)}) collective-permute-start(f32[13,4,8,128]{3,2,1,0:T(8,128)S(1)} %get-tuple-element.44), channel_id=1, source_target_pairs={{1,2},{2,1},{3,4},{4,3},{5,6},{6,5},{7,8},{8,7},{9,10},{10,9},{11,... | collective-permute-start | bytes 638984 | tf_op jit(solution)/shard_map/ppermute | solution.py:549
  21.8 17.1 %collective-permute-start.33 = (f32[13,4,8,128]{3,2,1,0:T(8,128)S(1)}, f32[13,4,8,128]{3,2,1,0:T(8,128)S(1)}, u32[]{:S(2)}, u32[]{:S(2)}) collective-permute-start(f32[13,4,8,128]{3,2,1,0:T(8,128)S(1)} %get-tuple-element.45), channel_id=1, source_target_pairs={{0,1},{1,0},{2,3},{3,2},{4,5},{5,4},{6,7},{7,6},{8,9},{9,8},{10,11... | collective-permute-start | bytes 638984 | tf_op jit(solution)/shard_map/ppermute | solution.py:550
  23.8 15.1 %collective-permute-start.34 = (f32[12,4,8,128]{3,2,1,0:T(8,128)S(1)}, f32[12,4,8,128]{3,2,1,0:T(8,128)S(1)}, u32[]{:S(2)}, u32[]{:S(2)}) collective-permute-start(f32[12,4,8,128]{3,2,1,0:T(8,128)S(1)} %get-tuple-element.46), channel_id=1, source_target_pairs={{1,2},{2,1},{3,4},{4,3},{5,6},{6,5},{7,8},{8,7},{9,10},{10,9},{11,... | collective-permute-start | bytes 589832 | tf_op jit(solution)/shard_map/ppermute | solution.py:546
  25.7 13.2 %collective-permute-start.35 = (f32[12,4,8,128]{3,2,1,0:T(8,128)S(1)}, f32[12,4,8,128]{3,2,1,0:T(8,128)S(1)}, u32[]{:S(2)}, u32[]{:S(2)}) collective-permute-start(f32[12,4,8,128]{3,2,1,0:T(8,128)S(1)} %get-tuple-element.47), channel_id=1, source_target_pairs={{0,1},{1,0},{2,3},{3,2},{4,5},{5,4},{6,7},{7,6},{8,9},{9,8},{10,11... | collective-permute-start | bytes 589832 | tf_op jit(solution)/shard_map/ppermute | solution.py:547
  68.4 28.3 %copy-start.2 = (f32[16,32,128]{2,1,0:T(8,128)}, f32[16,32,128]{2,1,0:T(8,128)S(1)}, u32[]{:S(2)}) copy-start(f32[16,32,128]{2,1,0:T(8,128)S(1)} %get-tuple-element.19) | copy-start | bytes 786436 | tf_op jit(solution)/shard_map/cond
  68.4 10.9 %collective-permute-start = (f32[16,32,128]{2,1,0:T(8,128)S(1)}, f32[16,32,128]{2,1,0:T(8,128)S(1)}, u32[]{:S(2)}, u32[]{:S(2)}) collective-permute-start(f32[16,32,128]{2,1,0:T(8,128)S(1)} %bitcast.62), channel_id=1, source_target_pairs={{0,16},{16,32},{32,48},{48,64},{64,80},{80,96},{96,112},{112,128},... | collective-permute-start | bytes 786440 | tf_op jit(solution)/shard_map/cond/branch_0_fun/ppermute | solution.py:611
  74.3 14.5 %collective-permute-start.3 = (f32[1,32,128]{2,1,0:T(8,128)S(1)}, f32[1,32,128]{2,1,0:T(8,128)S(1)}, u32[]{:S(2)}, u32[]{:S(2)}) collective-permute-start(f32[1,32,128]{2,1,0:T(8,128)S(1)} %get-tuple-element.127), channel_id=1, source_target_pairs={{0,1},{1,2},{2,3},{3,4},{4,5},{5,6},{6,7},{7,8},{8,9},{9,10},{10,1... | collective-permute-start | bytes 49160 | tf_op jit(solution)/shard_map/cond/branch_0_fun/ppermute | solution.py:599
  77.4 11.5 %collective-permute-start.1 = (f32[1,32,128]{2,1,0:T(8,128)S(1)}, f32[1,32,128]{2,1,0:T(8,128)S(1)}, u32[]{:S(2)}, u32[]{:S(2)}) collective-permute-start(f32[1,32,128]{2,1,0:T(8,128)S(1)} %get-tuple-element.128), channel_id=1, source_target_pairs={{1,0},{2,1},{3,2},{4,3},{5,4},{6,5},{7,6},{8,7},{9,8},{10,9},{11,1... | collective-permute-start | bytes 49160 | tf_op jit(solution)/shard_map/cond/branch_0_fun/ppermute | solution.py:601
  79.4 9.8 %collective-permute-start.4 = (f32[1,32,128]{2,1,0:T(8,128)S(1)}, f32[1,32,128]{2,1,0:T(8,128)S(1)}, u32[]{:S(2)}, u32[]{:S(2)}) collective-permute-start(f32[1,32,128]{2,1,0:T(8,128)S(1)} %get-tuple-element.129), channel_id=1, source_target_pairs={{0,1},{1,2},{2,3},{3,4},{4,5},{5,6},{6,7},{7,8},{8,9},{9,10},{10,1... | collective-permute-start | bytes 49160 | tf_op jit(solution)/shard_map/cond/branch_0_fun/ppermute | solution.py:599
  86.9 9.0 %collective-permute-start.2 = (f32[1,32,128]{2,1,0:T(8,128)S(1)}, f32[1,32,128]{2,1,0:T(8,128)S(1)}, u32[]{:S(2)}, u32[]{:S(2)}) collective-permute-start(f32[1,32,128]{2,1,0:T(8,128)S(1)} %get-tuple-element.130), channel_id=1, source_target_pairs={{1,0},{2,1},{3,2},{4,3},{5,4},{6,5},{7,6},{8,7},{9,8},{10,9},{11,1... | collective-permute-start | bytes 49160 | tf_op jit(solution)/shard_map/cond/branch_0_fun/ppermute | solution.py:601
  96.7 4.5 collective-permute-start.6
  98.7 10.6 %collective-permute-start.5 = (f32[1,32,128]{2,1,0:T(8,128)S(1)}, f32[1,32,128]{2,1,0:T(8,128)S(1)}, u32[]{:S(2)}, u32[]{:S(2)}) collective-permute-start(f32[1,32,128]{2,1,0:T(8,128)S(1)} %get-tuple-element.126), channel_id=1, source_target_pairs={{1,0},{2,1},{3,2},{4,3},{5,4},{6,5},{7,6},{8,7},{9,8},{10,9},{11,1... | collective-permute-start | bytes 49160 | tf_op jit(solution)/shard_map/cond/branch_0_fun/ppermute | solution.py:601
  132.4 4.7 collective-permute-start.8
  135.1 9.0 %collective-permute-start.7 = (f32[1,32,128]{2,1,0:T(8,128)S(1)}, f32[1,32,128]{2,1,0:T(8,128)S(1)}, u32[]{:S(2)}, u32[]{:S(2)}) collective-permute-start(f32[1,32,128]{2,1,0:T(8,128)S(1)} %get-tuple-element.124), channel_id=1, source_target_pairs={{1,0},{2,1},{3,2},{4,3},{5,4},{6,5},{7,6},{8,7},{9,8},{10,9},{11,1... | collective-permute-start | bytes 49160 | tf_op jit(solution)/shard_map/cond/branch_0_fun/ppermute | solution.py:601
  170.3 4.7 collective-permute-start.10
  173.1 9.0 %collective-permute-start.9 = (f32[1,32,128]{2,1,0:T(8,128)S(1)}, f32[1,32,128]{2,1,0:T(8,128)S(1)}, u32[]{:S(2)}, u32[]{:S(2)}) collective-permute-start(f32[1,32,128]{2,1,0:T(8,128)S(1)} %get-tuple-element.122), channel_id=1, source_target_pairs={{1,0},{2,1},{3,2},{4,3},{5,4},{6,5},{7,6},{8,7},{9,8},{10,9},{11,1... | collective-permute-start | bytes 49160 | tf_op jit(solution)/shard_map/cond/branch_0_fun/ppermute | solution.py:601
  209.2 49.5 %copy-start.3 = (f32[16,32,128]{2,1,0:T(8,128)}, f32[16,32,128]{2,1,0:T(8,128)S(1)}, u32[]{:S(2)}) copy-start(f32[16,32,128]{2,1,0:T(8,128)S(1)} %get-tuple-element.92) | copy-start | bytes 786436 | tf_op jit(solution)/shard_map/cond
  209.3 4.7 collective-permute-start.12
  212.0 9.0 %collective-permute-start.11 = (f32[1,32,128]{2,1,0:T(8,128)S(1)}, f32[1,32,128]{2,1,0:T(8,128)S(1)}, u32[]{:S(2)}, u32[]{:S(2)}) collective-permute-start(f32[1,32,128]{2,1,0:T(8,128)S(1)} %get-tuple-element.120), channel_id=1, source_target_pairs={{1,0},{2,1},{3,2},{4,3},{5,4},{6,5},{7,6},{8,7},{9,8},{10,9},{11,1... | collective-permute-start | bytes 49160 | tf_op jit(solution)/shard_map/cond/branch_0_fun/ppermute | solution.py:601
  246.7 4.7 collective-permute-start.14
  249.5 9.0 %collective-permute-start.13 = (f32[1,32,128]{2,1,0:T(8,128)S(1)}, f32[1,32,128]{2,1,0:T(8,128)S(1)}, u32[]{:S(2)}, u32[]{:S(2)}) collective-permute-start(f32[1,32,128]{2,1,0:T(8,128)S(1)} %get-tuple-element.118), channel_id=1, source_target_pairs={{1,0},{2,1},{3,2},{4,3},{5,4},{6,5},{7,6},{8,7},{9,8},{10,9},{11,1... | collective-permute-start | bytes 49160 | tf_op jit(solution)/shard_map/cond/branch_0_fun/ppermute | solution.py:601
  285.5 4.7 collective-permute-start.16
  288.3 9.0 %collective-permute-start.15 = (f32[1,32,128]{2,1,0:T(8,128)S(1)}, f32[1,32,128]{2,1,0:T(8,128)S(1)}, u32[]{:S(2)}, u32[]{:S(2)}) collective-permute-start(f32[1,32,128]{2,1,0:T(8,128)S(1)} %get-tuple-element.116), channel_id=1, source_target_pairs={{1,0},{2,1},{3,2},{4,3},{5,4},{6,5},{7,6},{8,7},{9,8},{10,9},{11,1... | collective-permute-start | bytes 49160 | tf_op jit(solution)/shard_map/cond/branch_0_fun/ppermute | solution.py:601
  322.9 4.7 collective-permute-start.18
  325.6 9.0 %collective-permute-start.17 = (f32[1,32,128]{2,1,0:T(8,128)S(1)}, f32[1,32,128]{2,1,0:T(8,128)S(1)}, u32[]{:S(2)}, u32[]{:S(2)}) collective-permute-start(f32[1,32,128]{2,1,0:T(8,128)S(1)} %get-tuple-element.114), channel_id=1, source_target_pairs={{1,0},{2,1},{3,2},{4,3},{5,4},{6,5},{7,6},{8,7},{9,8},{10,9},{11,1... | collective-permute-start | bytes 49160 | tf_op jit(solution)/shard_map/cond/branch_0_fun/ppermute | solution.py:601
  336.2 4.3 collective-permute-start.20
  338.2 9.7 %collective-permute-start.19 = (f32[1,32,128]{2,1,0:T(8,128)S(1)}, f32[1,32,128]{2,1,0:T(8,128)S(1)}, u32[]{:S(2)}, u32[]{:S(2)}) collective-permute-start(f32[1,32,128]{2,1,0:T(8,128)S(1)} %get-tuple-element.112), channel_id=1, source_target_pairs={{1,0},{2,1},{3,2},{4,3},{5,4},{6,5},{7,6},{8,7},{9,8},{10,9},{11,1... | collective-permute-start | bytes 49160 | tf_op jit(solution)/shard_map/cond/branch_0_fun/ppermute | solution.py:601
  371.1 4.7 collective-permute-start.22
  373.8 9.0 %collective-permute-start.21 = (f32[1,32,128]{2,1,0:T(8,128)S(1)}, f32[1,32,128]{2,1,0:T(8,128)S(1)}, u32[]{:S(2)}, u32[]{:S(2)}) collective-permute-start(f32[1,32,128]{2,1,0:T(8,128)S(1)} %get-tuple-element.110), channel_id=1, source_target_pairs={{1,0},{2,1},{3,2},{4,3},{5,4},{6,5},{7,6},{8,7},{9,8},{10,9},{11,1... | collective-permute-start | bytes 49160 | tf_op jit(solution)/shard_map/cond/branch_0_fun/ppermute | solution.py:601
  408.9 4.7 collective-permute-start.24
  411.7 9.0 %collective-permute-start.23 = (f32[1,32,128]{2,1,0:T(8,128)S(1)}, f32[1,32,128]{2,1,0:T(8,128)S(1)}, u32[]{:S(2)}, u32[]{:S(2)}) collective-permute-start(f32[1,32,128]{2,1,0:T(8,128)S(1)} %get-tuple-element.108), channel_id=1, source_target_pairs={{1,0},{2,1},{3,2},{4,3},{5,4},{6,5},{7,6},{8,7},{9,8},{10,9},{11,1... | collective-permute-start | bytes 49160 | tf_op jit(solution)/shard_map/cond/branch_0_fun/ppermute | solution.py:601
  447.7 4.7 collective-permute-start.26
  450.4 9.0 %collective-permute-start.25 = (f32[1,32,128]{2,1,0:T(8,128)S(1)}, f32[1,32,128]{2,1,0:T(8,128)S(1)}, u32[]{:S(2)}, u32[]{:S(2)}) collective-permute-start(f32[1,32,128]{2,1,0:T(8,128)S(1)} %get-tuple-element.106), channel_id=1, source_target_pairs={{1,0},{2,1},{3,2},{4,3},{5,4},{6,5},{7,6},{8,7},{9,8},{10,9},{11,1... | collective-permute-start | bytes 49160 | tf_op jit(solution)/shard_map/cond/branch_0_fun/ppermute | solution.py:601
  460.7 62.4 %copy-start.4 = (f32[16,32,128]{2,1,0:T(8,128)}, f32[16,32,128]{2,1,0:T(8,128)S(1)}, u32[]{:S(2)}) copy-start(f32[16,32,128]{2,1,0:T(8,128)S(1)} %get-tuple-element.83) | copy-start | bytes 786436 | tf_op jit(solution)/shard_map/cond
  484.9 4.7 collective-permute-start.28
  487.7 9.0 %collective-permute-start.27 = (f32[1,32,128]{2,1,0:T(8,128)S(1)}, f32[1,32,128]{2,1,0:T(8,128)S(1)}, u32[]{:S(2)}, u32[]{:S(2)}) collective-permute-start(f32[1,32,128]{2,1,0:T(8,128)S(1)} %get-tuple-element.104), channel_id=1, source_target_pairs={{1,0},{2,1},{3,2},{4,3},{5,4},{6,5},{7,6},{8,7},{9,8},{10,9},{11,1... | collective-permute-start | bytes 49160 | tf_op jit(solution)/shard_map/cond/branch_0_fun/ppermute | solution.py:601
  524.2 4.7 collective-permute-start.30
  527.0 9.0 %collective-permute-start.29 = (f32[1,32,128]{2,1,0:T(8,128)S(1)}, f32[1,32,128]{2,1,0:T(8,128)S(1)}, u32[]{:S(2)}, u32[]{:S(2)}) collective-permute-start(f32[1,32,128]{2,1,0:T(8,128)S(1)} %get-tuple-element.102), channel_id=1, source_target_pairs={{1,0},{2,1},{3,2},{4,3},{5,4},{6,5},{7,6},{8,7},{9,8},{10,9},{11,1... | collective-permute-start | bytes 49160 | tf_op jit(solution)/shard_map/cond/branch_0_fun/ppermute | solution.py:601

commit v3 on v2

--- a/solution.py
+++ b/solution.py
@@ -21,12 +21,12 @@
 FACE = 0.5 * STEP_RATE * SIGMA
 
 RIM = STEPS * ITERS
-KEEP = ITERS - 1
 SUB = 8
 LANES = 128
 TOTALS = 2 * RIM + 1 + ITERS
 GROUPS_OF_8 = (TOTALS + 7) // 8
 NOISE = 1e-8
+ROUNDING = 5e-7
 ALLOWED = 5e-5
 
 
@@ -232,10 +232,20 @@
     size = totals[2 * RIM][0] + energy(best1, nu)
     for i in range(ITERS):
         size = size + 2.0 * best1[i] * totals[2 * RIM + 1 + i][0]
+    d = [jnp.zeros_like(c1[0])] * RIM
+    for i, u in enumerate(q):
+        for j, v in enumerate(best2):
+            half = 0.5 * (proper(u) * v)
+            d[i + j] = d[i + j] + half
+            d[abs(i - j)] = d[abs(i - j)] + half
+    for k in range(ITERS):
+        d[k] = d[k] + best1[k]
+    for k in range(RIM):
+        moved = moved + (0.5 * ROUNDING**2) * (d[k] * d[k]) * (nu[0][0] + nu[2 * k][0])
     good = jnp.where(moved <= ALLOWED**2 * size, 1.0, 0.0)
     for shift in (4, 2, 1):
         good = jnp.minimum(good, roll(good, shift, 0))
-    return best1, [proper(v) for v in q], best2, good
+    return best1, d, good
 
 
 def fill_weights(conduct, fields, first, last):
@@ -372,7 +382,7 @@
         swap(far, near, RIM, q, odd, x[depth - 1, q], x[0, q])
 
 
-def basis_kernel(x, res, far, near, a, afar, anear, basis, sums, kept, ring, done, *fields):
+def basis_kernel(x, res, far, near, a, afar, anear, basis, sums, kept, done, *fields):
     depth = x.shape[0]
     span = depth + 2 * RIM
     low, high = RIM - 1, RIM + depth
@@ -382,7 +392,6 @@
     mask = inside(alo, ahi, low, high)
     fill_weights(conductivities(a, alo, ahi), fields, 0, span - 1)
     wz = fields[0]
-    first, count = RIM - KEEP, depth + 2 * KEEP
     totals = {}
 
     def take(key, terms):
@@ -393,16 +402,12 @@
         else:
             totals[key] = (s, jnp.zeros_like(s))
 
-    def place(k):
-        return (kept, k) if k <= ITERS else (ring, k % 3)
-
     def store(k, e, new, old):
         if e in mask:
             new = [n * mask[e] for n in new]
         if k < RIM:
-            ref, slot = place(k)
             for q in range(4):
-                ref[slot, e, q] = new[q]
+                kept[k, e, q] = new[q]
         if RIM <= e < RIM + depth:
             if k < RIM:
                 take(2 * k, [n * n for n in new])
@@ -415,7 +420,7 @@
                 take(2 * RIM + 1 + k, [n * u for n, u in zip(new, v)])
 
     def copy(k):
-        return pltpu.make_async_copy(kept.at[k, pl.ds(first, count)], basis.at[k], done.at[k])
+        return pltpu.make_async_copy(kept.at[k, pl.ds(RIM, depth)], basis.at[k], done.at[k])
 
     for e in range(span):
         if e < RIM:
@@ -438,73 +443,36 @@
             if k == 1:
                 new = [0.5 * i for i in image]
             else:
-                ref, slot = place(k - 2)
-                new = [i - ref[slot, e, q] for q, i in enumerate(image)]
+                new = [i - kept[k - 2, e, q] for q, i in enumerate(image)]
             store(k, e, new, v)
 
-        across(planes(*place(k - 1)), fields, k, span - 1 - k, emit)
-        if k <= ITERS:
+        across(planes(kept, k - 1), fields, k, span - 1 - k, emit)
+        if k < RIM:
             copy(k).start()
     pack([totals[i] for i in range(TOTALS)], sums)
-    for k in range(ITERS + 1):
+    for k in range(RIM):
         copy(k).wait()
 
 
-def states_kernel(gathered, basis, x, a, afar, anear, out, flag, kept, ring, final, done, *fields):
+def states_kernel(gathered, basis, x, out, flag, kept, done):
     depth = x.shape[0]
-    first, count = RIM - KEEP, depth + 2 * KEEP
-    copies = [pltpu.make_async_copy(basis.at[k], kept.at[k], done.at[k]) for k in range(ITERS + 1)]
+    copies = [pltpu.make_async_copy(basis.at[k], kept.at[k], done.at[k]) for k in range(RIM)]
     for copy in copies:
         copy.start()
-    alo, ahi = sides(afar, anear, is_odd())
-    mask = inside(alo, ahi, KEEP - 1, KEEP + depth)
-    conduct = conductivities(a, alo, ahi)
-    fill_weights(lambda e: conduct(e + first), fields, 0, count - 1)
-    c1, q1, c2, good = solve(unpack(gathered))
+    c, d, good = solve(unpack(gathered))
     flag[0] = good[0, 0].astype(jnp.int32)
     for copy in copies:
         copy.wait()
-
-    def store(k, e, new):
-        if e in mask:
-            new = [n * mask[e] for n in new]
-        z = e - KEEP
+    for z in range(depth):
         for q in range(4):
-            if k < ITERS - 1:
-                ring[k % 3, e, q] = new[q]
-            if 0 <= z < depth:
-                s = final[z, q] + c2[k] * new[q]
-                if k < ITERS - 1:
-                    final[z, q] = s
-                else:
-                    out[0, 1, z, pl.ds(q, SUB, stride=4), :] = s
-
-    for e in range(count):
-        z = e - KEEP
-        new = []
-        for q in range(4):
-            parts = [kept[k, e, q] for k in range(ITERS + 1)]
-            if 0 <= z < depth:
-                s = x[z, q]
-                for k in range(ITERS):
-                    s = s + c1[k] * parts[k]
-                final[z, q] = s
-                out[0, 0, z, pl.ds(q, SUB, stride=4), :] = s
-            r = q1[0] * parts[0]
-            for k in range(1, ITERS + 1):
-                r = r + q1[k] * parts[k]
-            new.append(r)
-        store(0, e, new)
-    for k in range(1, ITERS):
-
-        def emit(e, v, image, k=k):
-            if k == 1:
-                new = [0.5 * i for i in image]
-            else:
-                new = [i - ring[(k - 2) % 3, e, q] for q, i in enumerate(image)]
-            store(k, e, new)
-
-        across(planes(ring, (k - 1) % 3), fields, k, count - 1 - k, emit)
+            one = two = x[z, q]
+            for k in range(RIM):
+                part = kept[k, z, q]
+                two = two + d[k] * part
+                if k < ITERS:
+                    one = one + c[k] * part
+            out[0, 0, z, pl.ds(q, SUB, stride=4), :] = one
+            out[0, 1, z, pl.ds(q, SUB, stride=4), :] = two
 
 
 def call(kernel, outs, scratch, sent=None, read=None, inputs=0, copies=0, weights=True):
@@ -532,7 +500,7 @@
 def fast(c_points, corrections, conductivity, forcing):
     times, slabs = lax.axis_size("tm"), lax.axis_size("space")
     depth = forcing.shape[0]
-    span, count = depth + 2 * RIM, depth + 2 * KEEP
+    span = depth + 2 * RIM
     tile = (4, SUB, LANES)
     far_pairs = [p for i in range(1, slabs - 1, 2) for p in ((i, i + 1), (i + 1, i))]
     near_pairs = [p for i in range(0, slabs - 1, 2) for p in ((i, i + 1), (i + 1, i))]
@@ -548,25 +516,26 @@
     x, res, far, near = call(open_kernel, [own, own, sent, sent], [], inputs=4)(own)(point, fix, source, cond)
     far = lax.ppermute(far, "space", far_pairs)
     near = lax.ppermute(near, "space", near_pairs)
-    field, part = (span, *tile), (count, *tile)
+    field = (span, *tile)
     basis, sums = call(
         basis_kernel,
-        [(ITERS + 1, *part), (slabs, 1, LANES)],
-        [(ITERS + 1, *field), (3, *field)],
+        [(RIM, *own), (slabs, 1, LANES)],
+        [(RIM, *field)],
         sent=0,
         inputs=7,
-        copies=ITERS + 1,
+        copies=RIM,
     )(field)(x, res, far, near, cond, afar, anear)
     basis = pltpu.with_memory_space_constraint(basis, pltpu.HBM)
     sums = lax.all_to_all(sums, "space", 0, 0, tiled=True)
     return call(
         states_kernel,
         [(1, STEPS, depth, 4 * SUB, LANES), None],
-        [(ITERS + 1, *part), (3, *part), own],
+        [(RIM, *own)],
         read=1,
-        inputs=6,
-        copies=ITERS + 1,
-    )(part)(sums, basis, x, cond, afar, anear)
+        inputs=3,
+        copies=RIM,
+        weights=False,
+    )(field)(sums, basis, x)
 
 
 def copy_for_each(array, axis):

time: 565 us -> 562 us (level)
  no operation moved by 1% of the time
where the time goes in v3:
time: 562 us; the launch traced here: 560 us
  blocking collectives  239 us (43%)
  waiting for transfers between devices  113 us (20%)
  starting transfers between devices  104 us (19%)
  other arithmetic  42.9 us (8%)
  loops' own time  42.6 us (8%)
  Pallas kernels  10.3 us (2%)
  local copies, waits for them, and re-layouts  7.75 us (1%)
    all_to_all x12, blocking collectives, copy_for_each(): lax.all_to_all(jnp.broadcast_to(array[None], (devices, *array.shape)), ax...  221 us
    ppermute x15, waiting for transfers between devices, extended(): lax.ppermute(head, axis, [((i + 1) % count, i) for i in range(ends)])  99.1 us
    ppermute x15, starting transfers between devices, extended(): lax.ppermute(tail, axis, [(i, (i + 1) % count) for i in range(ends)])  44.8 us
    another operation x1, loops' own time, body(): return lax.cond(good[0] > 0, lambda: out, lambda: plain(*args))  42.6 us
    ppermute x15, starting transfers between devices, extended(): lax.ppermute(head, axis, [((i + 1) % count, i) for i in range(ends)])  30.1 us
    all_to_all x1, blocking collectives, fast(): sums = lax.all_to_all(sums, 'space', 0, 0, tiled=True)  18 us
    concatenate x12, other arithmetic, packed_total(): subtotal = over_copies(jnp.concatenate([a.ravel() for a in arrays]), axis)  15.6 us
    reduce_sum x12, other arithmetic, pair_sums(): jnp.sum(residual * residual)  15.1 us
  transfers between devices with their start and end apart: 36, of which 16 were waited for; matrix products, arithmetic and copies ran while one was open for 0% of the time, Pallas kernels for 0%

profile of v3, /device:TPU:1, one launch (start us, length us, event | category | flops | bytes accessed | tf_op | source)
XLA Modules:
  0.0 560.0 jit_solution(17916686328676559442)
XLA Ops:
  0.0 4.8 collective-permute-start.31
  8.8 12.8 %collective-permute-start.32 = (f32[13,4,8,128]{3,2,1,0:T(8,128)S(1)}, f32[13,4,8,128]{3,2,1,0:T(8,128)S(1)}, u32[]{:S(2)}, u32[]{:S(2)}) collective-permute-start(f32[13,4,8,128]{3,2,1,0:T(8,128)S(1)} %get-tuple-element.44), channel_id=1, source_target_pairs={{1,2},{2,1},{3,4},{4,3},{5,6},{6,5},{7,8},{8,7},{9,10},{10,9},{11,... | collective-permute-start | bytes 638984 | tf_op jit(solution)/shard_map/ppermute | solution.py:517
  27.4 11.3 %collective-permute-done.34.afar = f32[12,4,8,128]{3,2,1,0:T(8,128)S(1)} collective-permute-done((f32[12,4,8,128]{3,2,1,0:T(8,128)S(1)}, f32[12,4,8,128]{3,2,1,0:T(8,128)S(1)}, u32[]{:S(2)}, u32[]{:S(2)}) %collective-permute-start.34) | collective-permute-done | bytes 196640 | tf_op jit(solution)/shard_map/ppermute | solution.py:514
  38.7 5.2 shard_map.50
  44.0 18.0 %all_to_all.77.gathered = f32[16,1,128]{2,1,0:T(1,128)S(1)} all-to-all(f32[16,1,128]{2,1,0:T(1,128)S(1)} %get-tuple-element.48), channel_id=1, replica_groups=mesh['tm'=32,'space'=16] {'space'}, dimensions={0} | all-to-all | bytes 16384 | tf_op jit(solution)/shard_map/all_to_all | solution.py:529
  62.0 3.5 shard_map.51
  66.1 493.9 %conditional.1 = (f32[1,2,16,32,128]{4,3,2,1,0:T(8,128)}) conditional(s32[]{:T(128)} %bitcast.55, (f32[1,16,32,128]{3,2,1,0:T(8,128)S(1)}, f32[1,16,32,128]{3,2,1,0:T(8,128)S(1)}, f32[16,32,128]{2,1,0:T(8,128)S(1)}, f32[16,32,128]{2,1,0:T(8,128)S(1)}) %tuple.77, f32[1,2,16,32,128]{4,3,2,1,0:T(8,128)} %get-tuple-element.56), branch_computations={%region_0.37_spmd, %region_37.38_spmd} | conditional | flops 52701000 | bytes 76249768 | solution.py:656
  66.1 5.9 %collective-permute-start = (f32[16,32,128]{2,1,0:T(8,128)S(1)}, f32[16,32,128]{2,1,0:T(8,128)S(1)}, u32[]{:S(2)}, u32[]{:S(2)}) collective-permute-start(f32[16,32,128]{2,1,0:T(8,128)S(1)} %bitcast.62), channel_id=1, source_target_pairs={{0,16},{16,32},{32,48},{48,64},{64,80},{80,96},{96,112},{112,128},... | collective-permute-start | bytes 786440 | tf_op jit(solution)/shard_map/cond/branch_0_fun/ppermute | solution.py:580
  72.0 3.0 collective-permute-start.3
  77.0 7.5 %collective-permute-start.4 = (f32[1,32,128]{2,1,0:T(8,128)S(1)}, f32[1,32,128]{2,1,0:T(8,128)S(1)}, u32[]{:S(2)}, u32[]{:S(2)}) collective-permute-start(f32[1,32,128]{2,1,0:T(8,128)S(1)} %get-tuple-element.129), channel_id=1, source_target_pairs={{0,1},{1,2},{2,3},{3,4},{4,5},{5,6},{6,7},{7,8},{8,9},{9,10},{10,1... | collective-permute-start | bytes 49160 | tf_op jit(solution)/shard_map/cond/branch_0_fun/ppermute | solution.py:568
  86.8 6.7 %collective-permute-done.2 = f32[1,32,128]{2,1,0:T(8,128)S(1)} collective-permute-done((f32[1,32,128]{2,1,0:T(8,128)S(1)}, f32[1,32,128]{2,1,0:T(8,128)S(1)}, u32[]{:S(2)}, u32[]{:S(2)}) %collective-permute-start.2) | collective-permute-done | bytes 16416 | tf_op jit(solution)/shard_map/cond/branch_0_fun/ppermute | solution.py:570
  96.3 2.4 collective-permute-start.5
  98.7 8.2 %collective-permute-done.5 = f32[1,32,128]{2,1,0:T(8,128)S(1)} collective-permute-done((f32[1,32,128]{2,1,0:T(8,128)S(1)}, f32[1,32,128]{2,1,0:T(8,128)S(1)}, u32[]{:S(2)}, u32[]{:S(2)}) %collective-permute-start.5) | collective-permute-done | bytes 16416 | tf_op jit(solution)/shard_map/cond/branch_0_fun/ppermute | solution.py:570
  109.5 18.6 %all_to_all.65 = f32[16,1,2]{2,1,0:T(1,128)S(1)} all-to-all(f32[16,1,2]{2,1,0:T(1,128)S(1)} %broadcast_in_dim.0), channel_id=1, replica_groups=mesh['tm'=32,'space'=16] {'space'}, dimensions={0} | all-to-all | bytes 256 | tf_op jit(solution)/shard_map/cond/branch_0_fun/all_to_all | solution.py:543
  130.0 2.8 collective-permute-start.8
  134.9 6.8 %collective-permute-done.7 = f32[1,32,128]{2,1,0:T(8,128)S(1)} collective-permute-done((f32[1,32,128]{2,1,0:T(8,128)S(1)}, f32[1,32,128]{2,1,0:T(8,128)S(1)}, u32[]{:S(2)}, u32[]{:S(2)}) %collective-permute-start.7) | collective-permute-done | bytes 16416 | tf_op jit(solution)/shard_map/cond/branch_0_fun/ppermute | solution.py:570
  144.2 18.4 %all_to_all.66 = f32[16,1,2]{2,1,0:T(1,128)S(1)} all-to-all(f32[16,1,2]{2,1,0:T(1,128)S(1)} %broadcast_in_dim.1), channel_id=1, replica_groups=mesh['tm'=32,'space'=16] {'space'}, dimensions={0} | all-to-all | bytes 256 | tf_op jit(solution)/shard_map/cond/branch_0_fun/all_to_all | solution.py:543
  168.0 2.8 collective-permute-start.10
  172.7 7.0 %collective-permute-done.9 = f32[1,32,128]{2,1,0:T(8,128)S(1)} collective-permute-done((f32[1,32,128]{2,1,0:T(8,128)S(1)}, f32[1,32,128]{2,1,0:T(8,128)S(1)}, u32[]{:S(2)}, u32[]{:S(2)}) %collective-permute-start.9) | collective-permute-done | bytes 16416 | tf_op jit(solution)/shard_map/cond/branch_0_fun/ppermute | solution.py:570
  183.0 18.4 %all_to_all.67 = f32[16,1,2]{2,1,0:T(1,128)S(1)} all-to-all(f32[16,1,2]{2,1,0:T(1,128)S(1)} %broadcast_in_dim.2), channel_id=1, replica_groups=mesh['tm'=32,'space'=16] {'space'}, dimensions={0} | all-to-all | bytes 256 | tf_op jit(solution)/shard_map/cond/branch_0_fun/all_to_all | solution.py:543
  206.9 2.8 collective-permute-start.12
  211.6 7.0 %collective-permute-done.11 = f32[1,32,128]{2,1,0:T(8,128)S(1)} collective-permute-done((f32[1,32,128]{2,1,0:T(8,128)S(1)}, f32[1,32,128]{2,1,0:T(8,128)S(1)}, u32[]{:S(2)}, u32[]{:S(2)}) %collective-permute-start.11) | collective-permute-done | bytes 16416 | tf_op jit(solution)/shard_map/cond/branch_0_fun/ppermute | solution.py:570
  221.4 18.4 %all_to_all.68 = f32[16,1,2]{2,1,0:T(1,128)S(1)} all-to-all(f32[16,1,2]{2,1,0:T(1,128)S(1)} %broadcast_in_dim.3), channel_id=1, replica_groups=mesh['tm'=32,'space'=16] {'space'}, dimensions={0} | all-to-all | bytes 256 | tf_op jit(solution)/shard_map/cond/branch_0_fun/all_to_all | solution.py:543
  244.3 2.8 collective-permute-start.14
  249.0 7.0 %collective-permute-done.13 = f32[1,32,128]{2,1,0:T(8,128)S(1)} collective-permute-done((f32[1,32,128]{2,1,0:T(8,128)S(1)}, f32[1,32,128]{2,1,0:T(8,128)S(1)}, u32[]{:S(2)}, u32[]{:S(2)}) %collective-permute-start.13) | collective-permute-done | bytes 16416 | tf_op jit(solution)/shard_map/cond/branch_0_fun/ppermute | solution.py:570
  259.3 18.4 %all_to_all.69 = f32[16,1,2]{2,1,0:T(1,128)S(1)} all-to-all(f32[16,1,2]{2,1,0:T(1,128)S(1)} %broadcast_in_dim.4), channel_id=1, replica_groups=mesh['tm'=32,'space'=16] {'space'}, dimensions={0} | all-to-all | bytes 256 | tf_op jit(solution)/shard_map/cond/branch_0_fun/all_to_all | solution.py:543
  283.1 2.8 collective-permute-start.16
  287.8 7.0 %collective-permute-done.15 = f32[1,32,128]{2,1,0:T(8,128)S(1)} collective-permute-done((f32[1,32,128]{2,1,0:T(8,128)S(1)}, f32[1,32,128]{2,1,0:T(8,128)S(1)}, u32[]{:S(2)}, u32[]{:S(2)}) %collective-permute-start.15) | collective-permute-done | bytes 16416 | tf_op jit(solution)/shard_map/cond/branch_0_fun/ppermute | solution.py:570
  297.5 18.4 %all_to_all.70 = f32[16,1,2]{2,1,0:T(1,128)S(1)} all-to-all(f32[16,1,2]{2,1,0:T(1,128)S(1)} %broadcast_in_dim.5), channel_id=1, replica_groups=mesh['tm'=32,'space'=16] {'space'}, dimensions={0} | all-to-all | bytes 256 | tf_op jit(solution)/shard_map/cond/branch_0_fun/all_to_all | solution.py:543
  320.5 2.8 collective-permute-start.18
  325.2 7.0 %collective-permute-done.17 = f32[1,32,128]{2,1,0:T(8,128)S(1)} collective-permute-done((f32[1,32,128]{2,1,0:T(8,128)S(1)}, f32[1,32,128]{2,1,0:T(8,128)S(1)}, u32[]{:S(2)}, u32[]{:S(2)}) %collective-permute-start.17) | collective-permute-done | bytes 16416 | tf_op jit(solution)/shard_map/cond/branch_0_fun/ppermute | solution.py:570
  338.2 7.3 %collective-permute-done.19 = f32[1,32,128]{2,1,0:T(8,128)S(1)} collective-permute-done((f32[1,32,128]{2,1,0:T(8,128)S(1)}, f32[1,32,128]{2,1,0:T(8,128)S(1)}, u32[]{:S(2)}, u32[]{:S(2)}) %collective-permute-start.19) | collective-permute-done | bytes 16416 | tf_op jit(solution)/shard_map/cond/branch_0_fun/ppermute | solution.py:570
  348.1 18.6 %all_to_all.71 = f32[16,1,2]{2,1,0:T(1,128)S(1)} all-to-all(f32[16,1,2]{2,1,0:T(1,128)S(1)} %broadcast_in_dim.6), channel_id=1, replica_groups=mesh['tm'=32,'space'=16] {'space'}, dimensions={0} | all-to-all | bytes 256 | tf_op jit(solution)/shard_map/cond/branch_0_fun/all_to_all | solution.py:543
  368.7 2.8 collective-permute-start.22
  373.4 7.0 %collective-permute-done.21 = f32[1,32,128]{2,1,0:T(8,128)S(1)} collective-permute-done((f32[1,32,128]{2,1,0:T(8,128)S(1)}, f32[1,32,128]{2,1,0:T(8,128)S(1)}, u32[]{:S(2)}, u32[]{:S(2)}) %collective-permute-start.21) | collective-permute-done | bytes 16416 | tf_op jit(solution)/shard_map/cond/branch_0_fun/ppermute | solution.py:570
  383.1 18.4 %all_to_all.72 = f32[16,1,2]{2,1,0:T(1,128)S(1)} all-to-all(f32[16,1,2]{2,1,0:T(1,128)S(1)} %broadcast_in_dim.7), channel_id=1, replica_groups=mesh['tm'=32,'space'=16] {'space'}, dimensions={0} | all-to-all | bytes 256 | tf_op jit(solution)/shard_map/cond/branch_0_fun/all_to_all | solution.py:543
  406.6 2.8 collective-permute-start.24
  411.3 7.0 %collective-permute-done.23 = f32[1,32,128]{2,1,0:T(8,128)S(1)} collective-permute-done((f32[1,32,128]{2,1,0:T(8,128)S(1)}, f32[1,32,128]{2,1,0:T(8,128)S(1)}, u32[]{:S(2)}, u32[]{:S(2)}) %collective-permute-start.23) | collective-permute-done | bytes 16416 | tf_op jit(solution)/shard_map/cond/branch_0_fun/ppermute | solution.py:570
  421.5 18.4 %all_to_all.73 = f32[16,1,2]{2,1,0:T(1,128)S(1)} all-to-all(f32[16,1,2]{2,1,0:T(1,128)S(1)} %broadcast_in_dim.8), channel_id=1, replica_groups=mesh['tm'=32,'space'=16] {'space'}, dimensions={0} | all-to-all | bytes 256 | tf_op jit(solution)/shard_map/cond/branch_0_fun/all_to_all | solution.py:543
  445.3 2.8 collective-permute-start.26
  450.0 7.0 %collective-permute-done.25 = f32[1,32,128]{2,1,0:T(8,128)S(1)} collective-permute-done((f32[1,32,128]{2,1,0:T(8,128)S(1)}, f32[1,32,128]{2,1,0:T(8,128)S(1)}, u32[]{:S(2)}, u32[]{:S(2)}) %collective-permute-start.25) | collective-permute-done | bytes 16416 | tf_op jit(solution)/shard_map/cond/branch_0_fun/ppermute | solution.py:570
  459.6 18.4 %all_to_all.74 = f32[16,1,2]{2,1,0:T(1,128)S(1)} all-to-all(f32[16,1,2]{2,1,0:T(1,128)S(1)} %broadcast_in_dim.9), channel_id=1, replica_groups=mesh['tm'=32,'space'=16] {'space'}, dimensions={0} | all-to-all | bytes 256 | tf_op jit(solution)/shard_map/cond/branch_0_fun/all_to_all | solution.py:543
  482.4 2.8 collective-permute-start.28
  487.3 6.8 %collective-permute-done.27 = f32[1,32,128]{2,1,0:T(8,128)S(1)} collective-permute-done((f32[1,32,128]{2,1,0:T(8,128)S(1)}, f32[1,32,128]{2,1,0:T(8,128)S(1)}, u32[]{:S(2)}, u32[]{:S(2)}) %collective-permute-start.27) | collective-permute-done | bytes 16416 | tf_op jit(solution)/shard_map/cond/branch_0_fun/ppermute | solution.py:570
  497.5 18.4 %all_to_all.75 = f32[16,1,2]{2,1,0:T(1,128)S(1)} all-to-all(f32[16,1,2]{2,1,0:T(1,128)S(1)} %broadcast_in_dim.10), channel_id=1, replica_groups=mesh['tm'=32,'space'=16] {'space'}, dimensions={0} | all-to-all | bytes 256 | tf_op jit(solution)/shard_map/cond/branch_0_fun/all_to_all | solution.py:543
  521.7 2.8 collective-permute-start.30
  526.4 7.0 %collective-permute-done.29 = f32[1,32,128]{2,1,0:T(8,128)S(1)} collective-permute-done((f32[1,32,128]{2,1,0:T(8,128)S(1)}, f32[1,32,128]{2,1,0:T(8,128)S(1)}, u32[]{:S(2)}, u32[]{:S(2)}) %collective-permute-start.29) | collective-permute-done | bytes 16416 | tf_op jit(solution)/shard_map/cond/branch_0_fun/ppermute | solution.py:570
  536.0 18.4 %all_to_all.76 = f32[16,1,2]{2,1,0:T(1,128)S(1)} all-to-all(f32[16,1,2]{2,1,0:T(1,128)S(1)} %broadcast_in_dim.11), channel_id=1, replica_groups=mesh['tm'=32,'space'=16] {'space'}, dimensions={0} | all-to-all | bytes 256 | tf_op jit(solution)/shard_map/cond/branch_0_fun/all_to_all | solution.py:543
  (162 shorter events, 92.1 us)
Async XLA Ops:
  0.0 8.4 %collective-permute-start.31 = (f32[16,32,128]{2,1,0:T(8,128)}, f32[16,32,128]{2,1,0:T(8,128)S(1)}, u32[]{:S(2)}, u32[]{:S(2)}) collective-permute-start(f32[16,32,128]{2,1,0:T(8,128)} %bitcast.61), channel_id=1, source_target_pairs={{0,16},{16,32},{32,48},{48,64},{64,80},{80,96},{96,112},{112,128},... | collective-permute-start | bytes 786440 | tf_op jit(solution)/shard_map/ppermute | solution.py:510
  6.0 60.0 %copy-start = (f32[16,32,128]{2,1,0:T(8,128)S(1)}, f32[16,32,128]{2,1,0:T(8,128)}, u32[]{:S(2)}) copy-start(f32[16,32,128]{2,1,0:T(8,128)} %a.1) | copy-start | bytes 786436
  6.0 60.0 %copy-start.1 = (f32[16,32,128]{2,1,0:T(8,128)S(1)}, f32[16,32,128]{2,1,0:T(8,128)}, u32[]{:S(2)}) copy-start(f32[16,32,128]{2,1,0:T(8,128)} %f.1) | copy-start | bytes 786436
  6.1 60.0 %copy-start.5 = (f32[1,16,32,128]{3,2,1,0:T(8,128)S(1)}, f32[1,16,32,128]{3,2,1,0:T(8,128)}, u32[]{:S(2)}) copy-start(f32[1,16,32,128]{3,2,1,0:T(8,128)} %param.6) | copy-start | bytes 786436
  6.1 60.0 %copy-start.6 = (f32[1,16,32,128]{3,2,1,0:T(8,128)S(1)}, f32[1,16,32,128]{3,2,1,0:T(8,128)}, u32[]{:S(2)}) copy-start(f32[1,16,32,128]{3,2,1,0:T(8,128)} %param.7) | copy-start | bytes 786436
  8.8 29.9 %collective-permute-start.32 = (f32[13,4,8,128]{3,2,1,0:T(8,128)S(1)}, f32[13,4,8,128]{3,2,1,0:T(8,128)S(1)}, u32[]{:S(2)}, u32[]{:S(2)}) collective-permute-start(f32[13,4,8,128]{3,2,1,0:T(8,128)S(1)} %get-tuple-element.44), channel_id=1, source_target_pairs={{1,2},{2,1},{3,4},{4,3},{5,6},{6,5},{7,8},{8,7},{9,10},{10,9},{11,... | collective-permute-start | bytes 638984 | tf_op jit(solution)/shard_map/ppermute | solution.py:517
  21.7 17.1 %collective-permute-start.33 = (f32[13,4,8,128]{3,2,1,0:T(8,128)S(1)}, f32[13,4,8,128]{3,2,1,0:T(8,128)S(1)}, u32[]{:S(2)}, u32[]{:S(2)}) collective-permute-start(f32[13,4,8,128]{3,2,1,0:T(8,128)S(1)} %get-tuple-element.45), channel_id=1, source_target_pairs={{0,1},{1,0},{2,3},{3,2},{4,5},{5,4},{6,7},{7,6},{8,9},{9,8},{10,11... | collective-permute-start | bytes 638984 | tf_op jit(solution)/shard_map/ppermute | solution.py:518
  23.6 15.1 %collective-permute-start.34 = (f32[12,4,8,128]{3,2,1,0:T(8,128)S(1)}, f32[12,4,8,128]{3,2,1,0:T(8,128)S(1)}, u32[]{:S(2)}, u32[]{:S(2)}) collective-permute-start(f32[12,4,8,128]{3,2,1,0:T(8,128)S(1)} %get-tuple-element.46), channel_id=1, source_target_pairs={{1,2},{2,1},{3,4},{4,3},{5,6},{6,5},{7,8},{8,7},{9,10},{10,9},{11,... | collective-permute-start | bytes 589832 | tf_op jit(solution)/shard_map/ppermute | solution.py:514
  25.5 13.2 %collective-permute-start.35 = (f32[12,4,8,128]{3,2,1,0:T(8,128)S(1)}, f32[12,4,8,128]{3,2,1,0:T(8,128)S(1)}, u32[]{:S(2)}, u32[]{:S(2)}) collective-permute-start(f32[12,4,8,128]{3,2,1,0:T(8,128)S(1)} %get-tuple-element.47), channel_id=1, source_target_pairs={{0,1},{1,0},{2,3},{3,2},{4,5},{5,4},{6,7},{7,6},{8,9},{9,8},{10,11... | collective-permute-start | bytes 589832 | tf_op jit(solution)/shard_map/ppermute | solution.py:515
  66.1 28.3 %copy-start.2 = (f32[16,32,128]{2,1,0:T(8,128)}, f32[16,32,128]{2,1,0:T(8,128)S(1)}, u32[]{:S(2)}) copy-start(f32[16,32,128]{2,1,0:T(8,128)S(1)} %get-tuple-element.19) | copy-start | bytes 786436 | tf_op jit(solution)/shard_map/cond
  66.1 10.9 %collective-permute-start = (f32[16,32,128]{2,1,0:T(8,128)S(1)}, f32[16,32,128]{2,1,0:T(8,128)S(1)}, u32[]{:S(2)}, u32[]{:S(2)}) collective-permute-start(f32[16,32,128]{2,1,0:T(8,128)S(1)} %bitcast.62), channel_id=1, source_target_pairs={{0,16},{16,32},{32,48},{48,64},{64,80},{80,96},{96,112},{112,128},... | collective-permute-start | bytes 786440 | tf_op jit(solution)/shard_map/cond/branch_0_fun/ppermute | solution.py:580
  72.0 14.5 %collective-permute-start.3 = (f32[1,32,128]{2,1,0:T(8,128)S(1)}, f32[1,32,128]{2,1,0:T(8,128)S(1)}, u32[]{:S(2)}, u32[]{:S(2)}) collective-permute-start(f32[1,32,128]{2,1,0:T(8,128)S(1)} %get-tuple-element.127), channel_id=1, source_target_pairs={{0,1},{1,2},{2,3},{3,4},{4,5},{5,6},{6,7},{7,8},{8,9},{9,10},{10,1... | collective-permute-start | bytes 49160 | tf_op jit(solution)/shard_map/cond/branch_0_fun/ppermute | solution.py:568
  75.0 11.5 %collective-permute-start.1 = (f32[1,32,128]{2,1,0:T(8,128)S(1)}, f32[1,32,128]{2,1,0:T(8,128)S(1)}, u32[]{:S(2)}, u32[]{:S(2)}) collective-permute-start(f32[1,32,128]{2,1,0:T(8,128)S(1)} %get-tuple-element.128), channel_id=1, source_target_pairs={{1,0},{2,1},{3,2},{4,3},{5,4},{6,5},{7,6},{8,7},{9,8},{10,9},{11,1... | collective-permute-start | bytes 49160 | tf_op jit(solution)/shard_map/cond/branch_0_fun/ppermute | solution.py:570
  77.0 9.8 %collective-permute-start.4 = (f32[1,32,128]{2,1,0:T(8,128)S(1)}, f32[1,32,128]{2,1,0:T(8,128)S(1)}, u32[]{:S(2)}, u32[]{:S(2)}) collective-permute-start(f32[1,32,128]{2,1,0:T(8,128)S(1)} %get-tuple-element.129), channel_id=1, source_target_pairs={{0,1},{1,2},{2,3},{3,4},{4,5},{5,6},{6,7},{7,8},{8,9},{9,10},{10,1... | collective-permute-start | bytes 49160 | tf_op jit(solution)/shard_map/cond/branch_0_fun/ppermute | solution.py:568
  84.6 9.0 %collective-permute-start.2 = (f32[1,32,128]{2,1,0:T(8,128)S(1)}, f32[1,32,128]{2,1,0:T(8,128)S(1)}, u32[]{:S(2)}, u32[]{:S(2)}) collective-permute-start(f32[1,32,128]{2,1,0:T(8,128)S(1)} %get-tuple-element.130), channel_id=1, source_target_pairs={{1,0},{2,1},{3,2},{4,3},{5,4},{6,5},{7,6},{8,7},{9,8},{10,9},{11,1... | collective-permute-start | bytes 49160 | tf_op jit(solution)/shard_map/cond/branch_0_fun/ppermute | solution.py:570
  94.4 4.3 collective-permute-start.6
  96.3 10.6 %collective-permute-start.5 = (f32[1,32,128]{2,1,0:T(8,128)S(1)}, f32[1,32,128]{2,1,0:T(8,128)S(1)}, u32[]{:S(2)}, u32[]{:S(2)}) collective-permute-start(f32[1,32,128]{2,1,0:T(8,128)S(1)} %get-tuple-element.126), channel_id=1, source_target_pairs={{1,0},{2,1},{3,2},{4,3},{5,4},{6,5},{7,6},{8,7},{9,8},{10,9},{11,1... | collective-permute-start | bytes 49160 | tf_op jit(solution)/shard_map/cond/branch_0_fun/ppermute | solution.py:570
  130.0 4.9 collective-permute-start.8
  132.8 9.0 %collective-permute-start.7 = (f32[1,32,128]{2,1,0:T(8,128)S(1)}, f32[1,32,128]{2,1,0:T(8,128)S(1)}, u32[]{:S(2)}, u32[]{:S(2)}) collective-permute-start(f32[1,32,128]{2,1,0:T(8,128)S(1)} %get-tuple-element.124), channel_id=1, source_target_pairs={{1,0},{2,1},{3,2},{4,3},{5,4},{6,5},{7,6},{8,7},{9,8},{10,9},{11,1... | collective-permute-start | bytes 49160 | tf_op jit(solution)/shard_map/cond/branch_0_fun/ppermute | solution.py:570
  168.0 4.7 collective-permute-start.10
  170.7 9.0 %collective-permute-start.9 = (f32[1,32,128]{2,1,0:T(8,128)S(1)}, f32[1,32,128]{2,1,0:T(8,128)S(1)}, u32[]{:S(2)}, u32[]{:S(2)}) collective-permute-start(f32[1,32,128]{2,1,0:T(8,128)S(1)} %get-tuple-element.122), channel_id=1, source_target_pairs={{1,0},{2,1},{3,2},{4,3},{5,4},{6,5},{7,6},{8,7},{9,8},{10,9},{11,1... | collective-permute-start | bytes 49160 | tf_op jit(solution)/shard_map/cond/branch_0_fun/ppermute | solution.py:570
  206.9 51.2 %copy-start.3 = (f32[16,32,128]{2,1,0:T(8,128)}, f32[16,32,128]{2,1,0:T(8,128)S(1)}, u32[]{:S(2)}) copy-start(f32[16,32,128]{2,1,0:T(8,128)S(1)} %get-tuple-element.92) | copy-start | bytes 786436 | tf_op jit(solution)/shard_map/cond
  206.9 4.7 collective-permute-start.12
  209.7 9.0 %collective-permute-start.11 = (f32[1,32,128]{2,1,0:T(8,128)S(1)}, f32[1,32,128]{2,1,0:T(8,128)S(1)}, u32[]{:S(2)}, u32[]{:S(2)}) collective-permute-start(f32[1,32,128]{2,1,0:T(8,128)S(1)} %get-tuple-element.120), channel_id=1, source_target_pairs={{1,0},{2,1},{3,2},{4,3},{5,4},{6,5},{7,6},{8,7},{9,8},{10,9},{11,1... | collective-permute-start | bytes 49160 | tf_op jit(solution)/shard_map/cond/branch_0_fun/ppermute | solution.py:570
  244.3 4.7 collective-permute-start.14
  247.1 9.0 %collective-permute-start.13 = (f32[1,32,128]{2,1,0:T(8,128)S(1)}, f32[1,32,128]{2,1,0:T(8,128)S(1)}, u32[]{:S(2)}, u32[]{:S(2)}) collective-permute-start(f32[1,32,128]{2,1,0:T(8,128)S(1)} %get-tuple-element.118), channel_id=1, source_target_pairs={{1,0},{2,1},{3,2},{4,3},{5,4},{6,5},{7,6},{8,7},{9,8},{10,9},{11,1... | collective-permute-start | bytes 49160 | tf_op jit(solution)/shard_map/cond/branch_0_fun/ppermute | solution.py:570
  283.1 4.7 collective-permute-start.16
  285.9 9.0 %collective-permute-start.15 = (f32[1,32,128]{2,1,0:T(8,128)S(1)}, f32[1,32,128]{2,1,0:T(8,128)S(1)}, u32[]{:S(2)}, u32[]{:S(2)}) collective-permute-start(f32[1,32,128]{2,1,0:T(8,128)S(1)} %get-tuple-element.116), channel_id=1, source_target_pairs={{1,0},{2,1},{3,2},{4,3},{5,4},{6,5},{7,6},{8,7},{9,8},{10,9},{11,1... | collective-permute-start | bytes 49160 | tf_op jit(solution)/shard_map/cond/branch_0_fun/ppermute | solution.py:570
  320.5 4.7 collective-permute-start.18
  323.3 9.0 %collective-permute-start.17 = (f32[1,32,128]{2,1,0:T(8,128)S(1)}, f32[1,32,128]{2,1,0:T(8,128)S(1)}, u32[]{:S(2)}, u32[]{:S(2)}) collective-permute-start(f32[1,32,128]{2,1,0:T(8,128)S(1)} %get-tuple-element.114), channel_id=1, source_target_pairs={{1,0},{2,1},{3,2},{4,3},{5,4},{6,5},{7,6},{8,7},{9,8},{10,9},{11,1... | collective-permute-start | bytes 49160 | tf_op jit(solution)/shard_map/cond/branch_0_fun/ppermute | solution.py:570
  333.9 4.3 collective-permute-start.20
  335.8 9.7 %collective-permute-start.19 = (f32[1,32,128]{2,1,0:T(8,128)S(1)}, f32[1,32,128]{2,1,0:T(8,128)S(1)}, u32[]{:S(2)}, u32[]{:S(2)}) collective-permute-start(f32[1,32,128]{2,1,0:T(8,128)S(1)} %get-tuple-element.112), channel_id=1, source_target_pairs={{1,0},{2,1},{3,2},{4,3},{5,4},{6,5},{7,6},{8,7},{9,8},{10,9},{11,1... | collective-permute-start | bytes 49160 | tf_op jit(solution)/shard_map/cond/branch_0_fun/ppermute | solution.py:570
  368.7 4.7 collective-permute-start.22
  371.5 9.0 %collective-permute-start.21 = (f32[1,32,128]{2,1,0:T(8,128)S(1)}, f32[1,32,128]{2,1,0:T(8,128)S(1)}, u32[]{:S(2)}, u32[]{:S(2)}) collective-permute-start(f32[1,32,128]{2,1,0:T(8,128)S(1)} %get-tuple-element.110), channel_id=1, source_target_pairs={{1,0},{2,1},{3,2},{4,3},{5,4},{6,5},{7,6},{8,7},{9,8},{10,9},{11,1... | collective-permute-start | bytes 49160 | tf_op jit(solution)/shard_map/cond/branch_0_fun/ppermute | solution.py:570
  406.6 4.7 collective-permute-start.24
  409.3 9.0 %collective-permute-start.23 = (f32[1,32,128]{2,1,0:T(8,128)S(1)}, f32[1,32,128]{2,1,0:T(8,128)S(1)}, u32[]{:S(2)}, u32[]{:S(2)}) collective-permute-start(f32[1,32,128]{2,1,0:T(8,128)S(1)} %get-tuple-element.108), channel_id=1, source_target_pairs={{1,0},{2,1},{3,2},{4,3},{5,4},{6,5},{7,6},{8,7},{9,8},{10,9},{11,1... | collective-permute-start | bytes 49160 | tf_op jit(solution)/shard_map/cond/branch_0_fun/ppermute | solution.py:570
  445.3 4.7 collective-permute-start.26
  448.1 9.0 %collective-permute-start.25 = (f32[1,32,128]{2,1,0:T(8,128)S(1)}, f32[1,32,128]{2,1,0:T(8,128)S(1)}, u32[]{:S(2)}, u32[]{:S(2)}) collective-permute-start(f32[1,32,128]{2,1,0:T(8,128)S(1)} %get-tuple-element.106), channel_id=1, source_target_pairs={{1,0},{2,1},{3,2},{4,3},{5,4},{6,5},{7,6},{8,7},{9,8},{10,9},{11,1... | collective-permute-start | bytes 49160 | tf_op jit(solution)/shard_map/cond/branch_0_fun/ppermute | solution.py:570
  458.3 62.2 %copy-start.4 = (f32[16,32,128]{2,1,0:T(8,128)}, f32[16,32,128]{2,1,0:T(8,128)S(1)}, u32[]{:S(2)}) copy-start(f32[16,32,128]{2,1,0:T(8,128)S(1)} %get-tuple-element.83) | copy-start | bytes 786436 | tf_op jit(solution)/shard_map/cond
  482.4 4.9 collective-permute-start.28
  485.2 9.0 %collective-permute-start.27 = (f32[1,32,128]{2,1,0:T(8,128)S(1)}, f32[1,32,128]{2,1,0:T(8,128)S(1)}, u32[]{:S(2)}, u32[]{:S(2)}) collective-permute-start(f32[1,32,128]{2,1,0:T(8,128)S(1)} %get-tuple-element.104), channel_id=1, source_target_pairs={{1,0},{2,1},{3,2},{4,3},{5,4},{6,5},{7,6},{8,7},{9,8},{10,9},{11,1... | collective-permute-start | bytes 49160 | tf_op jit(solution)/shard_map/cond/branch_0_fun/ppermute | solution.py:570
  521.7 4.7 collective-permute-start.30
  524.4 9.0 %collective-permute-start.29 = (f32[1,32,128]{2,1,0:T(8,128)S(1)}, f32[1,32,128]{2,1,0:T(8,128)S(1)}, u32[]{:S(2)}, u32[]{:S(2)}) collective-permute-start(f32[1,32,128]{2,1,0:T(8,128)S(1)} %get-tuple-element.102), channel_id=1, source_target_pairs={{1,0},{2,1},{3,2},{4,3},{5,4},{6,5},{7,6},{8,7},{9,8},{10,9},{11,1... | collective-permute-start | bytes 49160 | tf_op jit(solution)/shard_map/cond/branch_0_fun/ppermute | solution.py:570
